TPU v7x, 32 devices: a whole 2x2x4 slice. The times are simulated.
32 devices in a mesh: dp: 16 (over z, y, x), tensor: 2 (over core).
Axes of the slice: x: 2, y: 2, z: 4, core: 2. Of those that a mesh axis runs over, the one named last changes fastest.
Arguments:
- residual: bfloat16 [16384, 1536], P(('dp', 'tensor')), may hold values from -6 to 6
- cotangent: bfloat16 [16384, 1536], P(('dp', 'tensor')), may hold values from -6 to 6
- segment_ids: int32 [16, 1024], P('dp'), may hold values from 0 to 3, never falling along the last dimension, each value on 1 to 800 neighbouring positions
- adapter_ids: int32 [16], P('dp'), may hold values from 0 to 7
- conv_gain: float32 [1536], replicated, may hold values from 0.1 to 1.9
- proj_in: bfloat16 [1536, 3, 1536], P('dp', None, 'tensor'), may hold values from -0.15625 to 0.15625
- conv_taps: bfloat16 [3, 1536], P(None, 'tensor'), may hold values from -3.5 to 3.5
- proj_out: bfloat16 [1536, 1536], P('dp', 'tensor'), may hold values from -0.15625 to 0.15625
- ffn_gain: float32 [1536], replicated, may hold values from 0.1 to 1.9
- gate_up: bfloat16 [1536, 2, 6912], P('dp', None, 'tensor'), may hold values from -0.15625 to 0.15625
- proj_down: bfloat16 [1536, 6912], P('dp', 'tensor'), may hold values from -0.109375 to 0.109375
- in_shrink: bfloat16 [1536, 8, 16], replicated, may hold values from -0.15625 to 0.15625
- input_lift_weight: bfloat16 [8, 16, 3, 1536], P(None, None, None, 'tensor'), may hold values from -1 to 1
- output_reduce_weight: bfloat16 [1536, 8, 16], P('tensor'), may hold values from -0.15625 to 0.15625
- output_lift_weight: bfloat16 [8, 16, 1536], replicated, may hold values from -1 to 1
- ffn_reduce_weight: bfloat16 [1536, 2, 8, 16], replicated, may hold values from -0.15625 to 0.15625
- ffn_expand: bfloat16 [2, 8, 16, 6912], P(None, None, None, 'tensor'), may hold values from -1 to 1
- down_shrink: bfloat16 [6912, 8, 16], P('tensor'), may hold values from -0.078125 to 0.078125
- down_lift_weight: bfloat16 [8, 16, 1536], replicated, may hold values from -1 to 1
Outputs:
- block_output: bfloat16 [16384, 1536], P(('dp', 'tensor'))
- grad_residual: bfloat16 [16384, 1536], P(('dp', 'tensor'))
- grad_in_shrink: float32 [1536, 8, 16], replicated
- grad_in_expand: float32 [8, 16, 3, 1536], P(None, None, None, 'tensor')
- grad_out_shrink: float32 [1536, 8, 16], P('tensor')
- grad_out_expand: float32 [8, 16, 1536], replicated
- grad_ffn_shrink: float32 [1536, 2, 8, 16], replicated
- grad_ffn_expand: float32 [2, 8, 16, 6912], P(None, None, None, 'tensor')
- grad_down_shrink: float32 [6912, 8, 16], P('tensor')
- grad_down_expand: float32 [8, 16, 1536], replicated
Inputs may be any that keep to these rules, and one draw needn't show every extreme that they name: `segment_ids`: within a sequence the ids never fall; each sequence holds four documents of 1 to 800 tokens, one exactly 800.
All inputs are finite; a program needn't handle non-finite values.
Results may differ from a plain program's by a relative error of at most 0.015.
Values may be sent and summed in bfloat16 or wider, within the bound.
A program may use at most 320 MiB of HBM per device.

v0:
```python
import jax
import jax.numpy as jnp
from jax import lax
from jax.sharding import PartitionSpec as P

ADAPTER_COUNT = 8
ADAPTER_RANK = 16


EPSILON = 1e-05


def contract_simple(left, right):
    return jnp.dot(left, right, preferred_element_type=jnp.float32)


def contract_against(left, right):
    return lax.dot_general(
        left, right, (((1,), (1,)), ((), ())), preferred_element_type=jnp.float32
    )


def dot_over_rows(left, right):
    return lax.dot_general(
        left, right, (((0,), (0,)), ((), ())), preferred_element_type=jnp.float32
    )


def split_pair(values):
    upper = values.astype(jnp.bfloat16)
    lower = (values - upper.astype(jnp.float32)).astype(jnp.bfloat16)
    return (upper, lower)


def broad_contract(values, right):
    upper, lower = split_pair(values)
    return contract_against(upper, right) + contract_against(lower, right)


def wide_over_rows(left, values):
    upper, lower = split_pair(values)
    return dot_over_rows(left, upper) + dot_over_rows(left, lower)


def normalize(values, gain):
    factor = lax.rsqrt(jnp.mean(values * values, axis=-1, keepdims=True) + EPSILON)
    return (values * factor * gain, factor)


def normalize_back(values, factor, gain, grad):
    unit = values * factor
    scaled = grad * gain
    return factor * (scaled - unit * jnp.mean(scaled * unit, axis=-1, keepdims=True))


def masked_rows(codes, adapter_selector, groups):
    count = codes.shape[0]
    return (
        codes.reshape(count, groups, ADAPTER_COUNT, ADAPTER_RANK)
        * adapter_selector[:, None, :, None]
    ).reshape(count, groups * ADAPTER_COUNT * ADAPTER_RANK)


def lagged(values, lag):
    return jnp.pad(values, ((0, 0), (lag, 0), (0, 0)))[:, : values.shape[1]]


def leading(values, lag):
    return jnp.pad(values, ((0, 0), (0, lag), (0, 0)))[:, lag:]


def same_document(segment_ids, lag):
    shifted = jnp.pad(segment_ids, ((0, 0), (lag, 0)), constant_values=-1)[
        :, : segment_ids.shape[1]
    ]
    return (segment_ids == shifted).astype(jnp.float32)[:, :, None]


def per_device(
    residual,
    cotangent,
    segment_ids,
    adapter_ids,
    conv_gain,
    proj_in,
    conv_taps,
    proj_out,
    ffn_gain,
    gate_up,
    proj_down,
    in_shrink,
    input_lift_weight,
    output_reduce_weight,
    output_lift_weight,
    ffn_reduce_weight,
    ffn_expand,
    down_shrink,
    down_lift_weight,
):
    quarter = residual.shape[0]
    sequences, length = segment_ids.shape
    row_count = sequences * length
    hidden_width = residual.shape[1]
    channel_count = proj_in.shape[2]
    hidden_shard = gate_up.shape[2]
    first_row = lax.axis_index("tensor") * quarter
    adapter_row = (
        adapter_ids[:, None] == jnp.arange(ADAPTER_COUNT, dtype=jnp.int32)[None, :]
    ).astype(jnp.float32)
    adapter_selector_total = jnp.broadcast_to(
        adapter_row[:, None, :], (sequences, length, ADAPTER_COUNT)
    ).reshape(row_count, ADAPTER_COUNT)
    local_adapter_selector = lax.dynamic_slice_in_dim(adapter_selector_total, first_row, quarter, 0)
    first_same_sequence = same_document(segment_ids, 1)
    second_same_sequence = same_document(segment_ids, 2)
    tap_values = conv_taps.astype(jnp.float32)
    local_input = residual.astype(jnp.float32)
    normed_one, factor_one = normalize(local_input, conv_gain)
    first_norm = lax.all_gather(normed_one.astype(jnp.bfloat16), "tensor", axis=0, tiled=True)
    in_full, out_full = (
        lax.all_gather(proj_in, "dp", axis=0, tiled=True),
        lax.all_gather(proj_out, "dp", axis=0, tiled=True),
    )
    input_latent = masked_rows(
        contract_simple(first_norm, in_shrink.reshape(hidden_width, ADAPTER_COUNT * ADAPTER_RANK)),
        adapter_selector_total,
        1,
    ).astype(jnp.bfloat16)
    input_projection_matrix = in_full.reshape(hidden_width, 3 * channel_count)
    input_adapter_term = input_lift_weight.reshape(ADAPTER_COUNT * ADAPTER_RANK, 3 * channel_count)
    residual_lanes = contract_simple(first_norm, input_projection_matrix) + contract_simple(
        input_latent, input_adapter_term
    )
    residual_lanes = residual_lanes.reshape(sequences, length, 3, channel_count)
    bgate, cgate, xval = (residual_lanes[:, :, 0], residual_lanes[:, :, 1], residual_lanes[:, :, 2])
    product = bgate * xval
    mixed_sum = (
        tap_values[0] * product
        + tap_values[1] * lagged(product, 1) * first_same_sequence
        + tap_values[2] * lagged(product, 2) * second_same_sequence
    )
    convolved_rows = (cgate * mixed_sum).astype(jnp.bfloat16).reshape(row_count, channel_count)
    output_adapter_input = output_reduce_weight.reshape(channel_count, ADAPTER_COUNT * ADAPTER_RANK)
    branch_part = contract_against(convolved_rows, out_full)
    latent_slice = contract_simple(convolved_rows, output_adapter_input)
    local_branch, code_own = (
        lax.psum_scatter(branch_part, "tensor", scatter_dimension=0, tiled=True),
        lax.psum_scatter(latent_slice, "tensor", scatter_dimension=0, tiled=True),
    )
    output_latent = masked_rows(code_own, local_adapter_selector, 1).astype(jnp.bfloat16)
    output_adapter_term = output_lift_weight.reshape(ADAPTER_COUNT * ADAPTER_RANK, hidden_width)
    second_input = local_input + local_branch + contract_simple(output_latent, output_adapter_term)
    normed_two, factor_two = normalize(second_input, ffn_gain)
    norm_local = normed_two.astype(jnp.bfloat16)
    gu_full, down_full = (
        lax.all_gather(gate_up, "dp", axis=0, tiled=True),
        lax.all_gather(proj_down, "dp", axis=0, tiled=True),
    )
    expand_weights, down_reduce_weight = (ffn_expand, down_shrink)
    second_norm = lax.all_gather(norm_local, "tensor", axis=0, tiled=True)
    hidden_rows = gu_full.shape[2]
    ffn_adapter_input = ffn_reduce_weight.reshape(hidden_width, 2 * ADAPTER_COUNT * ADAPTER_RANK)
    ffn_latent = masked_rows(
        contract_simple(second_norm, ffn_adapter_input), adapter_selector_total, 2
    ).astype(jnp.bfloat16)
    expand = expand_weights.reshape(2, ADAPTER_COUNT * ADAPTER_RANK, hidden_rows)
    base_sum = contract_simple(second_norm, gu_full.reshape(hidden_width, 2 * hidden_rows))
    gate_sum = base_sum[:, :hidden_rows] + contract_simple(
        ffn_latent[:, : ADAPTER_COUNT * ADAPTER_RANK], expand[0]
    )
    up_sum = base_sum[:, hidden_rows:] + contract_simple(
        ffn_latent[:, ADAPTER_COUNT * ADAPTER_RANK :], expand[1]
    )
    sigmoid_gate = jax.nn.sigmoid(gate_sum)
    silu_gate = gate_sum * sigmoid_gate
    activation_rows = (silu_gate * up_sum).astype(jnp.bfloat16)
    down_adapter_input = down_reduce_weight.reshape(hidden_rows, ADAPTER_COUNT * ADAPTER_RANK)
    down_part = contract_against(activation_rows, down_full)
    down_latent_slice = contract_simple(activation_rows, down_adapter_input)
    local_down, down_code_own = (
        lax.psum_scatter(
            down_part.astype(jnp.bfloat16), "tensor", scatter_dimension=0, tiled=True
        ).astype(jnp.float32),
        lax.psum_scatter(
            down_latent_slice.astype(jnp.bfloat16), "tensor", scatter_dimension=0, tiled=True
        ).astype(jnp.float32),
    )
    down_latent = masked_rows(down_code_own, local_adapter_selector, 1).astype(jnp.bfloat16)
    down_adapter_term = down_lift_weight.reshape(ADAPTER_COUNT * ADAPTER_RANK, hidden_width)
    block_output = (
        second_input + local_down + contract_simple(down_latent, down_adapter_term)
    ).astype(jnp.bfloat16)
    grad_top = cotangent.astype(jnp.float32)
    grad_down_expand = dot_over_rows(down_latent, cotangent)
    down_latent_gradient = masked_rows(
        contract_against(cotangent, down_adapter_term), local_adapter_selector, 1
    ).astype(jnp.bfloat16)
    gu_full, down_full = (
        lax.all_gather(gate_up, "dp", axis=0, tiled=True),
        lax.all_gather(proj_down, "dp", axis=0, tiled=True),
    )
    grad_branch_all, down_latent_gradient_total = (
        lax.all_gather(cotangent, "tensor", axis=0, tiled=True),
        lax.all_gather(down_latent_gradient, "tensor", axis=0, tiled=True),
    )
    grad_activation = contract_simple(grad_branch_all, down_full) + contract_against(
        down_latent_gradient_total, down_adapter_input
    )
    grad_down_shrink = dot_over_rows(activation_rows, down_latent_gradient_total)
    grad_gate = grad_activation * up_sum * sigmoid_gate * (1.0 + gate_sum * (1.0 - sigmoid_gate))
    grad_up = grad_activation * silu_gate
    grad_gu = jnp.concatenate([grad_gate, grad_up], axis=1).astype(jnp.bfloat16)
    ffn_latent_gradient = masked_rows(
        jnp.concatenate(
            [
                contract_against(grad_gu[:, :hidden_rows], expand[0]),
                contract_against(grad_gu[:, hidden_rows:], expand[1]),
            ],
            axis=1,
        ),
        adapter_selector_total,
        2,
    )
    grad_ffn_expand = jnp.stack(
        [
            dot_over_rows(ffn_latent[:, : ADAPTER_COUNT * ADAPTER_RANK], grad_gu[:, :hidden_rows]),
            dot_over_rows(ffn_latent[:, ADAPTER_COUNT * ADAPTER_RANK :], grad_gu[:, hidden_rows:]),
        ]
    )
    grad_ffn_shrink = wide_over_rows(second_norm, ffn_latent_gradient)
    grad_norm_two = contract_against(
        grad_gu, gu_full.reshape(hidden_width, 2 * hidden_rows)
    ) + broad_contract(ffn_latent_gradient, ffn_adapter_input)
    grad_norm_two_own = lax.psum_scatter(grad_norm_two, "tensor", scatter_dimension=0, tiled=True)
    second_input_gradient = grad_top + normalize_back(
        second_input, factor_two, ffn_gain, grad_norm_two_own
    )
    grad_out_expand = wide_over_rows(output_latent, second_input_gradient)
    output_latent_gradient = masked_rows(
        broad_contract(second_input_gradient, output_adapter_term), local_adapter_selector, 1
    ).astype(jnp.bfloat16)
    grad_branch_conv, output_latent_gradient_total = (
        lax.all_gather(second_input_gradient.astype(jnp.bfloat16), "tensor", axis=0, tiled=True),
        lax.all_gather(output_latent_gradient, "tensor", axis=0, tiled=True),
    )
    in_full, out_full = (
        lax.all_gather(proj_in, "dp", axis=0, tiled=True),
        lax.all_gather(proj_out, "dp", axis=0, tiled=True),
    )
    input_projection_matrix = in_full.reshape(hidden_width, 3 * channel_count)
    grad_conv_out = contract_simple(grad_branch_conv, out_full) + contract_against(
        output_latent_gradient_total, output_adapter_input
    )
    grad_out_shrink = dot_over_rows(convolved_rows, output_latent_gradient_total)
    grad_conv_out = grad_conv_out.reshape(sequences, length, channel_count)
    grad_cgate = grad_conv_out * mixed_sum
    grad_mixed = grad_conv_out * cgate
    grad_product = (
        tap_values[0] * grad_mixed
        + leading(tap_values[1] * grad_mixed * first_same_sequence, 1)
        + leading(tap_values[2] * grad_mixed * second_same_sequence, 2)
    )
    gradient_lanes = jnp.stack([grad_product * xval, grad_cgate, grad_product * bgate], axis=2)
    gradient_lanes = gradient_lanes.reshape(row_count, 3 * channel_count).astype(jnp.bfloat16)
    input_latent_gradient = masked_rows(
        contract_against(gradient_lanes, input_adapter_term), adapter_selector_total, 1
    )
    grad_in_expand = dot_over_rows(input_latent, gradient_lanes)
    grad_in_shrink = wide_over_rows(first_norm, input_latent_gradient)
    grad_norm_one = contract_against(gradient_lanes, input_projection_matrix) + broad_contract(
        input_latent_gradient, in_shrink.reshape(hidden_width, ADAPTER_COUNT * ADAPTER_RANK)
    )
    grad_norm_one_own = lax.psum_scatter(
        grad_norm_one.astype(jnp.bfloat16), "tensor", scatter_dimension=0, tiled=True
    ).astype(jnp.float32)
    grad_residual = (
        second_input_gradient
        + normalize_back(local_input, factor_one, conv_gain, grad_norm_one_own)
    ).astype(jnp.bfloat16)
    whole_in_shrink, whole_ffn_shrink, whole_out_expand, whole_down_expand = lax.psum(
        (grad_in_shrink, grad_ffn_shrink, grad_out_expand, grad_down_expand), ("dp", "tensor")
    )
    whole_in_expand, whole_ffn_expand, whole_out_shrink, whole_down_shrink = (
        lax.psum(grad_in_expand.astype(jnp.bfloat16), "dp").astype(jnp.float32),
        lax.psum(grad_ffn_expand.astype(jnp.bfloat16), "dp").astype(jnp.float32),
        lax.psum(grad_out_shrink.astype(jnp.bfloat16), "dp").astype(jnp.float32),
        lax.psum(grad_down_shrink.astype(jnp.bfloat16), "dp").astype(jnp.float32),
    )
    return (
        block_output,
        grad_residual,
        whole_in_shrink.reshape(hidden_width, ADAPTER_COUNT, ADAPTER_RANK),
        whole_in_expand.reshape(ADAPTER_COUNT, ADAPTER_RANK, 3, channel_count),
        whole_out_shrink.reshape(channel_count, ADAPTER_COUNT, ADAPTER_RANK),
        whole_out_expand.reshape(ADAPTER_COUNT, ADAPTER_RANK, hidden_width),
        whole_ffn_shrink.reshape(hidden_width, 2, ADAPTER_COUNT, ADAPTER_RANK),
        whole_ffn_expand.reshape(2, ADAPTER_COUNT, ADAPTER_RANK, hidden_shard),
        whole_down_shrink.reshape(hidden_shard, ADAPTER_COUNT, ADAPTER_RANK),
        whole_down_expand.reshape(ADAPTER_COUNT, ADAPTER_RANK, hidden_width),
    )


def solution(mesh):
    placed = (
        P(("dp", "tensor"), None),
        P(("dp", "tensor"), None),
        P("dp", None),
        P("dp"),
        P(),
        P("dp", None, "tensor"),
        P(None, "tensor"),
        P("dp", "tensor"),
        P(),
        P("dp", None, "tensor"),
        P("dp", "tensor"),
        P(),
        P(None, None, None, "tensor"),
        P("tensor", None, None),
        P(),
        P(),
        P(None, None, None, "tensor"),
        P("tensor", None, None),
        P(),
    )
    return jax.shard_map(
        per_device,
        mesh=mesh,
        in_specs=placed,
        out_specs=(
            P(("dp", "tensor"), None),
            P(("dp", "tensor"), None),
            P(),
            P(None, None, None, "tensor"),
            P("tensor", None, None),
            P(),
            P(),
            P(None, None, None, "tensor"),
            P("tensor", None, None),
            P(),
        ),
        check_vma=False,
    )
```

profile of v0, /device:TPU:0, one launch (start us, length us, event | category | flops | bytes accessed | tf_op | source)
XLA Modules:
  0.0 1191.7 jit_solution(14177401779273440955)
XLA Ops:
  9.7 3.0 fusion.22
  15.7 12.1 %all-gather.9.cloned.1.call-done = bf16[1024,1536]{1,0:T(8,128)(2,1)} async-done(((bf16[512,1536]{1,0:T(8,128)(2,1)}), bf16[1024,1536]{1,0:T(8,128)(2,1)}) %all-gather.9.cloned.1.call-update) | async-done | bytes 3145744 | tf_op jit(solution)/shard_map/all_gather | solution.py:119
  27.7 3.0 fusion.53
  30.8 101.4 %all-gather.11.cloned.1.call-done = bf16[1536,3,768]{2,0,1:T(8,128)(2,1)} async-done(((bf16[96,3,768]{2,0,1:T(8,128)(2,1)}), bf16[1536,3,768]{2,0,1:T(8,128)(2,1)}) %all-gather.11.cloned.1.call-update) | async-done | bytes 7077904 | tf_op jit(solution)/shard_map/all_gather | solution.py:121
  132.2 10.3 copy.43
  142.6 10.5 fusion.93
  153.1 5.0 convolution_add_fusion.1
  158.1 9.7 copy.45
  167.8 7.9 fusion.91
  175.8 3.8 copy.57
  179.6 3.6 copy.58
  183.2 3.5 copy.56
  186.7 3.4 bitcast_multiply_fusion.3
  190.5 2.9 fusion.38
  195.7 6.1 fusion.94
  205.7 16.3 %reduce-scatter.7.cloned.1.call-done = f32[512,1536]{1,0:T(8,128)} async-done(((f32[1024,1536]{1,0:T(8,128)}), f32[512,1536]{1,0:T(8,128)}) %reduce-scatter.7.cloned.1.call-update) | async-done | bytes 3145744 | tf_op jit(solution)/shard_map/reduce_scatter | solution.py:147
  222.0 2.6 multiply_reduce_fusion.1
  230.3 2.9 all_gather.41
  234.2 3.5 all-gather.21.cloned.1.call-done
  237.6 136.7 %all-gather.19.cloned.1.call-done = bf16[1536,3456]{1,0:T(8,128)(2,1)} async-done(((bf16[96,3456]{1,0:T(8,128)(2,1)}), bf16[1536,3456]{1,0:T(8,128)(2,1)}) %all-gather.19.cloned.1.call-update) | async-done | bytes 10616848 | tf_op jit(solution)/shard_map/all_gather | solution.py:157
  374.4 15.6 %fusion.97 = f32[1024,3456]{1,0:T(8,128)S(1)} fusion(bf16[1024,1536]{1,0:T(8,128)(2,1)} %all-gather.21.cloned.1.call-done, bf16[1536,3456]{1,0:T(8,128)(2,1)} %all-gather.19.cloned.1.call-done), kind=kOutput, calls=%fused_computation.146 | convolution fusion | flops 10871635968 | bytes 27918336 | tf_op jit(solution)/shard_map/dot_general | solution.py:14
  390.0 7.1 convolution_add_fusion
  397.0 3.2 fusion.47
  400.2 223.8 %all-gather.17.cloned.1.call-done = bf16[1536,2,3456]{2,1,0:T(2,128)(2,1)} async-done(((bf16[96,2,3456]{2,1,0:T(2,128)(2,1)}), bf16[1536,2,3456]{2,1,0:T(2,128)(2,1)}) %all-gather.17.cloned.1.call-update) | async-done | bytes 21233680 | tf_op jit(solution)/shard_map/all_gather | solution.py:156
  624.0 20.5 %copy.61 = bf16[192,8,2,3456]{3,1,2,0:T(8,128)(2,1)} copy(bf16[192,8,2,3456]{3,2,1,0:T(2,128)(2,1)} %bitcast.202) | data formatting | bytes 42467328
  644.5 29.6 %fusion.96 = f32[1024,6912]{1,0:T(8,128)} fusion(bf16[1024,1536]{1,0:T(8,128)(2,1)S(1)} %copy-done.18, bf16[1536,6912]{1,0:T(8,128)(2,1)} %bitcast.203), kind=kOutput, calls=%fused_computation.145 | convolution fusion | flops 21743271936 | bytes 52690944 | tf_op jit(solution)/shard_map/dot_general | solution.py:14
  674.0 12.0 %slice_add_fusion = f32[1024,3456]{1,0:T(8,128)} fusion(f32[1024,6912]{1,0:T(8,128)} %fusion.96, bf16[128,3456]{1,0:T(8,128)(2,1)S(1)} %bitcast.224, bf16[1024,256]{0,1:T(8,128)(2,1)S(1)} %bitcast.216), kind=kOutput, calls=%fused_computation | convolution fusion | flops 909508608 | bytes 29458432 | tf_op jit(solution)/shard_map/dot_general | solution.py:14
  686.0 23.1 %multiply_convert_fusion.1 = (bf16[1024,3456]{1,0:T(8,128)(2,1)}, bf16[1024,3456]{1,0:T(8,128)(2,1)S(1)}, bf16[1024,3456]{1,0:T(8,128)(2,1)}) fusion(f32[1024,3456]{1,0:T(8,128)} %convolution_add_fusion, f32[1024,3456]{1,0:T(8,128)} %slice_add_fusion, bf16[128,3456]{1,0:T(8,128)(2,1)} %bitcast.236, bf16[1024,256]{0,1:T(8,128)(2,1)} %bitcast.217, ...), kind=kOutput, calls=%fused_computation.7 | convolution fusion | flops 962592768 | bytes 64847872 | tf_op jit(solution)/shard_map/dot_general | solution.py:14
  709.1 8.1 fusion.98
  717.3 2.3 fusion.99
  719.7 3.8 fusion.87
  723.5 3.7 fusion.85
  727.2 34.7 %add_add_fusion = f32[1024,1536]{1,0:T(8,128)} fusion(f32[1024,1536]{1,0:T(8,128)} %fusion.85, f32[1024,1536]{1,0:T(8,128)} %fusion.87, bf16[1536,6912]{1,0:T(8,128)(2,1)} %bitcast.204, bf16[1024,3456]{1,0:T(8,128)(2,1)} %copy-done.12, bf16[1024,3456]{1,0:T(8,128)(2,1)} %get-tuple-element.49), kind=kOutput, calls=%fused_computation.16 | convolution fusion | flops 21774729216 | bytes 54263808 | tf_op jit(solution)/shard_map/dot_general | solution.py:18
  762.0 12.3 %reduce-scatter.15.cloned.1.call-done = f32[512,1536]{1,0:T(8,128)} async-done(((f32[1024,1536]{1,0:T(8,128)}), f32[512,1536]{1,0:T(8,128)}) %reduce-scatter.15.cloned.1.call-update) | async-done | bytes 3145744 | tf_op jit(solution)/shard_map/reduce_scatter | solution.py:234
  774.3 3.5 multiply_reduce_fusion
  778.1 5.0 fusion.89
  783.4 5.7 convolution_convert_fusion.5
  789.1 18.0 %convolution_convert_fusion.3 = bf16[1024,1536]{1,0:T(8,128)(2,1)} fusion(bf16[1024,3456]{1,0:T(8,128)(2,1)} %get-tuple-element.51, bf16[1536,3456]{1,0:T(8,128)(2,1)} %all-gather.19.cloned.1.call-done), kind=kOutput, calls=%fused_computation.29 | convolution fusion | flops 10873208832 | bytes 20840448 | tf_op jit(solution)/shard_map/dot_general | solution.py:18
  807.2 2.0 copy.59
  809.2 4.3 fusion.9
  813.5 4.3 fusion.10
  817.9 2.1 convolution_convert_fusion
  823.8 3.0 all_gather.43
  828.0 5.2 fusion.100
  838.0 2.5 fusion.40
  842.4 2.4 pad_maximum_fusion
  844.8 6.7 copy.49
  851.5 4.0 convolution_convert_fusion.4
  857.6 3.3 convolution_multiply_fusion
  864.1 7.7 fusion.101
  871.8 2.7 fusion.6
  875.6 3.1 fusion.83
  878.7 2.2 convolution_add_fusion.4
  881.0 2.3 fusion.75
  883.3 2.4 fusion.78
  891.2 4.1 fusion.37
  895.3 120.4 %all-reduce.13.cloned.1.call-done = (bf16[8,16,3,768]{3,2,1,0:T(4,128)(2,1)}, bf16[768,8,16]{0,2,1:T(8,128)(2,1)}, bf16[2,8,16,3456]{3,2,1,0:T(8,128)(2,1)}, bf16[3456,8,16]{0,2,1:T(8,128)(2,1)}) async-done(((bf16[8,16,3,768]{3,2,1,0:T(4,128)(2,1)}, bf16[768,8,16]{0,2,1:T(8,128)(2,1)}, bf16[2,8,16,3456]{3,2,1,0:T(8,128)(2,1)}, bf16[3456,8,16]{0,2,1:T(8,128)(2,1)}), (bf16[8,16,3,768]{3,2,1,0:T(4,128)(2,1)}, ...) | async-done | bytes 3440656 | tf_op jit(solution)/shard_map/psum | solution.py:284
  1015.7 3.6 reshape.360
  1022.7 5.3 reduce-scatter.17.cloned.1.call-done
  1028.0 2.3 fusion.23
  1030.4 3.5 fusion.27
  1033.9 144.8 %all-reduce.11.cloned.1.call-done = (f32[1536,8,16]{0,2,1:T(8,128)}, f32[8,16,1536]{2,1,0:T(8,128)}, f32[1536,2,8,16]{0,3,2,1:T(8,128)}, f32[8,16,1536]{2,1,0:T(8,128)}) async-done(((f32[1536,8,16]{0,2,1:T(8,128)}, f32[8,16,1536]{2,1,0:T(8,128)}, f32[1536,2,8,16]{0,3,2,1:T(8,128)}, f32[8,16,1536]{2,1,0:T(8,128)}), (f32[1536,8,16]{0,2,1:T(8,128)}, f32[8,16,1536]{2,1,0:T(8,128)}, ...) | async-done | bytes 3932176 | tf_op jit(solution)/shard_map/psum | solution.py:280
  1178.7 2.2 copy.71
  1180.9 2.1 copy.72
  (257 shorter events, 47.2 us)
Async XLA Ops:
  7.2 382.8 %copy-start = (bf16[3456,8,16]{0,2,1:T(8,128)(2,1)S(1)}, bf16[3456,8,16]{0,2,1:T(8,128)(2,1)}, u32[]{:S(2)}) copy-start(bf16[3456,8,16]{0,2,1:T(8,128)(2,1)} %param.36) | copy-start | bytes 2654212
  7.2 7.8 copy-start.37
  7.2 20.5 %all-gather.9.cloned.1.call-start = ((), (), s32[]{:S(2)}) async-start(), calls=%async_computation.6 | async-start | bytes 4718592 | tf_op jit(solution)/shard_map/all_gather | solution.py:119
  12.7 15.0 %copy-start.81 = (bf16[1536,8,16]{0,2,1:T(8,128)(2,1)S(1)}, bf16[1536,8,16]{0,2,1:T(8,128)(2,1)}, u32[]{:S(2)}) copy-start(bf16[1536,8,16]{0,2,1:T(8,128)(2,1)} %param.30) | copy-start | bytes 1179652
  12.7 119.5 %all-gather.11.cloned.1.call-start = ((), (), s32[]{:S(2)}) async-start(), calls=%async_computation.7 | async-start | bytes 7520256 | tf_op jit(solution)/shard_map/all_gather | solution.py:121
  13.5 182.2 %all-gather.13.cloned.1.call-start = ((), (), s32[]{:S(2)}) async-start(), calls=%async_computation.8 | async-start | bytes 2506752 | tf_op jit(solution)/shard_map/all_gather | solution.py:122
  14.2 190.4 %reduce-scatter.9.cloned.1.call-start = ((), (), s32[]{:S(2)}) async-start(), calls=%async_computation.10 | async-start | bytes 786432 | tf_op jit(solution)/shard_map/reduce_scatter | solution.py:148
  14.9 382.1 %copy-start.79 = (f32[8]{0:T(128)}, f32[8]{0:T(128)S(1)}, u32[]{:S(2)}) copy-start(f32[8]{0:T(128)S(1)} %compare_convert_fusion.2) | copy-start | bytes 100
  15.5 174.6 %copy-start.65 = (f32[768]{0:T(1024)}, f32[768]{0:T(1024)S(1)}, u32[]{:S(2)}) copy-start(f32[768]{0:T(1024)S(1)} %get-tuple-element.31) | copy-start | bytes 9220
  15.5 174.6 %copy-start.67 = (f32[768]{0:T(1024)}, f32[768]{0:T(1024)S(1)}, u32[]{:S(2)}) copy-start(f32[768]{0:T(1024)S(1)} %get-tuple-element.32) | copy-start | bytes 9220
  15.5 174.6 %copy-start.69 = (f32[768]{0:T(1024)}, f32[768]{0:T(1024)S(1)}, u32[]{:S(2)}) copy-start(f32[768]{0:T(1024)S(1)} %get-tuple-element.30) | copy-start | bytes 9220
  15.6 174.5 %copy-start.61 = (f32[1,1024]{1,0:T(1,128)}, f32[1,1024]{1,0:T(1,128)S(1)}, u32[]{:S(2)}) copy-start(f32[1,1024]{1,0:T(1,128)S(1)} %get-tuple-element.60) | copy-start | bytes 12292
  15.6 174.5 %copy-start.63 = (f32[1,1024]{1,0:T(1,128)}, f32[1,1024]{1,0:T(1,128)S(1)}, u32[]{:S(2)}) copy-start(f32[1,1024]{1,0:T(1,128)S(1)} %get-tuple-element.61) | copy-start | bytes 12292
  30.8 122.3 %copy-start.42 = (bf16[1024,8,16]{0,2,1:T(8,128)(2,1)}, bf16[1024,8,16]{0,2,1:T(8,128)(2,1)S(1)}, u32[]{:S(2)}) copy-start(bf16[1024,8,16]{0,2,1:T(8,128)(2,1)S(1)} %fusion.53) | copy-start | bytes 786436
  186.7 3.8 copy-start.6
  193.4 8.4 copy-start.15
  194.8 27.2 %reduce-scatter.7.cloned.1.call-start = ((), (), s32[]{:S(2)}) async-start(), calls=%async_computation.9 | async-start | bytes 9437184 | tf_op jit(solution)/shard_map/reduce_scatter | solution.py:147
  201.8 20.2 %copy-start.8 = (bf16[512,1536]{1,0:T(8,128)(2,1)S(1)}, bf16[512,1536]{1,0:T(8,128)(2,1)}, u32[]{:S(2)}) copy-start(bf16[512,1536]{1,0:T(8,128)(2,1)} %param.19) | copy-start | bytes 4718596
  201.8 20.2 %copy-start.31 = (bf16[8,16,1536]{2,1,0:T(8,128)(2,1)S(1)}, bf16[8,16,1536]{2,1,0:T(8,128)(2,1)}, u32[]{:S(2)}) copy-start(bf16[8,16,1536]{2,1,0:T(8,128)(2,1)} %param.33) | copy-start | bytes 1179652
  201.8 35.8 %all-gather.21.cloned.1.call-start = ((), (), s32[]{:S(2)}) async-start(), calls=%async_computation.16 | async-start | bytes 4718592 | tf_op jit(solution)/shard_map/all_gather | solution.py:203
  202.4 172.0 %all-gather.19.cloned.1.call-start = ((), (), s32[]{:S(2)}) async-start(), calls=%async_computation.13 | async-start | bytes 11280384 | tf_op jit(solution)/shard_map/all_gather | solution.py:157
  203.1 193.9 %all-gather.15.cloned.1.call-start = ((), (), s32[]{:S(2)}) async-start(), calls=%async_computation.11 | async-start | bytes 4718592 | tf_op jit(solution)/shard_map/all_gather | solution.py:160
  203.3 21.3 %copy-start.75 = (f32[128]{0:T(128)}, f32[128]{0:T(128)S(1)}, u32[]{:S(2)}) copy-start(f32[128]{0:T(128)S(1)} %mul.364) | copy-start | bytes 1540
  205.7 19.0 %copy-start.38 = (bf16[512,128]{1,0:T(8,128)(2,1)}, bf16[512,128]{1,0:T(8,128)(2,1)S(1)}, u32[]{:S(2)}) copy-start(bf16[512,128]{1,0:T(8,128)(2,1)S(1)} %multiply_convert_fusion.5) | copy-start | bytes 393220
  222.0 4.3 copy-start.58
  227.8 396.2 %all-gather.17.cloned.1.call-start = ((), (), s32[]{:S(2)}) async-start(), calls=%async_computation.12 | async-start | bytes 22560768 | tf_op jit(solution)/shard_map/all_gather | solution.py:156
  228.5 545.8 %reduce-scatter.15.cloned.1.call-start = ((), (), s32[]{:S(2)}) async-start(), calls=%async_computation.17 | async-start | bytes 9437184 | tf_op jit(solution)/shard_map/reduce_scatter | solution.py:234
  233.1 156.8 %copy-start.27 = (bf16[1024,128]{0,1:T(8,128)(2,1)}, bf16[1024,128]{0,1:T(8,128)(2,1)S(1)}, u32[]{:S(2)}) copy-start(bf16[1024,128]{0,1:T(8,128)(2,1)S(1)} %all_gather.41) | copy-start | bytes 786436
  234.2 439.9 %copy-start.33 = (bf16[1,8,16,3456]{3,2,1,0:T(8,128)(2,1)}, bf16[1,8,16,3456]{3,2,1,0:T(8,128)(2,1)S(1)}, u32[]{:S(2)}) copy-start(bf16[1,8,16,3456]{3,2,1,0:T(8,128)(2,1)S(1)} %get-tuple-element.59) | copy-start | bytes 2654212
  389.9 7.1 copy-start.35
  400.2 273.9 %copy-start.29 = (bf16[1024,2,8,16]{0,3,2,1:T(8,128)(2,1)}, bf16[1024,2,8,16]{0,3,2,1:T(8,128)(2,1)S(1)}, u32[]{:S(2)}) copy-start(bf16[1024,2,8,16]{0,3,2,1:T(8,128)(2,1)S(1)} %fusion.47) | copy-start | bytes 1572868
  624.0 20.5 %copy-start.18 = (bf16[1024,1536]{1,0:T(8,128)(2,1)S(1)}, bf16[1024,1536]{1,0:T(8,128)(2,1)}, u32[]{:S(2)}) copy-start(bf16[1024,1536]{1,0:T(8,128)(2,1)} %all-gather.15.cloned.1.call-done) | copy-start | bytes 9437188
  709.1 8.1 copy-start.12
  709.1 8.1 copy-start.34
  717.2 6.2 copy-start.21
  719.7 3.8 copy-start.23
  761.9 12.4 %copy-start.59 = (f32[1536]{0:T(1024)S(1)}, f32[1536]{0:T(1024)}, u32[]{:S(2)}) copy-start(f32[1536]{0:T(1024)} %param.27) | copy-start | bytes 18436
  761.9 12.4 %copy-start.72 = (f32[512]{0:T(512)S(1)}, f32[512]{0:T(512)}, u32[]{:S(2)}) copy-start(f32[512]{0:T(512)} %copy-done.71) | copy-start | bytes 6148
  761.9 15.9 %copy-start.14 = (bf16[512,1536]{1,0:T(8,128)(2,1)S(1)}, bf16[512,1536]{1,0:T(8,128)(2,1)}, u32[]{:S(2)}) copy-start(bf16[512,1536]{1,0:T(8,128)(2,1)} %param.20) | copy-start | bytes 4718596
  761.9 66.0 %all-gather.23.cloned.1.call-start = ((), (), s32[]{:S(2)}) async-start(), calls=%async_computation.18 | async-start | bytes 4718592 | tf_op jit(solution)/shard_map/all_gather | solution.py:243
  774.3 3.7 copy-start.5
  783.1 97.8 %reduce-scatter.13.cloned.1.call-start = ((), (), s32[]{:S(2)}) async-start(), calls=%async_computation.15 | async-start | bytes 393216 | tf_op jit(solution)/shard_map/reduce_scatter | solution.py:184
  789.1 101.1 %reduce-scatter.11.cloned.1.call-start = ((), (), s32[]{:S(2)}) async-start(), calls=%async_computation.14 | async-start | bytes 4718592 | tf_op jit(solution)/shard_map/reduce_scatter | solution.py:181
  807.2 208.6 %all-reduce.13.cloned.1.call-start = ((), (), s32[]{:S(2)}) async-start(), calls=%async_computation.21 | async-start | bytes 7274496 | tf_op jit(solution)/shard_map/psum | solution.py:284
  809.2 8.6 slice-start
  813.5 4.3 slice-start.1
  813.5 4.3 copy-start.28
  822.7 4.2 copy-start.16
  828.0 5.3 copy-start.46
  844.8 6.7 copy-start.43
  856.6 171.4 %reduce-scatter.17.cloned.1.call-start = ((), (), s32[]{:S(2)}) async-start(), calls=%async_computation.19 | async-start | bytes 4718592 | tf_op jit(solution)/shard_map/reduce_scatter | solution.py:273
  857.6 4.3 slice-start.2
  857.6 5.2 slice-start.4
  860.9 10.8 copy-start.50
  874.5 304.2 %all-reduce.11.cloned.1.call-start = ((), (), s32[]{:S(2)}) async-start(), calls=%async_computation.20 | async-start | bytes 7864320 | tf_op jit(solution)/shard_map/psum | solution.py:280
  881.0 4.7 copy-start.39
  881.0 4.7 copy-start.2
  1015.7 3.7 copy-start.44
  1015.7 5.0 copy-start.48
  1019.4 8.6 copy-start.9
  1019.4 8.6 copy-start.60
  1019.4 8.6 copy-start.74
  1178.7 4.3 copy-start.41
  1178.7 5.4 copy-start.47
  (41 other events, 88.8 us)
Sparse Core Ops, SparseCore 0:
  12.9 14.8 all-gather.8
  30.4 101.7 all-gather.10
  135.0 60.5 all-gather.12
  198.3 6.3 reduce-scatter.8
  206.8 15.1 reduce-scatter.6
  223.4 14.1 all-gather.20
  240.4 133.8 all-gather.18
  376.5 10.2 all-gather.14
  389.6 234.3 all-gather.16
  762.1 12.2 reduce-scatter.14
  783.2 14.1 all-gather.22
  800.1 8.9 reduce-scatter.12
  811.3 12.2 reduce-scatter.10
  856.7 158.9 all-reduce.12
  1017.8 10.1 reduce-scatter.16
  1035.1 143.5 all-reduce.10
where the time goes:
time: 1200 us; the launch traced here: 1190 us
  waiting for transfers between devices  782 us (65%)
  matrix products  251 us (21%)
  local copies, waits for them, and re-layouts  93.8 us (8%)
  other arithmetic  41.4 us (3%)
  between operations  15.7 us (1%)
    all_gather x1, waiting for transfers between devices, per_device(): lax.all_gather(gate_up, 'dp', axis=0, tiled=True)  224 us
    psum x1, waiting for transfers between devices, per_device(): lax.psum((grad_in_shrink, grad_ffn_shrink, grad_out_expand, grad_down_exp...  145 us
    all_gather x1, waiting for transfers between devices, per_device(): lax.all_gather(proj_down, 'dp', axis=0, tiled=True)  137 us
    dot_general x13, matrix products, contract_simple(): return jnp.dot(left, right, preferred_element_type=jnp.float32)  121 us
    psum x1, waiting for transfers between devices, per_device(): lax.psum(grad_in_expand.astype(jnp.bfloat16), 'dp').astype(jnp.float32)  120 us
    all_gather x1, waiting for transfers between devices, per_device(): lax.all_gather(proj_in, 'dp', axis=0, tiled=True)  101 us
    dot_general x16, matrix products, contract_against(): lax.dot_general(left, right, (((1,), (1,)), ((), ())), preferred_element_...  101 us
    unnamed x189, local copies, waits for them, and re-layouts  54.2 us
  transfers between devices with their start and end apart: 16, of which 12 were waited for; matrix products, arithmetic and copies ran while one was open for 18% of the time, Pallas kernels for 0%

commit v1 on v0

--- a/solution.py
+++ b/solution.py
@@ -1,7 +1,156 @@
+import functools
+
 import jax
 import jax.numpy as jnp
 from jax import lax
+from jax.experimental import pallas as pl
+from jax.experimental.pallas import tpu as pltpu
 from jax.sharding import PartitionSpec as P
+
+MESH = pl.DeviceIdType.MESH
+
+
+def split_ring(count):
+    if count % 16 == 0 and count >= 16:
+        return (4, count // 8, 2)
+    return (count, 1, 1)
+
+
+def position(index, dims):
+    return (index // (dims[1] * dims[2]), (index // dims[2]) % dims[1], index % dims[2])
+
+
+def flat(spot, dims):
+    return (spot[0] * dims[1] + spot[1]) * dims[2] + spot[2]
+
+
+def routes(column_ranges, dims):
+    out = []
+    for which, first, width in column_ranges:
+        half = (width // 256) * 128
+        out.append((which, first, half, (0, 1, 2)))
+        out.append((which, first + half, width - half, (0, 2, 1)))
+    return out
+
+
+def cut(which, columns, step):
+    return [(which, i, min(step, columns - i)) for i in range(0, columns, step)]
+
+
+class Gather:
+    def __init__(self, dims, spot, shards, wholes, pieces, send, recv):
+        self.dims, self.spot, self.shards, self.wholes = dims, spot, shards, wholes
+        self.pieces, self.send, self.recv = pieces, send, recv
+
+    def stage(self, piece, step):
+        which, first, width, order = self.pieces[piece]
+        axis = order[step]
+        columns = pl.ds(first, width)
+        place = tuple(
+            slice(None) if other in order[:step] else self.spot[other] for other in range(3)
+        )
+        whole = self.wholes[which].at[place + (slice(None), columns)]
+        base = sum(self.dims[other] - 1 for other in order[:step])
+        copies = []
+        for offset in range(1, self.dims[axis]):
+            peer = list(self.spot)
+            peer[axis] = lax.rem(self.spot[axis] + offset, self.dims[axis])
+            source = self.shards[which].at[:, columns] if step == 0 else whole
+            copies.append(
+                pltpu.make_async_remote_copy(
+                    src_ref=source,
+                    dst_ref=whole,
+                    send_sem=self.send.at[piece, base + offset - 1],
+                    recv_sem=self.recv.at[piece, base + offset - 1],
+                    device_id={"dp": flat(peer, self.dims)},
+                    device_id_type=MESH,
+                )
+            )
+        return copies
+
+    def start(self, piece, step):
+        for copy in self.stage(piece, step):
+            copy.start()
+
+    def arrive(self, piece, step):
+        for copy in self.stage(piece, step):
+            copy.wait_recv()
+
+    def drain(self, piece):
+        for step in range(3):
+            for copy in self.stage(piece, step):
+                copy.wait_send()
+
+    def greet(self):
+        barrier = pltpu.get_barrier_semaphore()
+        count = 0
+        for axis in range(3):
+            for offset in range(1, self.dims[axis]):
+                peer = list(self.spot)
+                peer[axis] = lax.rem(self.spot[axis] + offset, self.dims[axis])
+                pl.semaphore_signal(
+                    barrier, inc=1, device_id={"dp": flat(peer, self.dims)}, device_id_type=MESH
+                )
+                count += 1
+        pl.semaphore_wait(barrier, count)
+
+
+def gather_kernel(dims, pieces, amount, *refs):
+    shards, wholes = refs[:amount], refs[amount : 2 * amount]
+    held = refs[2 * amount : 3 * amount]
+    send, recv, local = refs[3 * amount :]
+    spot = position(lax.axis_index("dp"), dims)
+    gather = Gather(dims, spot, shards, wholes, pieces, send, recv)
+    gather.greet()
+    loads = [
+        pltpu.make_async_copy(shards[i], held[i], local.at[i]) for i in range(amount)
+    ]
+    for load in loads:
+        load.start()
+    for piece in range(len(pieces)):
+        gather.start(piece, 0)
+    stores = []
+    for i in range(amount):
+        loads[i].wait()
+        store = pltpu.make_async_copy(held[i], wholes[i].at[spot], local.at[i])
+        store.start()
+        stores.append(store)
+    for store in stores:
+        store.wait()
+    for piece in range(0, len(pieces) + 2, 2):
+        for part in (piece, piece + 1):
+            if part < len(pieces):
+                gather.arrive(part, 0)
+                gather.start(part, 1)
+        for part in (piece - 2, piece - 1):
+            if 0 <= part < len(pieces):
+                gather.arrive(part, 1)
+                gather.start(part, 2)
+    for piece in range(len(pieces)):
+        gather.arrive(piece, 2)
+        gather.drain(piece)
+
+
+def gather_all(shards, column_ranges, count):
+    dims = split_ring(count)
+    pieces = routes(column_ranges, dims)
+    amount = len(shards)
+    lanes = sum(d - 1 for d in dims)
+    anywhere = pl.BlockSpec(memory_space=pl.ANY)
+    outs = pl.pallas_call(
+        functools.partial(gather_kernel, dims, pieces, amount),
+        out_shape=[jax.ShapeDtypeStruct(dims + s.shape, s.dtype) for s in shards],
+        in_specs=[anywhere] * amount,
+        out_specs=[anywhere] * amount,
+        scratch_shapes=[pltpu.VMEM(s.shape, s.dtype) for s in shards]
+        + [
+            pltpu.SemaphoreType.DMA((len(pieces), lanes)),
+            pltpu.SemaphoreType.DMA((len(pieces), lanes)),
+            pltpu.SemaphoreType.DMA((amount,)),
+        ],
+        compiler_params=pltpu.CompilerParams(collective_id=0, has_side_effects=True),
+    )(*shards)
+    return [o.reshape(count * s.shape[0], s.shape[1]) for o, s in zip(outs, shards)]
 
 ADAPTER_COUNT = 8
 ADAPTER_RANK = 16
@@ -117,10 +266,20 @@
     local_input = residual.astype(jnp.float32)
     normed_one, factor_one = normalize(local_input, conv_gain)
     first_norm = lax.all_gather(normed_one.astype(jnp.bfloat16), "tensor", axis=0, tiled=True)
-    in_full, out_full = (
-        lax.all_gather(proj_in, "dp", axis=0, tiled=True),
-        lax.all_gather(proj_out, "dp", axis=0, tiled=True),
-    )
+    count = lax.axis_size("dp")
+    shard_rows = proj_in.shape[0]
+    hidden_shard_columns = proj_down.shape[1]
+    shards = [
+        jnp.concatenate([proj_in.reshape(shard_rows, 3 * channel_count), proj_out], axis=1),
+        gate_up.reshape(shard_rows, 2 * hidden_shard_columns),
+        proj_down,
+    ]
+    ranges = cut(0, 4 * channel_count, 512)
+    ranges += cut(1, 2 * hidden_shard_columns, 1152)
+    ranges += cut(2, hidden_shard_columns, 1152)
+    io_full, gu_rows, down_full = gather_all(shards, ranges, count)
+    in_full, out_full = io_full[:, : 3 * channel_count], io_full[:, 3 * channel_count :]
+    gu_full = gu_rows.reshape(hidden_width, 2, hidden_shard_columns)
     input_latent = masked_rows(
         contract_simple(first_norm, in_shrink.reshape(hidden_width, ADAPTER_COUNT * ADAPTER_RANK)),
         adapter_selector_total,
@@ -152,10 +311,6 @@
     second_input = local_input + local_branch + contract_simple(output_latent, output_adapter_term)
     normed_two, factor_two = normalize(second_input, ffn_gain)
     norm_local = normed_two.astype(jnp.bfloat16)
-    gu_full, down_full = (
-        lax.all_gather(gate_up, "dp", axis=0, tiled=True),
-        lax.all_gather(proj_down, "dp", axis=0, tiled=True),
-    )
     expand_weights, down_reduce_weight = (ffn_expand, down_shrink)
     second_norm = lax.all_gather(norm_local, "tensor", axis=0, tiled=True)
     hidden_rows = gu_full.shape[2]
@@ -195,10 +350,6 @@
     down_latent_gradient = masked_rows(
         contract_against(cotangent, down_adapter_term), local_adapter_selector, 1
     ).astype(jnp.bfloat16)
-    gu_full, down_full = (
-        lax.all_gather(gate_up, "dp", axis=0, tiled=True),
-        lax.all_gather(proj_down, "dp", axis=0, tiled=True),
-    )
     grad_branch_all, down_latent_gradient_total = (
         lax.all_gather(cotangent, "tensor", axis=0, tiled=True),
         lax.all_gather(down_latent_gradient, "tensor", axis=0, tiled=True),
@@ -242,10 +393,6 @@
     grad_branch_conv, output_latent_gradient_total = (
         lax.all_gather(second_input_gradient.astype(jnp.bfloat16), "tensor", axis=0, tiled=True),
         lax.all_gather(output_latent_gradient, "tensor", axis=0, tiled=True),
-    )
-    in_full, out_full = (
-        lax.all_gather(proj_in, "dp", axis=0, tiled=True),
-        lax.all_gather(proj_out, "dp", axis=0, tiled=True),
     )
     input_projection_matrix = in_full.reshape(hidden_width, 3 * channel_count)
     grad_conv_out = contract_simple(grad_branch_conv, out_full) + contract_against(

time: 1200 us -> 1090 us (0.908)
  waiting for transfers between devices: 782 us -> 310 us
  Pallas kernels: 0 us -> 383 us
  local copies, waits for them, and re-layouts: 93.8 us -> 67.8 us
    all_gather x4 -> x0, waiting for transfers between devices: 463 us -> none  [the longest x1 224 us: per_device(): lax.all_gather(gate_up, 'dp', axis=0, tiled=True)]
    pallas_call x0 -> x1, Pallas kernels: none -> 383 us  [gather_all(): pl.pallas_call(functools.partial(gather_kernel, dims, pieces, amount), ou...]
    unnamed x189 -> x195, local copies, waits for them, and re-layouts: 54.2 us -> 36.7 us
    all_gather x1, waiting for transfers between devices: 12.1 us -> 0.02 us  [per_device(): lax.all_gather(normed_one.astype(jnp.bfloat16), 'tensor', axis=0, tiled=T...]
  transfers between devices with their start and end apart: 16 -> 12, of which waited for: 12 -> 7; matrix products, arithmetic and copies ran while one was open for 18% -> 14% of each run, Pallas kernels for 0% -> 35%
where the time goes in v1:
time: 1090 us; the launch traced here: 1080 us
  Pallas kernels  383 us (35%)
  waiting for transfers between devices  310 us (28%)
  matrix products  255 us (23%)
  local copies, waits for them, and re-layouts  67.8 us (6%)
  other arithmetic  42.3 us (4%)
  between operations  16.4 us (2%)
    pallas_call x1, Pallas kernels, gather_all(): pl.pallas_call(functools.partial(gather_kernel, dims, pieces, amount), ou...  383 us
    psum x1, waiting for transfers between devices, per_device(): lax.psum((grad_in_shrink, grad_ffn_shrink, grad_out_expand, grad_down_exp...  145 us
    dot_general x13, matrix products, contract_simple(): return jnp.dot(left, right, preferred_element_type=jnp.float32)  118 us
    psum x1, waiting for transfers between devices, per_device(): lax.psum(grad_in_expand.astype(jnp.bfloat16), 'dp').astype(jnp.float32)  114 us
    dot_general x16, matrix products, contract_against(): lax.dot_general(left, right, (((1,), (1,)), ((), ())), preferred_element_...  108 us
    unnamed x195, local copies, waits for them, and re-layouts  36.7 us
    dot_general x12, matrix products, dot_over_rows(): lax.dot_general(left, right, (((0,), (0,)), ((), ())), preferred_element_...  29.3 us
  transfers between devices with their start and end apart: 12, of which 7 were waited for; matrix products, arithmetic and copies ran while one was open for 14% of the time, Pallas kernels for 35%

profile of v1, /device:TPU:0, one launch (start us, length us, event | category | flops | bytes accessed | tf_op | source)
XLA Modules:
  0.0 1081.5 jit_solution(18023864723884375190)
XLA Ops:
  7.2 1.9 fusion.32
  9.8 3.0 fusion.26
  16.3 383.2 %shard_map.258 = (bf16[4,2,2,96,3072]{4,3,2,1,0:T(8,128)(2,1)}, bf16[4,2,2,96,6912]{4,3,2,1,0:T(8,128)(2,1)}, bf16[4,2,2,96,3456]{4,3,2,1,0:T(8,128)(2,1)}) custom-call(bf16[96,3072]{1,0:T(8,128)(2,1)} %pad_maximum_fusion.1.refs_0_, bf16[96,6912]{1,0:T(8,128)(2,1)} %bitcast.205, bf16[96,3456]{1,0:T(8,128)(2,1)} %refs_2_.1), custom_call_target="tpu_custom_call" | custom-call | tf_op jit(solution)/shard_map/pallas_call | solution.py:140
  399.8 11.0 %fusion.9 = f32[1024,2304]{1,0:T(8,128)S(1)} fusion(bf16[1024,1536]{1,0:T(8,128)(2,1)} %all-gather.5.cloned.1.call-done, bf16[1536,3072]{1,0:T(8,128)(2,1)} %bitcast.245), kind=kOutput, calls=%fused_computation.20 | convolution fusion | flops 7247757312 | bytes 19660800 | tf_op jit(solution)/shard_map/dot_general | solution.py:163
  412.6 5.0 convolution_add_fusion
  417.6 9.7 copy.37
  427.3 8.0 fusion.96
  435.2 3.6 copy.51
  438.8 3.5 copy.52
  442.3 3.5 copy.50
  445.9 3.4 bitcast_multiply_fusion.3
  449.6 2.9 fusion.46
  454.2 6.2 fusion.44
  461.9 2.2 fusion.66
  464.1 2.0 all_gather.21
  466.1 2.9 fusion.97
  469.0 3.5 reduce-scatter.9.cloned.1.call-done
  473.4 16.5 %reduce-scatter.7.cloned.1.call-done = f32[512,1536]{1,0:T(8,128)} async-done(((f32[1024,1536]{1,0:T(8,128)}), f32[512,1536]{1,0:T(8,128)}) %reduce-scatter.7.cloned.1.call-update) | async-done | bytes 3145744 | tf_op jit(solution)/shard_map/reduce_scatter | solution.py:306
  490.0 2.6 multiply_reduce_fusion.1
  492.6 1.6 copy-done.4
  495.8 9.8 all-gather.9.cloned.1.call-done
  505.5 15.6 %fusion.102 = f32[3456,1024]{0,1:T(8,128)S(1)} fusion(bf16[1024,1536]{1,0:T(8,128)(2,1)} %all-gather.9.cloned.1.call-done, bf16[1536,3456]{1,0:T(8,128)(2,1)} %bitcast.243), kind=kOutput, calls=%fused_computation.152 | convolution fusion | flops 10871635968 | bytes 27918336 | tf_op jit(solution)/shard_map/dot_general | solution.py:163
  521.2 7.1 bitcast_add_fusion
  528.3 30.5 %fusion.99 = f32[1024,6912]{1,0:T(8,128)} fusion(bf16[1024,1536]{1,0:T(8,128)(2,1)} %all-gather.7.cloned.1.call-done, bf16[1536,6912]{1,0:T(8,128)(2,1)} %bitcast.241), kind=kOutput, calls=%fused_computation.149 | convolution fusion | flops 21743271936 | bytes 52690944 | tf_op jit(solution)/shard_map/dot_general | solution.py:163
  560.0 12.0 %slice_add_fusion = f32[1024,3456]{1,0:T(8,128)} fusion(f32[1024,6912]{1,0:T(8,128)} %fusion.99, bf16[128,3456]{1,0:T(8,128)(2,1)S(1)} %bitcast.214, bf16[1024,256]{0,1:T(8,128)(2,1)S(1)} %bitcast.206), kind=kOutput, calls=%fused_computation | convolution fusion | flops 909508608 | bytes 29458432 | tf_op jit(solution)/shard_map/dot_general | solution.py:163
  572.0 23.1 %multiply_convert_fusion.1 = (bf16[1024,3456]{1,0:T(8,128)(2,1)}, bf16[1024,3456]{1,0:T(8,128)(2,1)S(1)}, bf16[1024,3456]{1,0:T(8,128)(2,1)}) fusion(f32[1024,3456]{1,0:T(8,128)} %bitcast_add_fusion, f32[1024,3456]{1,0:T(8,128)} %slice_add_fusion, bf16[128,3456]{1,0:T(8,128)(2,1)} %bitcast.228, bf16[1024,256]{0,1:T(8,128)(2,1)} %bitcast.207, ...), kind=kOutput, calls=%fused_computation.8 | convolution fusion | flops 962592768 | bytes 64847872 | tf_op jit(solution)/shard_map/dot_general | solution.py:163
  595.1 8.1 fusion.100
  603.3 2.4 fusion.101
  605.7 3.8 fusion.92
  609.5 3.7 fusion.90
  613.2 34.9 %add_add_fusion = f32[1024,1536]{1,0:T(8,128)} fusion(f32[1024,1536]{1,0:T(8,128)} %fusion.90, f32[1024,1536]{1,0:T(8,128)} %fusion.92, bf16[1536,6912]{1,0:T(8,128)(2,1)} %bitcast.242, bf16[1024,3456]{1,0:T(8,128)(2,1)} %copy-done.12, bf16[1024,3456]{1,0:T(8,128)(2,1)} %get-tuple-element.45), kind=kOutput, calls=%fused_computation.17 | convolution fusion | flops 21774729216 | bytes 54263808 | tf_op jit(solution)/shard_map/dot_general | solution.py:167
  648.2 15.3 %reduce-scatter.15.cloned.1.call-done = f32[512,1536]{1,0:T(8,128)} async-done(((f32[1024,1536]{1,0:T(8,128)}), f32[512,1536]{1,0:T(8,128)}) %reduce-scatter.15.cloned.1.call-update) | async-done | bytes 3145744 | tf_op jit(solution)/shard_map/reduce_scatter | solution.py:385
  663.5 3.5 multiply_reduce_fusion
  667.2 5.0 fusion.94
  672.3 5.7 convolution_convert_fusion.5
  678.1 17.8 %convolution_convert_fusion.3 = bf16[1024,1536]{1,0:T(8,128)(2,1)} fusion(bf16[1024,3456]{1,0:T(8,128)(2,1)} %get-tuple-element.47, bf16[1536,3456]{1,0:T(8,128)(2,1)} %bitcast.244), kind=kOutput, calls=%fused_computation.33 | convolution fusion | flops 10873208832 | bytes 20840448 | tf_op jit(solution)/shard_map/dot_general | solution.py:167
  696.2 1.9 copy.54
  698.1 4.3 fusion.13
  702.5 4.3 fusion.14
  706.8 2.1 convolution_convert_fusion
  712.7 3.1 all_gather.23
  717.0 5.2 fusion.42
  727.0 2.5 fusion.36
  731.4 2.4 maximum_convert_fusion
  733.9 6.7 copy.42
  740.5 4.0 convolution_convert_fusion.4
  746.6 3.3 convolution_multiply_fusion
  752.0 1.8 slice-done.5
  754.3 9.6 fusion.7
  763.9 5.9 fusion.6
  771.0 3.2 fusion.88
  774.2 2.2 convolution_add_fusion.3
  776.4 2.3 fusion.80
  778.8 2.4 fusion.83
  784.2 1.5 convolution_add_fusion.4
  786.7 4.1 fusion.41
  790.8 113.8 %all-reduce.13.cloned.1.call-done = (bf16[8,16,3,768]{3,2,1,0:T(4,128)(2,1)}, bf16[768,8,16]{0,2,1:T(8,128)(2,1)}, bf16[2,8,16,3456]{3,2,1,0:T(8,128)(2,1)}, bf16[3456,8,16]{0,2,1:T(8,128)(2,1)}) async-done(((bf16[8,16,3,768]{3,2,1,0:T(4,128)(2,1)}, bf16[768,8,16]{0,2,1:T(8,128)(2,1)}, bf16[2,8,16,3456]{3,2,1,0:T(8,128)(2,1)}, bf16[3456,8,16]{0,2,1:T(8,128)(2,1)}), (bf16[8,16,3,768]{3,2,1,0:T(4,128)(2,1)}, ...) | async-done | bytes 3440656 | tf_op jit(solution)/shard_map/psum | solution.py:431
  904.6 3.6 reshape.360
  911.5 5.5 reduce-scatter.17.cloned.1.call-done
  917.1 2.3 fusion.27
  919.4 3.5 fusion.31
  922.9 144.9 %all-reduce.11.cloned.1.call-done = (f32[1536,8,16]{0,2,1:T(8,128)}, f32[8,16,1536]{2,1,0:T(8,128)}, f32[1536,2,8,16]{0,3,2,1:T(8,128)}, f32[8,16,1536]{2,1,0:T(8,128)}) async-done(((f32[1536,8,16]{0,2,1:T(8,128)}, f32[8,16,1536]{2,1,0:T(8,128)}, f32[1536,2,8,16]{0,3,2,1:T(8,128)}, f32[8,16,1536]{2,1,0:T(8,128)}), (f32[1536,8,16]{0,2,1:T(8,128)}, f32[8,16,1536]{2,1,0:T(8,128)}, ...) | async-done | bytes 3932176 | tf_op jit(solution)/shard_map/psum | solution.py:427
  1067.9 2.2 copy.66
  1070.1 2.1 copy.67
  (253 shorter events, 40.0 us)
Async XLA Ops:
  7.2 514.0 %copy-start = (bf16[3456,8,16]{0,2,1:T(8,128)(2,1)S(1)}, bf16[3456,8,16]{0,2,1:T(8,128)(2,1)}, u32[]{:S(2)}) copy-start(bf16[3456,8,16]{0,2,1:T(8,128)(2,1)} %param.36) | copy-start | bytes 2654212
  7.2 6.4 copy-start.41
  7.2 392.5 %all-gather.5.cloned.1.call-start = ((), (), s32[]{:S(2)}) async-start(), calls=%async_computation.6 | async-start | bytes 4718592 | tf_op jit(solution)/shard_map/all_gather | solution.py:268
  9.8 5.0 copy-start.53
  12.8 459.6 %reduce-scatter.9.cloned.1.call-start = ((), (), s32[]{:S(2)}) async-start(), calls=%async_computation.8 | async-start | bytes 786432 | tf_op jit(solution)/shard_map/reduce_scatter | solution.py:307
  14.9 384.7 %copy-start.80 = (s32[1,1024]{1,0:T(1,128)S(1)}, s32[1,1024]{1,0:T(1,128)}, u32[]{:S(2)}) copy-start(s32[1,1024]{1,0:T(1,128)} %param.21) | copy-start | bytes 12292
  399.5 159.3 %copy-start.81 = (f32[8]{0:T(128)}, f32[8]{0:T(128)S(1)}, u32[]{:S(2)}) copy-start(f32[8]{0:T(128)S(1)} %compare_convert_fusion.2) | copy-start | bytes 100
  399.6 49.7 %copy-start.67 = (f32[768]{0:T(1024)}, f32[768]{0:T(1024)S(1)}, u32[]{:S(2)}) copy-start(f32[768]{0:T(1024)S(1)} %get-tuple-element.27) | copy-start | bytes 9220
  399.6 49.7 %copy-start.69 = (f32[768]{0:T(1024)}, f32[768]{0:T(1024)S(1)}, u32[]{:S(2)}) copy-start(f32[768]{0:T(1024)S(1)} %get-tuple-element.28) | copy-start | bytes 9220
  399.6 49.7 %copy-start.71 = (f32[768]{0:T(1024)}, f32[768]{0:T(1024)S(1)}, u32[]{:S(2)}) copy-start(f32[768]{0:T(1024)S(1)} %get-tuple-element.26) | copy-start | bytes 9220
  399.7 49.6 %copy-start.63 = (f32[1,1024]{1,0:T(1,128)}, f32[1,1024]{1,0:T(1,128)S(1)}, u32[]{:S(2)}) copy-start(f32[1,1024]{1,0:T(1,128)S(1)} %get-tuple-element.56) | copy-start | bytes 12292
  399.7 49.6 %copy-start.65 = (f32[1,1024]{1,0:T(1,128)}, f32[1,1024]{1,0:T(1,128)S(1)}, u32[]{:S(2)}) copy-start(f32[1,1024]{1,0:T(1,128)S(1)} %get-tuple-element.57) | copy-start | bytes 12292
  399.7 11.0 %copy-start.16 = (bf16[1024,1536]{1,0:T(8,128)(2,1)S(1)}, bf16[1024,1536]{1,0:T(8,128)(2,1)}, u32[]{:S(2)}) copy-start(bf16[1024,1536]{1,0:T(8,128)(2,1)} %all-gather.5.cloned.1.call-done) | copy-start | bytes 9437188
  399.7 11.0 %copy-start.83 = (bf16[1536,8,16]{0,2,1:T(8,128)(2,1)S(1)}, bf16[1536,8,16]{0,2,1:T(8,128)(2,1)}, u32[]{:S(2)}) copy-start(bf16[1536,8,16]{0,2,1:T(8,128)(2,1)} %param.30) | copy-start | bytes 1179652
  445.9 3.7 copy-start.6
  452.5 7.8 copy-start.14
  453.9 36.0 %reduce-scatter.7.cloned.1.call-start = ((), (), s32[]{:S(2)}) async-start(), calls=%async_computation.7 | async-start | bytes 9437184 | tf_op jit(solution)/shard_map/reduce_scatter | solution.py:306
  460.4 45.1 %all-gather.9.cloned.1.call-start = ((), (), s32[]{:S(2)}) async-start(), calls=%async_computation.12 | async-start | bytes 4718592 | tf_op jit(solution)/shard_map/all_gather | solution.py:354
  461.0 67.3 %all-gather.7.cloned.1.call-start = ((), (), s32[]{:S(2)}) async-start(), calls=%async_computation.9 | async-start | bytes 4718592 | tf_op jit(solution)/shard_map/all_gather | solution.py:315
  461.2 11.3 %copy-start.77 = (f32[128]{0:T(128)}, f32[128]{0:T(128)S(1)}, u32[]{:S(2)}) copy-start(f32[128]{0:T(128)S(1)} %mul.364) | copy-start | bytes 1540
  461.9 28.0 %copy-start.8 = (bf16[512,1536]{1,0:T(8,128)(2,1)S(1)}, bf16[512,1536]{1,0:T(8,128)(2,1)}, u32[]{:S(2)}) copy-start(bf16[512,1536]{1,0:T(8,128)(2,1)} %param.19) | copy-start | bytes 4718596
  461.9 28.0 %copy-start.31 = (bf16[8,16,1536]{2,1,0:T(8,128)(2,1)S(1)}, bf16[8,16,1536]{2,1,0:T(8,128)(2,1)}, u32[]{:S(2)}) copy-start(bf16[8,16,1536]{2,1,0:T(8,128)(2,1)} %param.33) | copy-start | bytes 1179652
  466.1 55.1 %copy-start.27 = (bf16[1024,128]{0,1:T(8,128)(2,1)}, bf16[1024,128]{0,1:T(8,128)(2,1)S(1)}, u32[]{:S(2)}) copy-start(bf16[1024,128]{0,1:T(8,128)(2,1)S(1)} %all_gather.21) | copy-start | bytes 786436
  473.4 19.2 %copy-start.38 = (bf16[512,128]{1,0:T(8,128)(2,1)}, bf16[512,128]{1,0:T(8,128)(2,1)S(1)}, u32[]{:S(2)}) copy-start(bf16[512,128]{1,0:T(8,128)(2,1)S(1)} %multiply_convert_fusion.5) | copy-start | bytes 393220
  490.0 4.3 copy-start.60
  495.7 167.8 %reduce-scatter.15.cloned.1.call-start = ((), (), s32[]{:S(2)}) async-start(), calls=%async_computation.13 | async-start | bytes 9437184 | tf_op jit(solution)/shard_map/reduce_scatter | solution.py:385
  528.3 30.5 %copy-start.18 = (bf16[1024,1536]{1,0:T(8,128)(2,1)S(1)}, bf16[1024,1536]{1,0:T(8,128)(2,1)}, u32[]{:S(2)}) copy-start(bf16[1024,1536]{1,0:T(8,128)(2,1)} %all-gather.7.cloned.1.call-done) | copy-start | bytes 9437188
  528.3 30.5 %copy-start.35 = (bf16[1536,2,8,16]{0,3,2,1:T(8,128)(2,1)S(1)}, bf16[1536,2,8,16]{0,3,2,1:T(8,128)(2,1)}, u32[]{:S(2)}) copy-start(bf16[1536,2,8,16]{0,3,2,1:T(8,128)(2,1)} %param.34) | copy-start | bytes 2359300
  559.8 12.2 %copy-start.29 = (bf16[1024,2,8,16]{0,3,2,1:T(8,128)(2,1)}, bf16[1024,2,8,16]{0,3,2,1:T(8,128)(2,1)S(1)}, u32[]{:S(2)}) copy-start(bf16[1024,2,8,16]{0,3,2,1:T(8,128)(2,1)S(1)} %fusion.52) | copy-start | bytes 1572868
  595.1 8.2 copy-start.12
  595.1 8.2 copy-start.34
  603.3 6.3 copy-start.21
  605.7 3.9 copy-start.23
  648.1 15.4 %copy-start.61 = (f32[1536]{0:T(1024)S(1)}, f32[1536]{0:T(1024)}, u32[]{:S(2)}) copy-start(f32[1536]{0:T(1024)} %param.27) | copy-start | bytes 18436
  648.1 15.4 %copy-start.74 = (f32[512]{0:T(512)S(1)}, f32[512]{0:T(512)}, u32[]{:S(2)}) copy-start(f32[512]{0:T(512)} %copy-done.73) | copy-start | bytes 6148
  648.1 18.9 %copy-start.13 = (bf16[512,1536]{1,0:T(8,128)(2,1)S(1)}, bf16[512,1536]{1,0:T(8,128)(2,1)}, u32[]{:S(2)}) copy-start(bf16[512,1536]{1,0:T(8,128)(2,1)} %param.20) | copy-start | bytes 4718596
  648.2 68.8 %all-gather.11.cloned.1.call-start = ((), (), s32[]{:S(2)}) async-start(), calls=%async_computation.14 | async-start | bytes 4718592 | tf_op jit(solution)/shard_map/all_gather | solution.py:394
  663.5 3.7 copy-start.5
  672.3 104.1 %reduce-scatter.13.cloned.1.call-start = ((), (), s32[]{:S(2)}) async-start(), calls=%async_computation.11 | async-start | bytes 393216 | tf_op jit(solution)/shard_map/reduce_scatter | solution.py:339
  678.0 107.7 %reduce-scatter.11.cloned.1.call-start = ((), (), s32[]{:S(2)}) async-start(), calls=%async_computation.10 | async-start | bytes 4718592 | tf_op jit(solution)/shard_map/reduce_scatter | solution.py:336
  695.9 208.7 %all-reduce.13.cloned.1.call-start = ((), (), s32[]{:S(2)}) async-start(), calls=%async_computation.17 | async-start | bytes 7274496 | tf_op jit(solution)/shard_map/psum | solution.py:431
  698.1 8.6 slice-start
  702.4 4.3 slice-start.1
  702.4 4.3 copy-start.28
  708.9 3.3 copy-start.78
  711.6 4.3 copy-start.15
  717.0 5.3 copy-start.46
  733.9 6.7 copy-start.43
  745.6 171.4 %reduce-scatter.17.cloned.1.call-start = ((), (), s32[]{:S(2)}) async-start(), calls=%async_computation.15 | async-start | bytes 4718592 | tf_op jit(solution)/shard_map/reduce_scatter | solution.py:420
  746.6 4.3 slice-start.2
  746.6 5.2 slice-start.4
  749.9 14.0 %copy-start.50 = (f32[1024,8,16]{0,2,1:T(8,128)}, f32[1024,8,16]{0,2,1:T(8,128)S(1)}, u32[]{:S(2)}) copy-start(f32[1024,8,16]{0,2,1:T(8,128)S(1)} %convolution_multiply_fusion) | copy-start | bytes 1572868
  749.9 3.8 slice-start.5
  750.0 4.3 slice-start.6
  769.8 298.0 %all-reduce.11.cloned.1.call-start = ((), (), s32[]{:S(2)}) async-start(), calls=%async_computation.16 | async-start | bytes 7864320 | tf_op jit(solution)/shard_map/psum | solution.py:427
  776.4 4.8 copy-start.39
  776.4 4.8 copy-start.2
  904.6 3.7 copy-start.44
  904.6 5.0 copy-start.48
  908.3 8.8 copy-start.9
  908.3 8.8 copy-start.62
  908.3 8.8 copy-start.76
  1067.8 4.3 copy-start.40
  1067.9 5.4 copy-start.47
  (40 other events, 75.9 us)
Sparse Core Ops, SparseCore 0:
  13.0 14.8 all-gather.4
  454.1 18.3 reduce-scatter.8
  474.8 15.1 reduce-scatter.6
  491.3 14.1 all-gather.8
  507.5 13.2 all-gather.6
  648.3 15.1 reduce-scatter.14
  672.4 14.1 all-gather.10
  689.4 8.9 reduce-scatter.12
  700.6 12.2 reduce-scatter.10
  745.7 158.8 all-reduce.12
  906.9 10.1 reduce-scatter.16
  924.2 143.6 all-reduce.10

commit v2 on v0

v2 whole, which is shorter than its diff:
```python
import functools
import types

import jax
import jax.numpy as jnp
from jax import lax
from jax.experimental import pallas as pl
from jax.experimental.pallas import tpu as pltpu
from jax.sharding import PartitionSpec as P

ADAPTER_COUNT = 8
ADAPTER_RANK = 16
EPSILON = 1e-05
MESH = pl.DeviceIdType.MESH
LANES = 128
HIDDEN_CHUNK = 384
ROW_TILE = 256


def dot(left, right):
    return jnp.dot(left, right, preferred_element_type=jnp.float32)


def dot_against(left, right):
    return lax.dot_general(
        left, right, (((1,), (1,)), ((), ())), preferred_element_type=jnp.float32
    )


def split_pair(values):
    upper = values.astype(jnp.bfloat16)
    lower = (values - upper.astype(jnp.float32)).astype(jnp.bfloat16)
    return (upper, lower)


def norm_factor(values):
    return lax.rsqrt(jnp.mean(values * values, axis=-1, keepdims=True) + EPSILON)


def normalize_back(values, factor, gain, grad):
    unit = values * factor
    scaled = grad * gain
    return factor * (scaled - unit * jnp.mean(scaled * unit, axis=-1, keepdims=True))


def split_ring(count):
    if count % 16 == 0:
        return (4, count // 8, 2)
    return (count, 1, 1)


def position(index, dims):
    return (index // (dims[1] * dims[2]), (index // dims[2]) % dims[1], index % dims[2])


def flat(spot, dims):
    return (spot[0] * dims[1] + spot[1]) * dims[2] + spot[2]


class Gather:
    def __init__(self, dims, spot, send, recv):
        self.dims, self.spot, self.send, self.recv = dims, spot, send, recv

    def copies(self, piece, step):
        shard, whole, columns, order, row = piece
        axis = order[step]
        place = tuple(
            slice(None) if other in order[:step] else self.spot[other] for other in range(3)
        )
        target = whole.at[place + (slice(None), columns)]
        base = sum(self.dims[other] - 1 for other in order[:step])
        out = []
        for offset in range(1, self.dims[axis]):
            peer = list(self.spot)
            peer[axis] = lax.rem(self.spot[axis] + offset, self.dims[axis])
            out.append(
                pltpu.make_async_remote_copy(
                    src_ref=shard.at[:, columns] if step == 0 else target,
                    dst_ref=target,
                    send_sem=self.send.at[row, base + offset - 1],
                    recv_sem=self.recv.at[row, base + offset - 1],
                    device_id={"dp": flat(peer, self.dims)},
                    device_id_type=MESH,
                )
            )
        return out

    def start(self, pieces, step):
        for piece in pieces:
            for copy in self.copies(piece, step):
                copy.start()

    def arrive(self, pieces, step):
        for piece in pieces:
            for copy in self.copies(piece, step):
                copy.wait_recv()

    def drain(self, pieces):
        for piece in pieces:
            for step in range(3):
                for copy in self.copies(piece, step):
                    copy.wait_send()


def greet(dims, spot, team, member):
    barrier = pltpu.get_barrier_semaphore()
    count = 0
    for axis in range(3):
        for offset in range(1, dims[axis]):
            peer = list(spot)
            peer[axis] = lax.rem(spot[axis] + offset, dims[axis])
            pl.semaphore_signal(
                barrier, inc=1, device_id={"dp": flat(peer, dims)}, device_id_type=MESH
            )
            count += 1
    for offset in range(1, team):
        pl.semaphore_signal(
            barrier,
            inc=1,
            device_id={"tensor": lax.rem(member + offset, team)},
            device_id_type=MESH,
        )
        count += 1
    pl.semaphore_wait(barrier, count)


NAMES = (
    "io_shard",
    "ff_shard",
    "x_own",
    "g_own",
    "expand",
    "down_shrink",
    "same",
    "conv_gain",
    "ffn_gain",
    "taps",
    "in_reduce",
    "in_lift",
    "out_reduce",
    "out_lift",
    "ffn_reduce",
    "down_lift",
    "io_whole",
    "ff_whole",
    "streams",
    "norm_one",
    "conv_out",
    "code_in",
    "code_out",
    "block_out",
    "grad_x_two",
    "ffn_split",
    "ffn_rep",
    "x_all",
    "g_all",
    "na",
    "nb",
    "w",
    "acc_a",
    "acc_b",
    "x_two",
    "halo",
    "co",
    "cp",
    "gcf",
    "cf",
    "gd",
    "cft",
    "gdt",
    "act",
    "ggu",
    "eb",
    "dsb",
    "rb",
    "rc",
    "rd",
    "code_t",
    "send",
    "recv",
    "team_send",
    "team_recv",
    "local",
    "load_sem",
)


def forward_kernel(shape, *refs):
    s = types.SimpleNamespace(**dict(zip(NAMES, refs)))
    dims, team, width, channels, length, chunks = shape
    own = length // team
    hc = HIDDEN_CHUNK
    tile = ROW_TILE
    tiles = length // tile
    member = lax.axis_index("tensor")
    spot = position(lax.axis_index("dp"), dims)
    gather = Gather(dims, spot, s.send, s.recv)
    own_rows = pl.ds(pl.multiple_of(member * own, own), own)

    io_step = 4 * channels // 6
    io_pieces = []
    for i in range(6):
        half = io_step // 2
        io_pieces.append(
            [
                (s.io_shard, s.io_whole, pl.ds(i * io_step, half), (0, 1, 2), 2 * i),
                (s.io_shard, s.io_whole, pl.ds(i * io_step + half, half), (0, 2, 1), 2 * i + 1),
            ]
        )
    last = chunks - 1
    cut = 640

    def chunk_pieces(k, orders=((0, 1, 2), (0, 2, 1))):
        shard, whole = s.ff_shard.at[k], s.ff_whole.at[k]
        return [
            (shard, whole, pl.ds(0, cut), orders[0], 12 + 2 * k),
            (shard, whole, pl.ds(cut, 3 * hc - cut), orders[1], 13 + 2 * k),
        ]

    tail_pieces = chunk_pieces(last, ((1, 2, 0), (2, 1, 0)))

    def team_copies(row, source, target):
        out = []
        for offset in range(1, team):
            peer = lax.rem(member + offset, team)
            out.append(
                pltpu.make_async_remote_copy(
                    src_ref=source(peer, offset),
                    dst_ref=target(peer, offset),
                    send_sem=s.team_send.at[row, offset - 1],
                    recv_sem=s.team_recv.at[row, offset - 1],
                    device_id={"tensor": peer},
                    device_id_type=MESH,
                )
            )
        return out

    def rows_of(ref):
        return lambda peer, offset: ref.at[pl.ds(pl.multiple_of(peer * own, own), own)]

    def slot_of(ref):
        return lambda peer, offset: ref.at[offset - 1]

    greet(dims, spot, team, member)
    x_copies = team_copies(0, lambda p, o: s.x_own, lambda p, o: s.x_all.at[own_rows])
    g_copies = team_copies(1, lambda p, o: s.g_own, lambda p, o: s.g_all.at[own_rows])
    for copy in x_copies + g_copies:
        copy.start()
    x_here = pltpu.make_async_copy(s.x_own, s.x_all.at[own_rows], s.local.at[0])
    g_here = pltpu.make_async_copy(s.g_own, s.g_all.at[own_rows], s.local.at[1])
    x_here.start()
    g_here.start()

    def bounce(k):
        spare = s.w.at[(1 + k // 2) // (dims[1] * dims[2]), ((1 + k // 2) // dims[2]) % dims[1], (1 + k // 2) % dims[2]]
        return spare.at[:, pl.ds((k % 2) * 3 * hc, 3 * hc)]

    io_spare = s.w.at[0, 0, 0, :, pl.ds(0, 4 * channels)]
    ins = [pltpu.make_async_copy(s.io_shard, io_spare, s.local.at[2])]
    outs = [pltpu.make_async_copy(io_spare, s.io_whole.at[spot], s.local.at[2])]
    for k in range(chunks):
        ins.append(pltpu.make_async_copy(s.ff_shard.at[k], bounce(k), s.local.at[3 + k]))
        outs.append(pltpu.make_async_copy(bounce(k), s.ff_whole.at[(k,) + spot], s.local.at[3 + k]))
    for copy in ins:
        copy.start()
    for pieces in io_pieces:
        gather.start(pieces, 0)
    gather.start(tail_pieces, 0)
    for k in range(last):
        gather.start(chunk_pieces(k), 0)
    for first, second in zip(ins, outs):
        first.wait()
        second.start()

    x_here.wait()
    for copy in x_copies:
        copy.wait_recv()

    def first_norm(i, carry):
        rows = pl.ds(pl.multiple_of(i * tile, tile), tile)
        values = s.x_all[rows, :].astype(jnp.float32)
        s.na[rows, :] = (values * norm_factor(values) * s.conv_gain[...]).astype(jnp.bfloat16)
        return carry

    lax.fori_loop(0, tiles, first_norm, 0)
    norm_store = pltpu.make_async_copy(s.na, s.norm_one, s.local.at[0])
    norm_store.start()
    g_here.wait()
    for copy in g_copies:
        copy.wait_recv()

    def down_codes(i, carry):
        rows = pl.ds(pl.multiple_of(i * tile, tile), tile)
        code = dot_against(s.g_all[rows, :], s.down_lift[...])
        s.gd[rows, :] = code.astype(jnp.bfloat16)
        s.gdt[:, rows] = jnp.transpose(code)[:16].astype(jnp.bfloat16)
        return carry

    lax.fori_loop(0, tiles, down_codes, 0)
    for copy in outs:
        copy.wait()

    for i in range(7):
        if i < 6:
            gather.arrive(io_pieces[i], 0)
            gather.start(io_pieces[i], 1)
        if i > 0:
            gather.arrive(io_pieces[i - 1], 1)
            gather.start(io_pieces[i - 1], 2)
    gather.arrive(tail_pieces, 0)
    gather.start(tail_pieces, 1)
    gather.arrive(chunk_pieces(0), 0)
    gather.start(chunk_pieces(0), 1)
    io_loads = []
    for i in range(6):
        gather.arrive(io_pieces[i], 2)
        columns = pl.ds(i * io_step, io_step)
        load = pltpu.make_async_copy(
            s.io_whole.at[:, :, :, :, columns], s.w.at[:, :, :, :, columns], s.load_sem.at[i]
        )
        load.start()
        io_loads.append(load)
    gather.arrive(tail_pieces, 1)
    gather.start(tail_pieces, 2)
    gather.arrive(chunk_pieces(0), 1)
    gather.start(chunk_pieces(0), 2)
    gather.arrive(chunk_pieces(1), 0)
    gather.start(chunk_pieces(1), 1)
    norm_store.wait()
    for load in io_loads:
        load.wait()

    def weights(first, count):
        return s.w[:, :, :, :, pl.ds(first, count)].reshape(width, count)

    s.halo[pl.ds(0, 8), :] = jnp.zeros((8, channels), jnp.float32)

    def convolve(i, carry):
        rows = pl.ds(pl.multiple_of(i * tile, tile), tile)
        normed = s.na[rows, :]
        code = dot(normed, s.in_reduce[...])
        s.code_in[:, rows] = jnp.transpose(code)[:16].astype(jnp.bfloat16)
        code = code.astype(jnp.bfloat16)
        lanes = []
        for lane in range(3):
            value = dot(normed, weights(lane * channels, channels)) + dot(
                code, s.in_lift[:, pl.ds(lane * channels, channels)]
            )
            lanes.append(value)
            if lane < 2:
                s.acc_a[rows, pl.ds(lane * channels, channels)] = value
            else:
                s.acc_b[rows, pl.ds(0, channels)] = value
        product = lanes[0] * lanes[2]
        s.halo[pl.ds(8, tile), :] = product
        masks = s.same[rows, :]
        mixed = (
            s.taps[0:1, :] * product
            + s.taps[1:2, :] * s.halo[pl.ds(7, tile), :] * masks[:, 0:1]
            + s.taps[2:3, :] * s.halo[pl.ds(6, tile), :] * masks[:, 1:2]
        )
        s.halo[pl.ds(0, 8), :] = s.halo[pl.ds(tile, 8), :]
        convolved = (lanes[1] * mixed).astype(jnp.bfloat16)
        s.co[rows, :] = convolved
        s.na[rows, :] = dot_against(convolved, weights(3 * channels, channels)).astype(jnp.bfloat16)
        s.cp[rows, :] = dot(convolved, s.out_reduce[...])
        return carry

    lax.fori_loop(0, tiles, convolve, 0)
    stores = [
        pltpu.make_async_copy(s.acc_a.at[:, pl.ds(0, channels)], s.streams.at[0], s.local.at[3]),
        pltpu.make_async_copy(
            s.acc_a.at[:, pl.ds(channels, channels)], s.streams.at[1], s.local.at[4]
        ),
        pltpu.make_async_copy(s.acc_b.at[:, pl.ds(0, channels)], s.streams.at[2], s.local.at[5]),
        pltpu.make_async_copy(s.co, s.conv_out, s.local.at[6]),
    ]
    for copy in stores:
        copy.start()

    branch = team_copies(2, rows_of(s.na), slot_of(s.rb))
    codes = team_copies(3, rows_of(s.cp), slot_of(s.rc))
    for copy in codes + branch:
        copy.start()
    gather.arrive(chunk_pieces(1), 1)
    gather.start(chunk_pieces(1), 2)
    gather.arrive(chunk_pieces(2), 0)
    gather.start(chunk_pieces(2), 1)

    def load(c):
        slot = lax.rem(c, 2)
        columns = pl.ds(pl.multiple_of(slot * 3 * hc, LANES), 3 * hc)
        return [
            pltpu.make_async_copy(
                s.ff_whole.at[c], s.w.at[:, :, :, :, columns], s.load_sem.at[3 * slot]
            ),
            pltpu.make_async_copy(s.expand.at[c], s.eb.at[slot], s.load_sem.at[3 * slot + 1]),
            pltpu.make_async_copy(s.down_shrink.at[c], s.dsb.at[slot], s.load_sem.at[3 * slot + 2]),
        ]

    for copy in branch + codes:
        copy.wait_recv()
    code = s.cp[own_rows, :]
    for peer in range(team - 1):
        code = code + s.rc[peer]
    s.code_out[...] = jnp.transpose(code)[:16].astype(jnp.bfloat16)
    s.cf[pl.ds(0, own), :] = code.astype(jnp.bfloat16)

    own_tile = min(own, tile)

    def second_norm(i, carry):
        local_rows = pl.ds(pl.multiple_of(i * own_tile, own_tile), own_tile)
        rows = pl.ds(pl.multiple_of(member * own + i * own_tile, own_tile), own_tile)
        values = s.x_all[rows, :].astype(jnp.float32) + s.na[rows, :].astype(jnp.float32)
        for peer in range(team - 1):
            values = values + s.rb[peer, local_rows, :].astype(jnp.float32)
        values = values + dot(s.cf[local_rows, :], s.out_lift[...])
        s.x_two[local_rows, :] = values
        s.nb[rows, :] = (values * norm_factor(values) * s.ffn_gain[...]).astype(jnp.bfloat16)
        return carry

    lax.fori_loop(0, own // own_tile, second_norm, 0)
    norms = team_copies(4, lambda p, o: s.nb.at[own_rows], lambda p, o: s.nb.at[own_rows])
    for copy in norms:
        copy.start()
    gather.arrive(chunk_pieces(0), 2)
    for copy in load(0):
        copy.start()
    for copy in stores:
        copy.wait()
    s.acc_a[...] = jnp.zeros_like(s.acc_a)
    s.acc_b[...] = jnp.zeros_like(s.acc_b)
    for copy in branch + codes:
        copy.wait_send()
    s.cp[...] = jnp.zeros_like(s.cp)
    s.gcf[...] = jnp.zeros_like(s.gcf)
    for copy in norms:
        copy.wait_recv()

    def ffn_codes(i, carry):
        rows = pl.ds(pl.multiple_of(i * tile, tile), tile)
        value = dot(s.nb[rows, :], s.ffn_reduce[...])
        s.cf[rows, :] = value.astype(jnp.bfloat16)
        s.cft[:, rows] = jnp.transpose(value)[:32].astype(jnp.bfloat16)
        return carry

    lax.fori_loop(0, tiles, ffn_codes, 0)

    def chunk(c, carry):
        @pl.when(c + 3 < last)
        def _():
            gather.arrive(chunk_pieces(c + 3), 0)
            gather.start(chunk_pieces(c + 3), 1)

        @pl.when(c + 2 < last)
        def _():
            gather.arrive(chunk_pieces(c + 2), 1)
            gather.start(chunk_pieces(c + 2), 2)

        @pl.when(c + 1 < last)
        def _():
            gather.arrive(chunk_pieces(c + 1), 2)

        @pl.when(c + 1 == last)
        def _():
            gather.arrive(tail_pieces, 2)

        @pl.when(c + 1 < chunks)
        def _():
            for copy in load(c + 1):
                copy.start()

        for copy in load(c):
            copy.wait()
        slot = lax.rem(c, 2)
        first = pl.multiple_of(slot * 3 * hc, LANES)
        down_first = pl.multiple_of(slot * 3 * hc + 2 * hc, LANES)

        def row_tile(i, inner):
            rows = pl.ds(pl.multiple_of(i * tile, tile), tile)
            both = dot(s.nb[rows, :], weights(first, 2 * hc)) + dot(s.cf[rows, :], s.eb[slot])
            grad = dot(s.g_all[rows, :], weights(down_first, hc)) + dot_against(
                s.gd[rows, :], s.dsb[slot]
            )
            gate, up = both[:, :hc], both[:, hc:]
            gated = jax.nn.sigmoid(gate)
            silu = gate * gated
            act = (silu * up).astype(jnp.bfloat16)
            s.act[rows, :] = act
            s.ggu[rows, pl.ds(0, hc)] = (grad * up * gated * (1.0 + gate * (1.0 - gated))).astype(
                jnp.bfloat16
            )
            s.ggu[rows, pl.ds(hc, hc)] = (grad * silu).astype(jnp.bfloat16)
            s.acc_a[rows, :] += dot_against(act, weights(down_first, hc))
            s.cp[rows, :] += dot(act, s.dsb[slot])
            ggu = s.ggu[rows, :]
            s.acc_b[rows, :] += dot_against(ggu, weights(first, 2 * hc))
            s.gcf[rows, :] += dot_against(ggu, s.eb[slot])
            return inner

        lax.fori_loop(0, tiles, row_tile, 0)
        at = pl.multiple_of(c * hc, LANES)
        padded = chunks * hc
        spread = dot(s.cft[...], s.ggu[...])
        s.ffn_split[:, pl.ds(at, hc)] = spread[:16, :hc].astype(jnp.bfloat16)
        s.ffn_split[:, pl.ds(padded + at, hc)] = spread[16:, hc:].astype(jnp.bfloat16)
        shrunk = dot(s.gdt[...], s.act[...])
        s.ffn_split[:, pl.ds(2 * padded + at, hc)] = shrunk.astype(jnp.bfloat16)
        return carry

    lax.fori_loop(0, chunks, chunk, 0)

    def finish(i, carry):
        rows = pl.ds(pl.multiple_of(i * tile, tile), tile)
        s.na[rows, :] = s.acc_a[rows, :].astype(jnp.bfloat16)
        value = s.gcf[rows, :]
        s.code_t[:, rows] = jnp.transpose(value)[:32]
        upper, lower = split_pair(value)
        total = (
            s.acc_b[rows, :]
            + dot_against(upper, s.ffn_reduce[...])
            + dot_against(lower, s.ffn_reduce[...])
        )
        s.x_all[rows, :] = total.astype(jnp.bfloat16)
        return carry

    lax.fori_loop(0, tiles, finish, 0)
    grads = team_copies(5, rows_of(s.x_all), slot_of(s.rd))
    downs = team_copies(6, rows_of(s.na), slot_of(s.rb))
    codes = team_copies(7, rows_of(s.cp), slot_of(s.rc))
    for copy in grads + codes + downs:
        copy.start()
    upper, lower = split_pair(s.code_t[...])
    shrunk = (dot(upper, s.nb[...]) + dot(lower, s.nb[...])).astype(jnp.bfloat16)
    s.ffn_rep[:, pl.ds(0, width)] = shrunk[:16]
    s.ffn_rep[:, pl.ds(width, width)] = shrunk[16:]
    for copy in grads + codes + downs:
        copy.wait_recv()
    code = s.cp[own_rows, :]
    for peer in range(team - 1):
        code = code + s.rc[peer]
    rounded = code.astype(jnp.bfloat16)
    s.cf[pl.ds(0, own), :] = rounded
    turned = jnp.transpose(code)[:16].astype(jnp.bfloat16)
    s.ffn_rep[:, pl.ds(2 * width, width)] = dot(turned, s.g_all[own_rows, :]).astype(jnp.bfloat16)
    for copy in norms + grads + downs:
        copy.wait_send()

    def last_rows(i, carry):
        local_rows = pl.ds(pl.multiple_of(i * own_tile, own_tile), own_tile)
        rows = pl.ds(pl.multiple_of(member * own + i * own_tile, own_tile), own_tile)
        values = s.x_two[local_rows, :]
        down = s.acc_a[rows, :]
        grad = s.acc_b[rows, :]
        upper, lower = split_pair(s.gcf[rows, :])
        grad = grad + dot_against(upper, s.ffn_reduce[...]) + dot_against(lower, s.ffn_reduce[...])
        for peer in range(team - 1):
            down = down + s.rb[peer, local_rows, :].astype(jnp.float32)
            grad = grad + s.rd[peer, local_rows, :].astype(jnp.float32)
        out = values + down + dot(s.cf[local_rows, :], s.down_lift[...])
        s.nb[local_rows, :] = out.astype(jnp.bfloat16)
        s.x_two[local_rows, :] = s.g_all[rows, :].astype(jnp.float32) + normalize_back(
            values, norm_factor(values), s.ffn_gain[...], grad
        )
        return carry

    lax.fori_loop(0, own // own_tile, last_rows, 0)
    results = [
        pltpu.make_async_copy(s.nb.at[pl.ds(0, own)], s.block_out, s.local.at[0]),
        pltpu.make_async_copy(s.x_two, s.grad_x_two, s.local.at[1]),
    ]
    for copy in results:
        copy.start()
    for copy in x_copies + g_copies + codes:
        copy.wait_send()
    for pieces in io_pieces:
        gather.drain(pieces)
    gather.drain(tail_pieces)

    def drain(k, carry):
        gather.drain(chunk_pieces(k))
        return carry

    lax.fori_loop(0, last, drain, 0)
    for copy in results:
        copy.wait()


def forward_and_ffn(dims, team, operands):
    io_shard, ff_shard, x_own = operands[:3]
    rows = io_shard.shape[0]
    channels = io_shard.shape[1] // 4
    chunks = ff_shard.shape[0]
    own, width = x_own.shape
    length = own * team
    hc = HIDDEN_CHUNK
    columns = max(4 * channels, 6 * hc)
    lanes = sum(d - 1 for d in dims)
    shape = (dims, team, width, channels, length, chunks)
    bf16, f32 = jnp.bfloat16, jnp.float32
    anywhere = pl.BlockSpec(memory_space=pl.ANY)
    vmem = pl.BlockSpec(memory_space=pltpu.VMEM)
    outs = [
        (dims + (rows, 4 * channels), bf16, anywhere),
        ((chunks,) + dims + (rows, 3 * hc), bf16, anywhere),
        ((3, length, channels), f32, anywhere),
        ((length, width), bf16, anywhere),
        ((length, channels), bf16, anywhere),
        ((16, length), bf16, vmem),
        ((16, own), bf16, vmem),
        ((own, width), bf16, anywhere),
        ((own, width), f32, anywhere),
        ((16, 3 * chunks * hc), bf16, vmem),
        ((16, 3 * width), bf16, vmem),
    ]
    peers = max(team - 1, 1)
    row_count = 12 + 2 * chunks
    scratch = [
        pltpu.VMEM((length, width), bf16),
        pltpu.VMEM((length, width), bf16),
        pltpu.VMEM((length, width), bf16),
        pltpu.VMEM((length, width), bf16),
        pltpu.VMEM(dims + (rows, columns), bf16),
        pltpu.VMEM((length, width), f32),
        pltpu.VMEM((length, width), f32),
        pltpu.VMEM((own, width), f32),
        pltpu.VMEM((ROW_TILE + 8, channels), f32),
        pltpu.VMEM((length, channels), bf16),
        pltpu.VMEM((length, LANES), f32),
        pltpu.VMEM((length, LANES), f32),
        pltpu.VMEM((length, LANES), bf16),
        pltpu.VMEM((length, LANES), bf16),
        pltpu.VMEM((32, length), bf16),
        pltpu.VMEM((16, length), bf16),
        pltpu.VMEM((length, hc), bf16),
        pltpu.VMEM((length, 2 * hc), bf16),
        pltpu.VMEM((2, LANES, 2 * hc), bf16),
        pltpu.VMEM((2, hc, LANES), bf16),
        pltpu.VMEM((peers, own, width), bf16),
        pltpu.VMEM((peers, own, LANES), f32),
        pltpu.VMEM((peers, own, width), bf16),
        pltpu.VMEM((32, length), f32),
        pltpu.SemaphoreType.DMA((row_count, lanes)),
        pltpu.SemaphoreType.DMA((row_count, lanes)),
        pltpu.SemaphoreType.DMA((8, peers)),
        pltpu.SemaphoreType.DMA((8, peers)),
        pltpu.SemaphoreType.DMA((max(3 + chunks, 8),)),
        pltpu.SemaphoreType.DMA((6,)),
    ]
    return pl.pallas_call(
        functools.partial(forward_kernel, shape),
        out_shape=[jax.ShapeDtypeStruct(o[0], o[1]) for o in outs],
        in_specs=[anywhere] * 6 + [vmem] * 10,
        out_specs=[o[2] for o in outs],
        scratch_shapes=scratch,
        compiler_params=pltpu.CompilerParams(
            collective_id=0, has_side_effects=True, vmem_limit_bytes=67043328
        ),
    )(*operands)


BACK_NAMES = (
    "grad_x_two",
    "ffn_split",
    "ffn_rep",
    "io_whole",
    "streams",
    "norm_one",
    "conv_out",
    "x_own",
    "code_in",
    "code_out",
    "same",
    "conv_gain",
    "taps",
    "in_reduce",
    "in_lift",
    "out_reduce",
    "out_lift",
    "onehot",
    "grad_residual",
    "early",
    "late",
    "early_rep",
    "late_rep",
    "w",
    "gx",
    "gb",
    "gco",
    "gcot",
    "st",
    "gs",
    "ha",
    "hb",
    "halo",
    "na",
    "co",
    "pb",
    "gcit",
    "xo",
    "rb",
    "rep_a",
    "rep_b",
    "got_a",
    "got_b",
    "flat_a",
    "flat_b",
    "part_a",
    "part_b",
    "from_a",
    "from_b",
    "sum_a",
    "sum_b",
    "spare_a",
    "spare_b",
    "out",
    "send",
    "recv",
    "swap_send",
    "swap_recv",
    "team_send",
    "team_recv",
    "local",
)


class Share:
    def __init__(self, count, team, split, shared):
        self.split, self.shared, self.share = split, shared, shared // team
        self.total = split + self.share
        self.block = -(-self.total // (LANES * count)) * LANES
        self.first = split // self.block
        self.blocks = -(-self.total // self.block) - self.first


def backward_kernel(shape, *refs):
    s = types.SimpleNamespace(**dict(zip(BACK_NAMES, refs)))
    dims, team, width, channels, length, early, late = shape
    count = dims[0] * dims[1] * dims[2]
    own = length // team
    tile = ROW_TILE
    tiles = length // tile
    own_tile = min(own, tile)
    member = lax.axis_index("tensor")
    me = lax.axis_index("dp")
    spot = position(me, dims)
    gather = Gather(dims, spot, s.send, s.recv)
    own_rows = pl.ds(pl.multiple_of(member * own, own), own)

    barrier = pltpu.get_barrier_semaphore()
    for offset in range(1, count):
        pl.semaphore_signal(
            barrier, inc=1, device_id={"dp": lax.rem(me + offset, count)}, device_id_type=MESH
        )
    for offset in range(1, team):
        pl.semaphore_signal(
            barrier,
            inc=1,
            device_id={"tensor": lax.rem(member + offset, team)},
            device_id_type=MESH,
        )
    pl.semaphore_wait(barrier, count - 1 + team - 1)

    def team_copies(row, source, target):
        out = []
        for offset in range(1, team):
            peer = lax.rem(member + offset, team)
            out.append(
                pltpu.make_async_remote_copy(
                    src_ref=source(peer, offset),
                    dst_ref=target(peer, offset),
                    send_sem=s.team_send.at[row, offset - 1],
                    recv_sem=s.team_recv.at[row, offset - 1],
                    device_id={"tensor": peer},
                    device_id_type=MESH,
                )
            )
        return out

    def swap_copies(row, part, landing):
        out = []
        for offset in range(1, count):
            peer = lax.rem(me + offset, count)
            out.append(
                pltpu.make_async_remote_copy(
                    src_ref=part.at[peer],
                    dst_ref=landing.at[me],
                    send_sem=s.swap_send.at[row, offset - 1],
                    recv_sem=s.swap_recv.at[row, offset - 1],
                    device_id={"dp": peer},
                    device_id_type=MESH,
                )
            )
        return out

    def pieces_of(share, total, whole, row):
        cut = (share.block // 256) * 128
        if cut == 0:
            return [(total, whole, pl.ds(0, share.block), (0, 1, 2), row)]
        return [
            (total, whole, pl.ds(0, cut), (0, 1, 2), row),
            (total, whole, pl.ds(cut, share.block - cut), (0, 2, 1), row + 1),
        ]

    def hand_out(share, columns, part, landing, row):
        for peer in range(count):
            part[peer, :, pl.ds(0, share.block)] = columns[:, pl.ds(peer * share.block, share.block)]
            part[peer, :, pl.ds(share.block, LANES)] = s.onehot[...]
        landing[me] = part[me]
        copies = swap_copies(row, part, landing)
        for copy in copies:
            copy.start()
        return copies

    def take_in(share, landing, total):
        for adapter in range(ADAPTER_COUNT):

            def add(source, value):
                mask = landing[source, adapter : adapter + 1, pl.ds(share.block, LANES)]
                mask = mask.astype(jnp.float32)[:, 0:1]
                return value + mask * landing[source, :, pl.ds(0, share.block)].astype(jnp.float32)

            value = lax.fori_loop(0, count, add, jnp.zeros((16, share.block), jnp.float32))
            total[pl.ds(adapter * 16, 16), :] = value.astype(jnp.bfloat16)

    def shared_slice(share):
        return lambda peer, offset: pl.ds(pl.multiple_of(peer * share.share, LANES), share.share)

    def sum_shared(share, rep, got, columns):
        value = rep[:, pl.ds(pl.multiple_of(member * share.share, LANES), share.share)].astype(
            jnp.float32
        )
        for peer in range(team - 1):
            value = value + got[peer].astype(jnp.float32)
        columns[:, pl.ds(share.split, share.share)] = value.astype(jnp.bfloat16)
        rest = count * share.block - share.total
        if rest:
            columns[:, pl.ds(share.total, rest)] = jnp.zeros((16, rest), jnp.bfloat16)

    loads = {}
    for slot, (name, source, target) in enumerate(
        [
            ("gx", s.grad_x_two, s.gx),
            ("rep", s.ffn_rep, s.rep_a.at[:, pl.ds(0, 3 * width)]),
            ("split", s.ffn_split, s.flat_a.at[:, pl.ds(0, early.split - channels)]),
            ("co", s.conv_out, s.co),
            ("w", s.io_whole, s.w),
            ("b", s.streams.at[0], s.st.at[0, pl.ds(8, length)]),
            ("c", s.streams.at[1], s.st.at[1, pl.ds(8, length)]),
            ("x", s.streams.at[2], s.st.at[2, pl.ds(8, length)]),
            ("na", s.norm_one, s.na),
            ("xo", s.x_own, s.xo),
        ]
    ):
        loads[name] = pltpu.make_async_copy(source, target, s.local.at[slot])
        loads[name].start()
    s.st[0, pl.ds(0, 8), :] = jnp.zeros((8, channels), jnp.float32)
    s.st[2, pl.ds(0, 8), :] = jnp.zeros((8, channels), jnp.float32)
    s.ha[pl.ds(tile, 8), :] = jnp.zeros((8, channels), jnp.float32)
    s.hb[pl.ds(tile, 8), :] = jnp.zeros((8, channels), jnp.float32)

    loads["gx"].wait()

    def branch_rows(i, carry):
        local_rows = pl.ds(pl.multiple_of(i * own_tile, own_tile), own_tile)
        rows = pl.ds(pl.multiple_of(member * own + i * own_tile, own_tile), own_tile)
        upper, lower = split_pair(s.gx[local_rows, :])
        s.gb[rows, :] = upper
        code = dot_against(upper, s.out_lift[...]) + dot_against(lower, s.out_lift[...])
        s.gco[rows, :] = code.astype(jnp.bfloat16)
        return carry

    lax.fori_loop(0, own // own_tile, branch_rows, 0)
    swaps = team_copies(0, lambda p, o: s.gb.at[own_rows], lambda p, o: s.gb.at[own_rows])
    swaps += team_copies(1, lambda p, o: s.gco.at[own_rows], lambda p, o: s.gco.at[own_rows])
    for copy in swaps:
        copy.start()
    upper, lower = split_pair(s.gx[...])
    loads["rep"].wait()
    s.rep_a[:, pl.ds(3 * width, width)] = (
        dot(s.code_out[...], upper) + dot(s.code_out[...], lower)
    ).astype(jnp.bfloat16)
    cut_a = shared_slice(early)
    reps = team_copies(2, lambda p, o: s.rep_a.at[:, cut_a(p, o)], lambda p, o: s.got_a.at[o - 1])
    for copy in reps:
        copy.start()
    for copy in swaps:
        copy.wait_recv()

    def turn(i, carry):
        rows = pl.ds(pl.multiple_of(i * tile, tile), tile)
        value = jnp.transpose(s.gco[rows, :].astype(jnp.float32))[:16]
        s.gcot[:, rows] = value.astype(jnp.bfloat16)
        return carry

    lax.fori_loop(0, tiles, turn, 0)
    loads["co"].wait()
    loads["split"].wait()
    s.flat_a[:, pl.ds(early.split - channels, channels)] = dot(s.gcot[...], s.co[...]).astype(
        jnp.bfloat16
    )
    for copy in reps:
        copy.wait_recv()
    sum_shared(early, s.rep_a, s.got_a, s.flat_a)
    sent_a = hand_out(early, s.flat_a, s.part_a, s.from_a, 0)
    pieces_a = pieces_of(early, s.sum_a, s.early, 0)
    pieces_b = pieces_of(late, s.sum_b, s.late, 2)
    place_a = pltpu.make_async_copy(s.sum_a, s.early.at[spot], s.local.at[1])
    place_b = pltpu.make_async_copy(s.sum_b, s.late.at[spot], s.local.at[2])

    for name in ("w", "b", "c", "x"):
        loads[name].wait()

    def weights(first, amount):
        return s.w[:, :, :, :, pl.ds(first, amount)].reshape(width, amount)

    def back(j, carry):
        i = tiles - 1 - j
        start = pl.multiple_of(i * tile, tile)
        rows = pl.ds(start, tile)
        later = pl.ds(pl.multiple_of(start + 8, 8), tile)
        grad = dot(s.gb[rows, :], weights(3 * channels, channels)) + dot_against(
            s.gco[rows, :], s.out_reduce[...]
        )
        s.halo[pl.ds(0, 8), :] = s.st[0, pl.ds(start, 8), :] * s.st[2, pl.ds(start, 8), :]
        product = s.st[0, later, :] * s.st[2, later, :]
        s.halo[pl.ds(8, tile), :] = product
        masks = s.same[rows, :]
        mixed = (
            s.taps[0:1, :] * product
            + s.taps[1:2, :] * s.halo[pl.ds(7, tile), :] * masks[:, 0:1]
            + s.taps[2:3, :] * s.halo[pl.ds(6, tile), :] * masks[:, 1:2]
        )
        grad_mixed = grad * s.st[1, later, :]
        s.ha[pl.ds(0, tile), :] = s.taps[1:2, :] * grad_mixed * masks[:, 0:1]
        s.hb[pl.ds(0, tile), :] = s.taps[2:3, :] * grad_mixed * masks[:, 1:2]
        grad_product = (
            s.taps[0:1, :] * grad_mixed + s.ha[pl.ds(1, tile), :] + s.hb[pl.ds(2, tile), :]
        )
        s.ha[pl.ds(tile, 8), :] = s.ha[pl.ds(0, 8), :]
        s.hb[pl.ds(tile, 8), :] = s.hb[pl.ds(0, 8), :]
        s.gs[rows, pl.ds(0, channels)] = (grad_product * s.st[2, later, :]).astype(jnp.bfloat16)
        s.gs[rows, pl.ds(channels, channels)] = (grad * mixed).astype(jnp.bfloat16)
        s.gs[rows, pl.ds(2 * channels, channels)] = (grad_product * s.st[0, later, :]).astype(
            jnp.bfloat16
        )
        lanes = s.gs[rows, :]
        code = dot_against(lanes, s.in_lift[...])
        s.gcit[:, rows] = jnp.transpose(code)[:16]
        upper, lower = split_pair(code)
        s.pb[rows, :] = (
            dot_against(lanes, weights(0, 3 * channels))
            + dot_against(upper, s.in_reduce[...])
            + dot_against(lower, s.in_reduce[...])
        ).astype(jnp.bfloat16)

        @pl.when(j == tiles - 2)
        def _():
            for copy in sent_a:
                copy.wait_recv()
            take_in(early, s.from_a, s.sum_a)
            place_a.start()
            gather.start(pieces_a, 0)

        return carry

    lax.fori_loop(0, tiles, back, 0)
    grads = team_copies(
        3,
        lambda p, o: s.pb.at[pl.ds(pl.multiple_of(p * own, own), own)],
        lambda p, o: s.rb.at[o - 1],
    )
    for copy in grads:
        copy.start()
    loads["na"].wait()
    upper, lower = split_pair(s.gcit[...])
    s.rep_b[...] = (dot(upper, s.na[...]) + dot(lower, s.na[...])).astype(jnp.bfloat16)
    cut_b = shared_slice(late)
    more = team_copies(4, lambda p, o: s.rep_b.at[:, cut_b(p, o)], lambda p, o: s.got_b.at[o - 1])
    for copy in more:
        copy.start()
    s.flat_b[:, pl.ds(0, 3 * channels)] = dot(s.code_in[...], s.gs[...]).astype(jnp.bfloat16)
    for copy in more:
        copy.wait_recv()
    sum_shared(late, s.rep_b, s.got_b, s.flat_b)
    sent_b = hand_out(late, s.flat_b, s.part_b, s.from_b, 1)
    place_a.wait()
    gather.arrive(pieces_a, 0)
    gather.start(pieces_a, 1)
    loads["xo"].wait()
    for copy in grads:
        copy.wait_recv()

    def residual_rows(i, carry):
        local_rows = pl.ds(pl.multiple_of(i * own_tile, own_tile), own_tile)
        rows = pl.ds(pl.multiple_of(member * own + i * own_tile, own_tile), own_tile)
        values = s.xo[local_rows, :].astype(jnp.float32)
        grad = s.pb[rows, :].astype(jnp.float32)
        for peer in range(team - 1):
            grad = grad + s.rb[peer, local_rows, :].astype(jnp.float32)
        s.out[local_rows, :] = (
            s.gx[local_rows, :]
            + normalize_back(values, norm_factor(values), s.conv_gain[...], grad)
        ).astype(jnp.bfloat16)
        return carry

    lax.fori_loop(0, own // own_tile, residual_rows, 0)
    result = pltpu.make_async_copy(s.out, s.grad_residual, s.local.at[0])
    result.start()
    for copy in sent_b:
        copy.wait_recv()
    take_in(late, s.from_b, s.sum_b)
    place_b.start()
    gather.start(pieces_b, 0)
    gather.arrive(pieces_a, 1)
    gather.start(pieces_a, 2)
    place_b.wait()
    gather.arrive(pieces_b, 0)
    gather.start(pieces_b, 1)

    def pass_on(share, whole, reps, spare, base):
        for block in range(share.blocks):
            here = whole.at[position(share.first + block, dims)]
            load = pltpu.make_async_copy(here, spare.at[block], s.local.at[3 + block])
            load.start()
            load.wait()
        out = team_copies(base, lambda p, o: spare, lambda p, o: reps.at[member])
        for copy in out:
            copy.start()
        keep = pltpu.make_async_copy(spare, reps.at[member], s.local.at[3])
        keep.start()
        return out, keep

    gather.arrive(pieces_a, 2)
    out_a, keep_a = pass_on(early, s.early, s.early_rep, s.spare_a, 5)
    gather.arrive(pieces_b, 1)
    gather.start(pieces_b, 2)
    keep_a.wait()
    gather.arrive(pieces_b, 2)
    out_b, keep_b = pass_on(late, s.late, s.late_rep, s.spare_b, 6)
    for copy in out_a + out_b:
        copy.wait_recv()
    for copy in out_a + out_b + swaps + reps + grads + more + sent_a + sent_b:
        copy.wait_send()
    gather.drain(pieces_a)
    gather.drain(pieces_b)
    keep_b.wait()
    result.wait()


def backward(dims, team, early, late, operands):
    grad_x_two, ffn_split, ffn_rep, io_whole, streams, norm_one, conv_out, x_own = operands[:8]
    count = dims[0] * dims[1] * dims[2]
    own, width = x_own.shape
    length, channels = conv_out.shape
    lanes = sum(d - 1 for d in dims)
    bf16, f32 = jnp.bfloat16, jnp.float32
    anywhere = pl.BlockSpec(memory_space=pl.ANY)
    vmem = pl.BlockSpec(memory_space=pltpu.VMEM)
    rows = ADAPTER_COUNT * 16
    peers = max(team - 1, 1)
    outs = [
        ((own, width), bf16),
        (dims + (rows, early.block), bf16),
        (dims + (rows, late.block), bf16),
        ((team, early.blocks, rows, early.block), bf16),
        ((team, late.blocks, rows, late.block), bf16),
    ]
    scratch = [
        pltpu.VMEM(io_whole.shape, bf16),
        pltpu.VMEM((own, width), f32),
        pltpu.VMEM((length, width), bf16),
        pltpu.VMEM((length, LANES), bf16),
        pltpu.VMEM((16, length), bf16),
        pltpu.VMEM((3, length + 8, channels), f32),
        pltpu.VMEM((length, 3 * channels), bf16),
        pltpu.VMEM((ROW_TILE + 8, channels), f32),
        pltpu.VMEM((ROW_TILE + 8, channels), f32),
        pltpu.VMEM((ROW_TILE + 8, channels), f32),
        pltpu.VMEM((length, width), bf16),
        pltpu.VMEM((length, channels), bf16),
        pltpu.VMEM((length, width), bf16),
        pltpu.VMEM((16, length), f32),
        pltpu.VMEM((own, width), bf16),
        pltpu.VMEM((peers, own, width), bf16),
        pltpu.VMEM((16, early.shared), bf16),
        pltpu.VMEM((16, late.shared), bf16),
        pltpu.VMEM((peers, 16, early.share), bf16),
        pltpu.VMEM((peers, 16, late.share), bf16),
        pltpu.VMEM((16, count * early.block), bf16),
        pltpu.VMEM((16, count * late.block), bf16),
        pltpu.VMEM((count, 16, early.block + LANES), bf16),
        pltpu.VMEM((count, 16, late.block + LANES), bf16),
        pltpu.VMEM((count, 16, early.block + LANES), bf16),
        pltpu.VMEM((count, 16, late.block + LANES), bf16),
        pltpu.VMEM((rows, early.block), bf16),
        pltpu.VMEM((rows, late.block), bf16),
        pltpu.VMEM((early.blocks, rows, early.block), bf16),
        pltpu.VMEM((late.blocks, rows, late.block), bf16),
        pltpu.VMEM((own, width), bf16),
        pltpu.SemaphoreType.DMA((4, lanes)),
        pltpu.SemaphoreType.DMA((4, lanes)),
        pltpu.SemaphoreType.DMA((2, count - 1)),
        pltpu.SemaphoreType.DMA((2, count - 1)),
        pltpu.SemaphoreType.DMA((7, peers)),
        pltpu.SemaphoreType.DMA((7, peers)),
        pltpu.SemaphoreType.DMA((max(10, 3 + max(early.blocks, late.blocks)),)),
    ]
    return pl.pallas_call(
        functools.partial(backward_kernel, (dims, team, width, channels, length, early, late)),
        out_shape=[jax.ShapeDtypeStruct(*o) for o in outs],
        in_specs=[anywhere] * 8 + [vmem] * (len(operands) - 8),
        out_specs=[anywhere] * 5,
        scratch_shapes=scratch,
        compiler_params=pltpu.CompilerParams(
            collective_id=1, has_side_effects=True, vmem_limit_bytes=67043328
        ),
    )(*operands)


def lagged_segments(segment_ids, lag):
    shifted = jnp.pad(segment_ids, ((0, 0), (lag, 0)), constant_values=-1)[
        :, : segment_ids.shape[1]
    ]
    return (segment_ids == shifted).astype(jnp.float32)


def pad_axis(values, axis, size):
    widths = [(0, 0)] * values.ndim
    widths[axis] = (0, size - values.shape[axis])
    return jnp.pad(values, widths)


def per_device(
    residual,
    cotangent,
    segment_ids,
    adapter_ids,
    conv_gain,
    proj_in,
    conv_taps,
    proj_out,
    ffn_gain,
    gate_up,
    proj_down,
    in_shrink,
    input_lift_weight,
    output_reduce_weight,
    output_lift_weight,
    ffn_reduce_weight,
    ffn_expand,
    down_shrink,
    down_lift_weight,
):
    own, width = residual.shape
    length = segment_ids.shape[1]
    team = length // own
    count = lax.axis_size("dp")
    dims = split_ring(count)
    rows, _, channels = proj_in.shape
    hidden = proj_down.shape[1]
    hc = HIDDEN_CHUNK
    chunks = -(-hidden // hc)
    padded = chunks * hc
    adapter = adapter_ids[0]
    onehot = (adapter == jnp.arange(ADAPTER_COUNT, dtype=jnp.int32)).astype(jnp.float32)

    io_shard = jnp.concatenate([proj_in.reshape(rows, 3 * channels), proj_out], axis=1)
    ff_shard = jnp.concatenate([gate_up, proj_down[:, None, :]], axis=1)
    ff_shard = pad_axis(ff_shard, 2, padded).reshape(rows, 3, chunks, hc)
    ff_shard = jnp.transpose(ff_shard, (2, 0, 1, 3)).reshape(chunks, rows, 3 * hc)

    def pick(values, axis):
        return lax.dynamic_index_in_dim(values, adapter, axis, keepdims=False)

    in_reduce = pad_axis(pick(in_shrink, 1), 1, LANES)
    in_lift = pad_axis(pick(input_lift_weight, 0).reshape(ADAPTER_RANK, 3 * channels), 0, LANES)
    out_reduce = pad_axis(pick(output_reduce_weight, 1), 1, LANES)
    out_lift = pad_axis(pick(output_lift_weight, 0), 0, LANES)
    ffn_reduce = pad_axis(pick(ffn_reduce_weight, 2).reshape(width, 2 * ADAPTER_RANK), 1, LANES)
    expand = pad_axis(pick(ffn_expand, 1), 2, padded).reshape(2, ADAPTER_RANK, chunks, hc)
    expand = jnp.transpose(expand, (2, 0, 1, 3))
    blank = jnp.zeros((chunks, ADAPTER_RANK, hc), expand.dtype)
    expand = jnp.concatenate(
        [
            jnp.concatenate([expand[:, 0], blank], axis=2),
            jnp.concatenate([blank, expand[:, 1]], axis=2),
        ],
        axis=1,
    )
    expand = pad_axis(expand, 1, LANES)
    shrink = pad_axis(pad_axis(pick(down_shrink, 1), 1, LANES), 0, padded)
    shrink = shrink.reshape(chunks, hc, LANES)
    down_lift = pad_axis(pick(down_lift_weight, 0), 0, LANES)
    first_same, second_same = lagged_segments(segment_ids, 1)[0], lagged_segments(segment_ids, 2)[0]
    same = jnp.stack([first_same, second_same], axis=1)
    taps = conv_taps.astype(jnp.float32)
    (
        io_whole,
        _,
        streams,
        norm_one,
        conv_out,
        code_in,
        code_out,
        block_output,
        grad_x_two,
        ffn_split,
        ffn_rep,
    ) = forward_and_ffn(
        dims,
        team,
        (
            io_shard,
            ff_shard,
            residual,
            cotangent,
            expand,
            shrink,
            same,
            conv_gain.reshape(1, width),
            ffn_gain.reshape(1, width),
            taps,
            in_reduce,
            in_lift,
            out_reduce,
            out_lift,
            ffn_reduce,
            down_lift,
        ),
    )
    early = Share(count, team, 3 * padded + channels, 4 * width)
    late = Share(count, team, 3 * channels, width)
    marks = jnp.broadcast_to(pad_axis(onehot, 0, 16)[:, None], (16, LANES)).astype(jnp.bfloat16)
    grad_residual, early_sums, late_sums, early_shared, late_shared = backward(
        dims,
        team,
        early,
        late,
        (
            grad_x_two,
            ffn_split,
            ffn_rep,
            io_whole,
            streams,
            norm_one,
            conv_out,
            residual,
            code_in,
            code_out,
            same,
            conv_gain.reshape(1, width),
            taps,
            in_reduce,
            in_lift,
            out_reduce,
            out_lift,
            marks,
        ),
    )

    def columns_of(sums, share):
        sums = sums.reshape(count, ADAPTER_COUNT, ADAPTER_RANK, share.block)
        return jnp.transpose(sums, (1, 2, 0, 3)).reshape(
            ADAPTER_COUNT, ADAPTER_RANK, count * share.block
        )

    def shared_columns(sums, share):
        sums = sums.reshape(team, share.blocks, ADAPTER_COUNT, ADAPTER_RANK, share.block)
        sums = jnp.transpose(sums, (2, 3, 0, 1, 4)).reshape(
            ADAPTER_COUNT, ADAPTER_RANK, team, share.blocks * share.block
        )
        skip = share.split - share.first * share.block
        return sums[..., skip : skip + share.share].reshape(
            ADAPTER_COUNT, ADAPTER_RANK, share.shared
        )

    def rows_first(values):
        return jnp.transpose(values, (2, 0, 1)).astype(jnp.float32)

    early_columns, late_columns = columns_of(early_sums, early), columns_of(late_sums, late)
    early_rest, late_rest = shared_columns(early_shared, early), shared_columns(late_shared, late)
    ffn_e = jnp.stack([early_columns[..., :hidden], early_columns[..., padded : padded + hidden]])
    ffn_e = ffn_e.astype(jnp.float32)
    down_s = rows_first(early_columns[..., 2 * padded : 2 * padded + hidden])
    out_s = rows_first(early_columns[..., 3 * padded : 3 * padded + channels])
    ffn_s = jnp.stack(
        [rows_first(early_rest[..., :width]), rows_first(early_rest[..., width : 2 * width])],
        axis=1,
    )
    down_e = early_rest[..., 2 * width : 3 * width].astype(jnp.float32)
    out_e = early_rest[..., 3 * width :].astype(jnp.float32)
    in_e = late_columns[..., : 3 * channels].astype(jnp.float32)
    in_e = in_e.reshape(ADAPTER_COUNT, ADAPTER_RANK, 3, channels)
    in_s = rows_first(late_rest)
    return (block_output, grad_residual, in_s, in_e, out_s, out_e, ffn_s, ffn_e, down_s, down_e)


def solution(mesh):
    rows = P(("dp", "tensor"), None)
    placed = (
        rows,
        rows,
        P("dp", None),
        P("dp"),
        P(),
        P("dp", None, "tensor"),
        P(None, "tensor"),
        P("dp", "tensor"),
        P(),
        P("dp", None, "tensor"),
        P("dp", "tensor"),
        P(),
        P(None, None, None, "tensor"),
        P("tensor", None, None),
        P(),
        P(),
        P(None, None, None, "tensor"),
        P("tensor", None, None),
        P(),
    )
    return jax.shard_map(
        per_device,
        mesh=mesh,
        in_specs=placed,
        out_specs=(
            rows,
            rows,
            P(),
            P(None, None, None, "tensor"),
            P("tensor", None, None),
            P(),
            P(),
            P(None, None, None, "tensor"),
            P("tensor", None, None),
            P(),
        ),
        check_vma=False,
    )
```

time: 1200 us -> 603 us (0.50)
  waiting for transfers between devices: 782 us -> 0 us
  Pallas kernels: 0 us -> 542 us
  matrix products: 251 us -> 0 us
  local copies, waits for them, and re-layouts: 93.8 us -> 44.7 us
  other arithmetic: 41.4 us -> 12.7 us
  between operations: 15.7 us -> 1.58 us
    pallas_call x0 -> x2, Pallas kernels: none -> 542 us  [the longest x1 413 us: forward_and_ffn(): pl.pallas_call(functools.partial(forward_kernel, shape), out_shape=[jax.S...]
    all_gather x8 -> x0, waiting for transfers between devices: 478 us -> none  [the longest x1 224 us: per_device(): lax.all_gather(gate_up, 'dp', axis=0, tiled=True)]
    psum x2 -> x0, waiting for transfers between devices: 265 us -> none  [the longest x1 145 us: per_device(): lax.psum((grad_in_shrink, grad_ffn_shrink, grad_out_expand, grad_down_exp...]
    dot_general x41 -> x0, matrix products: 251 us -> none  [the longest x13 121 us: contract_simple(): return jnp.dot(left, right, preferred_element_type=jnp.float32)]
    unnamed x189 -> x33, local copies, waits for them, and re-layouts: 54.2 us -> 9.88 us
    reduce_scatter x6 -> x0, waiting for transfers between devices: 35.4 us -> none  [the longest x1 16.3 us: per_device(): lax.psum_scatter(branch_part, 'tensor', scatter_dimension=0, tiled=True)]
    reshape x1 -> x14, local copies, waits for them, and re-layouts: 1.02 us -> 13 us  [the longest x1 3.34 us: per_device(): jnp.transpose(ff_shard, (2, 0, 1, 3)).reshape(chunks, rows, 3 * hc)]
  transfers between devices with their start and end apart: 16 -> 0, of which waited for: 12 -> 0; matrix products, arithmetic and copies ran while one was open for 18% -> 0% of each run, Pallas kernels for 0% -> 0%
where the time goes in v2:
time: 603 us; the launch traced here: 601 us
  Pallas kernels  542 us (90%)
  local copies, waits for them, and re-layouts  44.7 us (7%)
  other arithmetic  12.7 us (2%)
    pallas_call x1, Pallas kernels, forward_and_ffn(): pl.pallas_call(functools.partial(forward_kernel, shape), out_shape=[jax.S...  413 us
    pallas_call x1, Pallas kernels, backward(): pl.pallas_call(functools.partial(backward_kernel, (dims, team, width, cha...  129 us

profile of v2, /device:TPU:0, one launch (start us, length us, event | category | flops | bytes accessed | tf_op | source)
XLA Modules:
  0.0 601.1 jit_solution(2628148593822457883)
XLA Ops:
  1.3 1.0 constant_dynamic-slice_fusion.4
  2.3 0.1 reshape.87
  2.5 1.4 pad.48.refs_4_
  3.9 0.8 dynamic-slice_bitcast_fusion.1
  4.7 0.8 pad.55.refs_13_.refs_16_
  5.5 0.8 constant_dynamic-slice_fusion.3
  6.3 0.2 copy.82
  6.5 0.8 pad.52.refs_10_.refs_13_
  7.3 0.9 constant_dynamic-slice_fusion.2
  8.2 0.1 copy.83
  8.3 0.9 pad.53.refs_11_.refs_14_
  9.2 0.8 pad.57.refs_15_
  9.9 0.7 constant_dynamic-slice_fusion.1
  10.7 0.2 copy.84
  10.8 0.7 pad.54.refs_12_.refs_15_
  11.6 0.9 dynamic-slice_bitcast_fusion
  12.5 0.5 copy.94
  12.9 0.0 copy-start.12
  13.0 0.0 copy-start.11
  13.0 0.0 copy-start.9
  13.0 0.0 copy-start.4
  13.0 1.1 pad.49.clone
  14.1 0.9 constant_dynamic-slice_fusion
  15.0 0.2 copy.86
  15.2 0.8 pad.56.refs_14_
  16.0 0.1 compare_bitcast_fusion.1
  16.2 0.3 copy.81
  16.4 0.8 stack.29.refs_6_.refs_10_
  17.3 0.6 convert_element_type.71.refs_9_.refs_12_
  17.9 0.6 reshape.89.refs_7_.refs_11_
  18.5 1.9 copy.76
  20.4 1.5 copy.77
  21.9 2.1 maximum_bitcast_fusion
  24.0 5.4 copy.78
  29.4 0.0 copy-start.6
  29.4 0.0 copy-start.8
  29.4 3.3 reshape.86.refs_1_
  32.8 0.9 pad_maximum_fusion.refs_0_
  33.6 0.6 reshape.90.refs_8_
  34.2 413.2 %shard_map.258 = (bf16[4,2,2,96,3072]{4,3,2,1,0:T(8,128)(2,1)}, bf16[9,4,2,2,96,1152]{5,4,3,2,1,0:T(8,128)(2,1)}, f32[3,1024,768]{2,1,0:T(8,128)}, bf16[1024,153...) custom-call(bf16[96,3072]{1,0:T(8,128)(2,1)} %pad_maximum_fusion.ref, ...), custom_call_target="tpu_custom_call" | custom-call | tf_op jit(solution)/shard_map/pallas_call | solution.py:650
  447.5 0.7 broadcast_in_dim.2.refs_17_
  448.1 128.9 %shard_map.259 = (bf16[512,1536]{1,0:T(8,128)(2,1)}, bf16[4,2,2,128,896]{4,3,2,1,0:T(8,128)(2,1)}, bf16[4,2,2,128,256]{4,3,2,1,0:T(8,128)(2,1)}, bf16[2,4,128,89...) custom-call(f32[512,1536]{1,0:T(8,128)} %get-tuple-element.26.refs_0_, bf16[16,10368]{1,0:T(8,128)(2,1)} %get-tuple-element.27.refs_1_, ...), custom_call_target="tpu_custom_call" | custom-call | tf_op jit(solution)/shard_map/pallas_call | solution.py:1109
  577.1 2.6 copy.97
  579.7 1.7 convert_bitcast_fusion
  581.4 0.6 copy-done
  582.0 2.0 maximum_convert_fusion
  584.1 0.2 copy-done.1
  584.3 1.4 copy.105
  585.7 1.7 reshape.100
  587.4 1.5 slice_bitcast_fusion
  589.0 0.1 copy.98
  589.1 1.4 slice_convert_fusion.1
  590.5 1.2 maximum_convert_fusion.1
  591.7 0.5 copy-done.5
  592.1 0.6 copy.107
  592.7 0.5 reshape.94
  593.3 0.1 slice_convert_fusion
  593.4 1.1 copy.106
  594.5 1.7 convert_bitcast_fusion.1
  596.2 0.3 copy.108
  596.6 1.4 reshape.104
  598.0 1.1 copy.113
  599.1 0.8 copy-done.3
  600.0 1.1 copy.114
  (24 shorter events, 0.2 us)
Async XLA Ops:
  12.9 3.1 copy-start.12
  13.0 4.3 copy-start.11
  13.0 4.9 copy-start.9
  13.0 5.5 copy-start.4
  29.4 3.4 copy-start.6
  29.4 3.4 copy-start.8
  32.7 0.9 copy-start.10
  579.7 2.4 copy-start
  582.0 2.3 copy-start.1
  590.5 1.7 copy-start.5
  593.4 2.9 copy-start.7
  596.2 1.8 copy-start.2
  598.0 2.0 copy-start.3

commit v3 on v2

v3 whole, which is shorter than its diff:
```python
import functools
import types

import jax
import jax.numpy as jnp
from jax import lax
from jax.experimental import pallas as pl
from jax.experimental.pallas import tpu as pltpu
from jax.sharding import PartitionSpec as P

ADAPTER_COUNT = 8
ADAPTER_RANK = 16
EPSILON = 1e-05
MESH = pl.DeviceIdType.MESH
LANES = 128
HIDDEN_CHUNK = 384
ROW_TILE = 256


def dot(left, right):
    return jnp.dot(left, right, preferred_element_type=jnp.float32)


def dot_against(left, right):
    return lax.dot_general(
        left, right, (((1,), (1,)), ((), ())), preferred_element_type=jnp.float32
    )


def split_pair(values):
    upper = values.astype(jnp.bfloat16)
    lower = (values - upper.astype(jnp.float32)).astype(jnp.bfloat16)
    return (upper, lower)


def norm_factor(values):
    return lax.rsqrt(jnp.mean(values * values, axis=-1, keepdims=True) + EPSILON)


def normalize_back(values, factor, gain, grad):
    unit = values * factor
    scaled = grad * gain
    return factor * (scaled - unit * jnp.mean(scaled * unit, axis=-1, keepdims=True))


def split_ring(count):
    if count % 16 == 0:
        return (4, count // 8, 2)
    return (count, 1, 1)


def position(index, dims):
    return (index // (dims[1] * dims[2]), (index // dims[2]) % dims[1], index % dims[2])


def flat(spot, dims):
    return (spot[0] * dims[1] + spot[1]) * dims[2] + spot[2]


class Gather:
    def __init__(self, dims, spot, send, recv):
        self.dims, self.spot, self.send, self.recv = dims, spot, send, recv

    def place(self, piece, step, along=None):
        whole, columns, order = piece[:3]
        spot = list(self.spot)
        if along is not None:
            spot[order[step]] = along
        place = tuple(
            slice(None) if other in order[:step] else spot[other] for other in range(3)
        )
        return whole.at[place + (slice(None), columns)]

    def lined(self, piece, step):
        return piece[4] and piece[2][step] == 0 and self.dims[0] == 4

    def copies(self, piece, step, offsets=None):
        _, _, order, row, _ = piece
        axis = order[step]
        target = self.place(piece, step)
        base = sum(self.dims[other] - 1 for other in order[:step])
        out = []
        for offset in offsets or range(1, self.dims[axis]):
            peer = list(self.spot)
            peer[axis] = lax.rem(self.spot[axis] + offset, self.dims[axis])
            out.append(
                pltpu.make_async_remote_copy(
                    src_ref=target,
                    dst_ref=target,
                    send_sem=self.send.at[row, base + offset - 1],
                    recv_sem=self.recv.at[row, base + offset - 1],
                    device_id={"dp": flat(peer, self.dims)},
                    device_id_type=MESH,
                )
            )
        return out

    def passed(self, piece, step, here):
        _, _, order, row, _ = piece
        block = self.place(piece, step, 3 if here == 1 else 0)
        base = sum(self.dims[other] - 1 for other in order[:step])
        lanes = sum(d - 1 for d in self.dims)
        peer = list(self.spot)
        peer[0] = 0 if here == 1 else 3
        return pltpu.make_async_remote_copy(
            src_ref=block,
            dst_ref=block,
            send_sem=self.send.at[row, lanes],
            recv_sem=self.recv.at[row, base + (0 if here == 1 else 2)],
            device_id={"dp": flat(peer, self.dims)},
            device_id_type=MESH,
        )

    def own(self, piece, step, act):
        copies = self.copies(piece, step)
        if not self.lined(piece, step):
            for copy in copies:
                act(copy)
            return
        act(copies[1])
        pl.when(self.spot[0] != 3)(lambda: act(copies[0]))
        pl.when(self.spot[0] != 0)(lambda: act(copies[2]))

    def start(self, pieces, step):
        for piece in pieces:
            self.own(piece, step, lambda copy: copy.start())

    def relay(self, pieces, step):
        for piece in pieces:
            if self.lined(piece, step):
                self.copies(piece, step, (2,))[0].wait_recv()
                for here in (1, 2):
                    copy = self.passed(piece, step, here)
                    pl.when(self.spot[0] == here)(copy.start)

    def arrive(self, pieces, step):
        for piece in pieces:
            for copy in self.copies(piece, step, (1, 3) if self.lined(piece, step) else None):
                copy.wait_recv()

    def drain(self, pieces):
        for piece in pieces:
            for step in range(3):
                self.own(piece, step, lambda copy: copy.wait_send())
                if self.lined(piece, step):
                    for here in (1, 2):
                        copy = self.passed(piece, step, here)
                        pl.when(self.spot[0] == here)(copy.wait_send)


def greet(dims, spot, team, member):
    barrier = pltpu.get_barrier_semaphore()
    count = 0
    for axis in range(3):
        for offset in range(1, dims[axis]):
            peer = list(spot)
            peer[axis] = lax.rem(spot[axis] + offset, dims[axis])
            pl.semaphore_signal(
                barrier, inc=1, device_id={"dp": flat(peer, dims)}, device_id_type=MESH
            )
            count += 1
    for offset in range(1, team):
        pl.semaphore_signal(
            barrier,
            inc=1,
            device_id={"tensor": lax.rem(member + offset, team)},
            device_id_type=MESH,
        )
        count += 1
    pl.semaphore_wait(barrier, count)


NAMES = (
    "in_shard",
    "out_shard",
    "gu_shard",
    "down_shard",
    "x_own",
    "g_own",
    "expand",
    "down_shrink",
    "same",
    "conv_gain",
    "ffn_gain",
    "taps",
    "in_reduce",
    "in_lift",
    "out_reduce",
    "out_lift",
    "ffn_reduce",
    "down_lift",
    "mask",
    "pick",
    "io_whole",
    "ff_whole",
    "streams",
    "norm_one",
    "conv_out",
    "code_in",
    "code_out",
    "block_out",
    "grad_x_two",
    "ffn_flat",
    "x_all",
    "g_all",
    "na",
    "nb",
    "w",
    "acc_a",
    "acc_b",
    "x_two",
    "halo",
    "co",
    "cp",
    "gcf",
    "cf",
    "gd",
    "cft",
    "gdt",
    "act",
    "ggu",
    "eb",
    "dsb",
    "rb",
    "rc",
    "rd",
    "code_t",
    "flat",
    "rep",
    "got",
    "send",
    "recv",
    "team_send",
    "team_recv",
    "local",
    "load_sem",
)


class Plan:
    def __init__(self, chunks):
        self.crossed = [4, chunks - 2] if chunks >= 8 else [max(chunks - 2, 0)]
        self.plain = [k for k in range(chunks) if k not in self.crossed]
        self.top = [[] for _ in range(chunks)]
        self.bottom = [[] for _ in range(chunks)]
        for m, k in enumerate(self.plain):
            self.add(self.top, k, "second", m + 3)
            self.add(self.top, k, "relay", m + 4)
            self.add(self.top, k, "first", m + 6)
            self.add(self.bottom, k, "third", m + 2)
        for m, k in enumerate(self.crossed):
            self.top[1 + m].append(("cross_third", k))
            self.top[k - 1 - m].append(("cross_relay", k))

    def add(self, where, at, step, m):
        if m < len(self.plain):
            where[at].append((step, self.plain[m]))


def forward_kernel(shape, *refs):
    s = types.SimpleNamespace(**dict(zip(NAMES, refs)))
    dims, team, width, channels, length, chunks, early = shape
    own = length // team
    hc = HIDDEN_CHUNK
    tile = ROW_TILE
    tiles = length // tile
    own_tile = min(own, tile)
    member = lax.axis_index("tensor")
    spot = position(lax.axis_index("dp"), dims)
    gather = Gather(dims, spot, s.send, s.recv)
    own_rows = pl.ds(pl.multiple_of(member * own, own), own)
    plan = Plan(chunks)

    io_step = 4 * channels // 6
    half = io_step // 2
    io_pieces = [
        [
            (s.io_whole, pl.ds(i * io_step, half), (0, 1, 2), 2 * i, False),
            (s.io_whole, pl.ds(i * io_step + half, half), (0, 2, 1), 2 * i + 1, False),
        ]
        for i in range(6)
    ]
    cut = 640

    def chunk_pieces(k):
        orders = ((1, 2, 0), (2, 1, 0)) if k in plan.crossed else ((0, 1, 2), (0, 2, 1))
        whole = s.ff_whole.at[k]
        return [
            (whole, pl.ds(0, cut), orders[0], 12 + 2 * k, True),
            (whole, pl.ds(cut, 3 * hc - cut), orders[1], 13 + 2 * k, True),
        ]

    def do(step, k):
        pieces = chunk_pieces(k)
        if step == "first" or step == "cross_first":
            gather.start(pieces, 0)
        elif step == "relay":
            gather.relay(pieces, 0)
        elif step == "second" or step == "cross_second":
            gather.arrive(pieces, 0)
            gather.start(pieces, 1)
        elif step == "third" or step == "cross_third":
            gather.arrive(pieces, 1)
            gather.start(pieces, 2)
        elif step == "cross_relay":
            gather.relay(pieces, 2)
        elif step == "last":
            gather.arrive(pieces, 2)

    def do_plain(step, m):
        if m < len(plan.plain):
            do(step, plan.plain[m])

    def team_copies(row, source, target):
        out = []
        for offset in range(1, team):
            peer = lax.rem(member + offset, team)
            out.append(
                pltpu.make_async_remote_copy(
                    src_ref=source(peer, offset),
                    dst_ref=target(peer, offset),
                    send_sem=s.team_send.at[row, offset - 1],
                    recv_sem=s.team_recv.at[row, offset - 1],
                    device_id={"tensor": peer},
                    device_id_type=MESH,
                )
            )
        return out

    def rows_of(ref):
        return lambda peer, offset: ref.at[pl.ds(pl.multiple_of(peer * own, own), own)]

    def slot_of(ref):
        return lambda peer, offset: ref.at[offset - 1]

    def spare(k):
        at = position(1 + k // 2, dims)
        return lambda first, amount: s.w.at[at + (slice(None), pl.ds((k % 2) * 3 * hc + first, amount))]

    io_spare = s.w.at[0, 0, 0, :, pl.ds(0, 4 * channels)]
    ins = [
        [
            pltpu.make_async_copy(
                s.in_shard, s.w.at[0, 0, 0, :, pl.ds(0, 3 * channels)], s.local.at[2]
            ),
            pltpu.make_async_copy(
                s.out_shard, s.w.at[0, 0, 0, :, pl.ds(3 * channels, channels)], s.local.at[3]
            ),
        ]
    ]
    outs = [pltpu.make_async_copy(io_spare, s.io_whole.at[spot], s.local.at[2])]
    for k in range(chunks):
        part = pl.ds(k * hc, hc)
        sources = (s.gu_shard.at[0, :, part], s.gu_shard.at[1, :, part], s.down_shard.at[:, part])
        ins.append(
            [
                pltpu.make_async_copy(source, spare(k)(n * hc, hc), s.local.at[4 + 3 * k + n])
                for n, source in enumerate(sources)
            ]
        )
        outs.append(
            pltpu.make_async_copy(
                spare(k)(0, 3 * hc), s.ff_whole.at[(k,) + spot], s.local.at[4 + 3 * k]
            )
        )
    for copies in ins:
        for copy in copies:
            copy.start()
    greet(dims, spot, team, member)
    x_copies = team_copies(0, lambda p, o: s.x_own, lambda p, o: s.x_all.at[own_rows])
    g_copies = team_copies(1, lambda p, o: s.g_own, lambda p, o: s.g_all.at[own_rows])
    for copy in x_copies + g_copies:
        copy.start()
    x_here = pltpu.make_async_copy(s.x_own, s.x_all.at[own_rows], s.local.at[0])
    g_here = pltpu.make_async_copy(s.g_own, s.g_all.at[own_rows], s.local.at[1])
    for first, second in zip(ins, outs):
        for copy in first:
            copy.wait()
        second.start()
    x_here.start()
    g_here.start()
    outs[0].wait()
    for pieces in io_pieces:
        gather.start(pieces, 0)
    for copy in outs[1:]:
        copy.wait()
    for k in plan.crossed:
        do("cross_first", k)
    do_plain("first", 0)
    do_plain("first", 1)

    x_here.wait()
    for copy in x_copies:
        copy.wait_recv()

    def first_norm(i, carry):
        rows = pl.ds(pl.multiple_of(i * tile, tile), tile)
        values = s.x_all[rows, :].astype(jnp.float32)
        s.na[rows, :] = (values * norm_factor(values) * s.conv_gain[...]).astype(jnp.bfloat16)
        return carry

    def down_codes(i, carry):
        rows = pl.ds(pl.multiple_of(i * tile, tile), tile)
        code = dot_against(s.g_all[rows, :], s.down_lift[...]) * s.mask[...]
        code = code.astype(jnp.bfloat16)
        s.gd[rows, :] = code
        s.gdt[:, rows] = dot_against(s.pick[...], code).astype(jnp.bfloat16)
        return carry

    norm_store = pltpu.make_async_copy(s.na, s.norm_one, s.local.at[0])
    for i in range(7):
        if i == 0:
            lax.fori_loop(0, tiles, first_norm, 0)
            norm_store.start()
        if i == 1:
            g_here.wait()
            for copy in g_copies:
                copy.wait_recv()
            lax.fori_loop(0, tiles, down_codes, 0)
        if i < 6:
            gather.arrive(io_pieces[i], 0)
            gather.start(io_pieces[i], 1)
        if i > 0:
            gather.arrive(io_pieces[i - 1], 1)
            gather.start(io_pieces[i - 1], 2)
    do_plain("relay", 0)
    for k in plan.crossed:
        do("cross_second", k)
    do_plain("relay", 1)
    do_plain("first", 2)
    do_plain("second", 0)
    io_loads = []
    for i in range(6):
        gather.arrive(io_pieces[i], 2)
        columns = pl.ds(i * io_step, io_step)
        load = pltpu.make_async_copy(
            s.io_whole.at[:, :, :, :, columns], s.w.at[:, :, :, :, columns], s.load_sem.at[i]
        )
        load.start()
        io_loads.append(load)
    do_plain("second", 1)
    do_plain("first", 3)
    norm_store.wait()
    for load in io_loads:
        load.wait()

    def weights(first, count):
        return s.w[:, :, :, :, pl.ds(first, count)].reshape(width, count)

    s.halo[pl.ds(0, 8), :] = jnp.zeros((8, channels), jnp.float32)

    def convolve(i, carry):
        rows = pl.ds(pl.multiple_of(i * tile, tile), tile)
        normed = s.na[rows, :]
        code = (dot(normed, s.in_reduce[...]) * s.mask[...]).astype(jnp.bfloat16)
        s.code_in[:, rows] = dot_against(s.pick[...], code).astype(jnp.bfloat16)
        lanes = []
        for lane in range(3):
            value = dot(normed, weights(lane * channels, channels)) + dot(
                code, s.in_lift[:, pl.ds(lane * channels, channels)]
            )
            lanes.append(value)
            if lane < 2:
                s.acc_a[rows, pl.ds(lane * channels, channels)] = value
            else:
                s.acc_b[rows, pl.ds(0, channels)] = value
        product = lanes[0] * lanes[2]
        s.halo[pl.ds(8, tile), :] = product
        masks = s.same[rows, :]
        taps = s.taps[...].astype(jnp.float32)
        mixed = (
            taps[0:1, :] * product
            + taps[1:2, :] * s.halo[pl.ds(7, tile), :] * masks[:, 0:1]
            + taps[2:3, :] * s.halo[pl.ds(6, tile), :] * masks[:, 1:2]
        )
        s.halo[pl.ds(0, 8), :] = s.halo[pl.ds(tile, 8), :]
        convolved = (lanes[1] * mixed).astype(jnp.bfloat16)
        s.co[rows, :] = convolved
        s.na[rows, :] = dot_against(convolved, weights(3 * channels, channels)).astype(jnp.bfloat16)
        s.cp[rows, :] = dot(convolved, s.out_reduce[...])

        @pl.when(i == 1)
        def _():
            do_plain("relay", 2)
            do_plain("third", 0)

        @pl.when(i == 2)
        def _():
            do_plain("first", 4)
            do_plain("second", 2)

        return carry

    lax.fori_loop(0, tiles, convolve, 0)
    stores = [
        pltpu.make_async_copy(s.acc_a.at[:, pl.ds(0, channels)], s.streams.at[0], s.local.at[3]),
        pltpu.make_async_copy(
            s.acc_a.at[:, pl.ds(channels, channels)], s.streams.at[1], s.local.at[4]
        ),
        pltpu.make_async_copy(s.acc_b.at[:, pl.ds(0, channels)], s.streams.at[2], s.local.at[5]),
        pltpu.make_async_copy(s.co, s.conv_out, s.local.at[6]),
    ]
    branch = team_copies(2, rows_of(s.na), slot_of(s.rb))
    codes = team_copies(3, rows_of(s.cp), slot_of(s.rc))
    for copy in codes + branch + stores:
        copy.start()
    do_plain("relay", 3)
    do_plain("first", 5)
    do_plain("third", 1)

    def load(c):
        slot = lax.rem(c, 2)
        columns = pl.ds(pl.multiple_of(slot * 3 * hc, LANES), 3 * hc)
        part = pl.ds(pl.multiple_of(c * hc, LANES), hc)
        return [
            pltpu.make_async_copy(
                s.ff_whole.at[c], s.w.at[:, :, :, :, columns], s.load_sem.at[3 * slot]
            ),
            pltpu.make_async_copy(
                s.expand.at[:, :, part], s.eb.at[slot], s.load_sem.at[3 * slot + 1]
            ),
            pltpu.make_async_copy(s.down_shrink.at[part], s.dsb.at[slot], s.load_sem.at[3 * slot + 2]),
        ]

    for copy in branch + codes:
        copy.wait_recv()
    code = s.cp[own_rows, :]
    for peer in range(team - 1):
        code = code + s.rc[peer]
    code = (code * s.mask[...]).astype(jnp.bfloat16)
    s.code_out[...] = dot_against(s.pick[...], code).astype(jnp.bfloat16)
    s.cf[pl.ds(0, own), pl.ds(0, LANES)] = code

    def second_norm(i, carry):
        local_rows = pl.ds(pl.multiple_of(i * own_tile, own_tile), own_tile)
        rows = pl.ds(pl.multiple_of(member * own + i * own_tile, own_tile), own_tile)
        values = s.x_all[rows, :].astype(jnp.float32) + s.na[rows, :].astype(jnp.float32)
        for peer in range(team - 1):
            values = values + s.rb[peer, local_rows, :].astype(jnp.float32)
        values = values + dot(s.cf[local_rows, pl.ds(0, LANES)], s.out_lift[...])
        s.x_two[local_rows, :] = values
        s.nb[rows, :] = (values * norm_factor(values) * s.ffn_gain[...]).astype(jnp.bfloat16)
        return carry

    lax.fori_loop(0, own // own_tile, second_norm, 0)
    norms = team_copies(4, lambda p, o: s.nb.at[own_rows], lambda p, o: s.nb.at[own_rows])
    for copy in norms:
        copy.start()
    do("last", 0)
    for copy in load(0):
        copy.start()
    for copy in stores:
        copy.wait()
    s.acc_a[...] = jnp.zeros_like(s.acc_a)
    s.acc_b[...] = jnp.zeros_like(s.acc_b)
    for copy in branch + codes:
        copy.wait_send()
    s.cp[...] = jnp.zeros_like(s.cp)
    s.gcf[...] = jnp.zeros_like(s.gcf)
    for copy in norms:
        copy.wait_recv()

    def ffn_codes(i, carry):
        rows = pl.ds(pl.multiple_of(i * tile, tile), tile)
        value = dot(s.nb[rows, :], s.ffn_reduce[...])
        for n in range(2):
            code = (value[:, n * LANES : (n + 1) * LANES] * s.mask[...]).astype(jnp.bfloat16)
            s.cf[rows, pl.ds(n * LANES, LANES)] = code
            s.cft[pl.ds(16 * n, 16), rows] = dot_against(s.pick[...], code).astype(jnp.bfloat16)
        return carry

    lax.fori_loop(0, tiles, ffn_codes, 0)

    def chunk(c, carry):
        for k in range(chunks):
            if plan.top[k]:

                @pl.when(c == k)
                def _():
                    for step, which in plan.top[k]:
                        do(step, which)

        for copy in load(c):
            copy.wait()
        slot = lax.rem(c, 2)
        first = pl.multiple_of(slot * 3 * hc, LANES)
        down_first = pl.multiple_of(slot * 3 * hc + 2 * hc, LANES)

        def row_tile(i, inner):
            rows = pl.ds(pl.multiple_of(i * tile, tile), tile)
            both = dot(s.nb[rows, :], weights(first, 2 * hc))
            grad = dot(s.g_all[rows, :], weights(down_first, hc)) + dot_against(
                s.gd[rows, :], s.dsb[slot]
            )
            gate = both[:, :hc] + dot(s.cf[rows, pl.ds(0, LANES)], s.eb[slot, 0])
            up = both[:, hc:] + dot(s.cf[rows, pl.ds(LANES, LANES)], s.eb[slot, 1])
            gated = jax.nn.sigmoid(gate)
            silu = gate * gated
            act = (silu * up).astype(jnp.bfloat16)
            s.act[rows, :] = act
            grad_gate = (grad * up * gated * (1.0 + gate * (1.0 - gated))).astype(jnp.bfloat16)
            grad_up = (grad * silu).astype(jnp.bfloat16)
            s.ggu[rows, pl.ds(0, hc)] = grad_gate
            s.ggu[rows, pl.ds(hc, hc)] = grad_up
            s.acc_a[rows, :] += dot_against(act, weights(down_first, hc))
            s.cp[rows, :] += dot(act, s.dsb[slot])
            s.acc_b[rows, :] += dot_against(s.ggu[rows, :], weights(first, 2 * hc))
            s.gcf[rows, pl.ds(0, LANES)] += dot_against(grad_gate, s.eb[slot, 0])
            s.gcf[rows, pl.ds(LANES, LANES)] += dot_against(grad_up, s.eb[slot, 1])
            return inner

        lax.fori_loop(0, tiles, row_tile, 0)
        for k in range(chunks - 1):

            @pl.when(c == k)
            def _():
                for step, which in plan.bottom[k]:
                    do(step, which)
                do("last", k + 1)

        @pl.when(c + 1 < chunks)
        def _():
            for copy in load(c + 1):
                copy.start()

        at = pl.multiple_of(c * hc, LANES)
        padded = chunks * hc
        for n in range(2):
            value = dot(s.cft[pl.ds(16 * n, 16), :], s.ggu[:, pl.ds(n * hc, hc)])
            s.flat[:, pl.ds(n * padded + at, hc)] = value.astype(jnp.bfloat16)
        value = dot(s.gdt[...], s.act[...])
        s.flat[:, pl.ds(2 * padded + at, hc)] = value.astype(jnp.bfloat16)
        return carry

    lax.fori_loop(0, chunks, chunk, 0)

    codes = team_copies(7, rows_of(s.cp), slot_of(s.rc))
    for copy in codes:
        copy.start()

    def finish(i, carry):
        rows = pl.ds(pl.multiple_of(i * tile, tile), tile)
        s.na[rows, :] = s.acc_a[rows, :].astype(jnp.bfloat16)
        total = s.acc_b[rows, :]
        for n in range(2):
            lanes = pl.ds(n * LANES, LANES)
            upper, lower = split_pair(s.gcf[rows, lanes] * s.mask[...])
            s.code_t[0, pl.ds(16 * n, 16), rows] = dot_against(s.pick[...], upper).astype(
                jnp.bfloat16
            )
            s.code_t[1, pl.ds(16 * n, 16), rows] = dot_against(s.pick[...], lower).astype(
                jnp.bfloat16
            )
            total = (
                total
                + dot_against(upper, s.ffn_reduce[:, lanes])
                + dot_against(lower, s.ffn_reduce[:, lanes])
            )
        s.acc_b[rows, :] = total
        s.x_all[rows, :] = total.astype(jnp.bfloat16)
        return carry

    lax.fori_loop(0, tiles, finish, 0)
    grads = team_copies(5, rows_of(s.x_all), slot_of(s.rd))
    downs = team_copies(6, rows_of(s.na), slot_of(s.rb))
    for copy in grads + downs:
        copy.start()
    for copy in codes:
        copy.wait_recv()
    code = s.cp[own_rows, :]
    for peer in range(team - 1):
        code = code + s.rc[peer]
    rounded = (code * s.mask[...]).astype(jnp.bfloat16)
    s.cf[pl.ds(0, own), pl.ds(0, LANES)] = rounded
    turned = dot_against(s.pick[...], rounded).astype(jnp.bfloat16)
    shrunk = (dot(s.code_t[0], s.nb[...]) + dot(s.code_t[1], s.nb[...])).astype(jnp.bfloat16)
    s.rep[:, pl.ds(0, width)] = shrunk[:16]
    s.rep[:, pl.ds(width, width)] = shrunk[16:]
    s.rep[:, pl.ds(2 * width, width)] = dot(turned, s.g_all[own_rows, :]).astype(jnp.bfloat16)
    share = early.share
    reps = team_copies(
        8,
        lambda p, o: s.rep.at[:, pl.ds(pl.multiple_of(p * share, LANES), share)],
        slot_of(s.got),
    )
    for copy in reps:
        copy.start()
    for copy in grads + downs:
        copy.wait_recv()
    for copy in norms + grads + downs:
        copy.wait_send()

    def last_rows(i, carry):
        local_rows = pl.ds(pl.multiple_of(i * own_tile, own_tile), own_tile)
        rows = pl.ds(pl.multiple_of(member * own + i * own_tile, own_tile), own_tile)
        values = s.x_two[local_rows, :]
        down = s.acc_a[rows, :]
        grad = s.acc_b[rows, :]
        for peer in range(team - 1):
            down = down + s.rb[peer, local_rows, :].astype(jnp.float32)
            grad = grad + s.rd[peer, local_rows, :].astype(jnp.float32)
        out = values + down + dot(s.cf[local_rows, pl.ds(0, LANES)], s.down_lift[...])
        s.nb[local_rows, :] = out.astype(jnp.bfloat16)
        s.x_two[local_rows, :] = s.g_all[rows, :].astype(jnp.float32) + normalize_back(
            values, norm_factor(values), s.ffn_gain[...], grad
        )
        return carry

    lax.fori_loop(0, own // own_tile, last_rows, 0)
    results = [
        pltpu.make_async_copy(s.nb.at[pl.ds(0, own)], s.block_out, s.local.at[0]),
        pltpu.make_async_copy(s.x_two, s.grad_x_two, s.local.at[1]),
    ]
    for copy in results:
        copy.start()
    for copy in reps:
        copy.wait_recv()
    value = s.rep[:, pl.ds(pl.multiple_of(member * share, LANES), share)].astype(jnp.float32)
    for peer in range(team - 1):
        value = value + s.got[peer].astype(jnp.float32)
    s.flat[:, pl.ds(early.split, share)] = value.astype(jnp.bfloat16)
    rest = s.flat.shape[1] - early.total
    if rest:
        s.flat[:, pl.ds(early.total, rest)] = jnp.zeros((16, rest), jnp.bfloat16)
    flat_store = pltpu.make_async_copy(s.flat, s.ffn_flat, s.local.at[2])
    flat_store.start()
    for copy in x_copies + g_copies + codes + reps:
        copy.wait_send()
    for pieces in io_pieces:
        gather.drain(pieces)
    for k in range(chunks):
        gather.drain(chunk_pieces(k))
    for copy in results:
        copy.wait()
    flat_store.wait()


def forward_and_ffn(dims, team, early, operands):
    in_shard, out_shard, gu_shard, down_shard, x_own = operands[:5]
    rows, channels = out_shard.shape
    hc = HIDDEN_CHUNK
    chunks = down_shard.shape[1] // hc
    own, width = x_own.shape
    length = own * team
    count = dims[0] * dims[1] * dims[2]
    columns = max(4 * channels, 6 * hc)
    lanes = sum(d - 1 for d in dims) + 1
    shape = (dims, team, width, channels, length, chunks, early)
    bf16, f32 = jnp.bfloat16, jnp.float32
    anywhere = pl.BlockSpec(memory_space=pl.ANY)
    vmem = pl.BlockSpec(memory_space=pltpu.VMEM)
    outs = [
        (dims + (rows, 4 * channels), bf16, anywhere),
        ((chunks,) + dims + (rows, 3 * hc), bf16, anywhere),
        ((3, length, channels), f32, anywhere),
        ((length, width), bf16, anywhere),
        ((length, channels), bf16, anywhere),
        ((16, length), bf16, vmem),
        ((16, own), bf16, vmem),
        ((own, width), bf16, anywhere),
        ((own, width), f32, anywhere),
        ((16, count * early.block), bf16, anywhere),
    ]
    peers = max(team - 1, 1)
    row_count = 12 + 2 * chunks
    scratch = [
        pltpu.VMEM((length, width), bf16),
        pltpu.VMEM((length, width), bf16),
        pltpu.VMEM((length, width), bf16),
        pltpu.VMEM((length, width), bf16),
        pltpu.VMEM(dims + (rows, columns), bf16),
        pltpu.VMEM((length, width), f32),
        pltpu.VMEM((length, width), f32),
        pltpu.VMEM((own, width), f32),
        pltpu.VMEM((ROW_TILE + 8, channels), f32),
        pltpu.VMEM((length, channels), bf16),
        pltpu.VMEM((length, LANES), f32),
        pltpu.VMEM((length, 2 * LANES), f32),
        pltpu.VMEM((length, 2 * LANES), bf16),
        pltpu.VMEM((length, LANES), bf16),
        pltpu.VMEM((32, length), bf16),
        pltpu.VMEM((16, length), bf16),
        pltpu.VMEM((length, hc), bf16),
        pltpu.VMEM((length, 2 * hc), bf16),
        pltpu.VMEM((2, 2, LANES, hc), bf16),
        pltpu.VMEM((2, hc, LANES), bf16),
        pltpu.VMEM((peers, own, width), bf16),
        pltpu.VMEM((peers, own, LANES), f32),
        pltpu.VMEM((peers, own, width), bf16),
        pltpu.VMEM((2, 32, length), bf16),
        pltpu.VMEM((16, count * early.block), bf16),
        pltpu.VMEM((16, early.shared), bf16),
        pltpu.VMEM((peers, 16, early.share), bf16),
        pltpu.SemaphoreType.DMA((row_count, lanes)),
        pltpu.SemaphoreType.DMA((row_count, lanes)),
        pltpu.SemaphoreType.DMA((9, peers)),
        pltpu.SemaphoreType.DMA((9, peers)),
        pltpu.SemaphoreType.DMA((max(4 + 3 * chunks, 8),)),
        pltpu.SemaphoreType.DMA((6,)),
    ]
    return pl.pallas_call(
        functools.partial(forward_kernel, shape),
        out_shape=[jax.ShapeDtypeStruct(o[0], o[1]) for o in outs],
        in_specs=[anywhere] * 8 + [vmem] * 12,
        out_specs=[o[2] for o in outs],
        scratch_shapes=scratch,
        compiler_params=pltpu.CompilerParams(
            collective_id=0, has_side_effects=True, vmem_limit_bytes=67043328
        ),
    )(*operands)


BACK_NAMES = (
    "grad_x_two",
    "ffn_flat",
    "io_whole",
    "streams",
    "norm_one",
    "conv_out",
    "x_own",
    "code_in",
    "code_out",
    "same",
    "conv_gain",
    "taps",
    "in_reduce",
    "in_lift",
    "out_reduce",
    "out_lift",
    "mask",
    "pick",
    "onehot",
    "grad_residual",
    "early",
    "late",
    "early_rep",
    "late_rep",
    "w",
    "gx",
    "gb",
    "gco",
    "gcot",
    "st",
    "gs",
    "gci",
    "ha",
    "hb",
    "halo",
    "na",
    "co",
    "pb",
    "gcit",
    "xo",
    "rb",
    "rep_b",
    "got_b",
    "flat_a",
    "flat_b",
    "part_a",
    "part_b",
    "from_a",
    "from_b",
    "sum_a",
    "sum_b",
    "spare_a",
    "spare_b",
    "out",
    "send",
    "recv",
    "swap_send",
    "swap_recv",
    "team_send",
    "team_recv",
    "local",
)


class Share:
    def __init__(self, count, team, split, shared):
        self.split, self.shared, self.share = split, shared, shared // team
        self.total = split + self.share
        self.block = -(-self.total // (LANES * count)) * LANES
        self.first = split // self.block
        self.blocks = -(-self.total // self.block) - self.first


def backward_kernel(shape, *refs):
    s = types.SimpleNamespace(**dict(zip(BACK_NAMES, refs)))
    dims, team, width, channels, length, early, late = shape
    count = dims[0] * dims[1] * dims[2]
    own = length // team
    tile = ROW_TILE
    tiles = length // tile
    own_tile = min(own, tile)
    member = lax.axis_index("tensor")
    me = lax.axis_index("dp")
    spot = position(me, dims)
    gather = Gather(dims, spot, s.send, s.recv)
    own_rows = pl.ds(pl.multiple_of(member * own, own), own)

    def enter():
        barrier = pltpu.get_barrier_semaphore()
        for offset in range(1, count):
            pl.semaphore_signal(
                barrier, inc=1, device_id={"dp": lax.rem(me + offset, count)}, device_id_type=MESH
            )
        for offset in range(1, team):
            pl.semaphore_signal(
                barrier,
                inc=1,
                device_id={"tensor": lax.rem(member + offset, team)},
                device_id_type=MESH,
            )
        pl.semaphore_wait(barrier, count - 1 + team - 1)

    def team_copies(row, source, target):
        out = []
        for offset in range(1, team):
            peer = lax.rem(member + offset, team)
            out.append(
                pltpu.make_async_remote_copy(
                    src_ref=source(peer, offset),
                    dst_ref=target(peer, offset),
                    send_sem=s.team_send.at[row, offset - 1],
                    recv_sem=s.team_recv.at[row, offset - 1],
                    device_id={"tensor": peer},
                    device_id_type=MESH,
                )
            )
        return out

    def swap_copies(row, part, landing):
        out = []
        for offset in range(1, count):
            peer = lax.rem(me + offset, count)
            out.append(
                pltpu.make_async_remote_copy(
                    src_ref=part.at[peer],
                    dst_ref=landing.at[me],
                    send_sem=s.swap_send.at[row, offset - 1],
                    recv_sem=s.swap_recv.at[row, offset - 1],
                    device_id={"dp": peer},
                    device_id_type=MESH,
                )
            )
        return out

    def pieces_of(share, whole, row):
        out = []
        step = max(share.block // 384, 1) * LANES
        for n, first in enumerate(range(0, share.block, step)):
            order = (0, 1, 2) if n % 2 == 0 else (0, 2, 1)
            out.append((whole, pl.ds(first, min(step, share.block - first)), order, row + n, False))
        return out

    def forward_on(pieces, step):
        for piece in pieces:
            gather.arrive([piece], step)
            gather.start([piece], step + 1)

    def hand_out(share, columns, part, landing, row):
        for peer in range(count):
            part[peer, :, pl.ds(0, share.block)] = columns[:, pl.ds(peer * share.block, share.block)]
            part[peer, :, pl.ds(share.block, LANES)] = s.onehot[...]
        landing[me] = part[me]
        copies = swap_copies(row, part, landing)
        for copy in copies:
            copy.start()
        return copies

    def take_in(share, landing, total):
        for adapter in range(ADAPTER_COUNT):

            def add(source, value):
                mask = landing[source, adapter : adapter + 1, pl.ds(share.block, LANES)]
                mask = mask.astype(jnp.float32)[:, 0:1]
                return value + mask * landing[source, :, pl.ds(0, share.block)].astype(jnp.float32)

            value = lax.fori_loop(0, count, add, jnp.zeros((16, share.block), jnp.float32))
            total[pl.ds(adapter * 16, 16), :] = value.astype(jnp.bfloat16)

    loads = {}
    for slot, (name, source, target) in enumerate(
        [
            ("flat", s.ffn_flat, s.flat_a),
            ("gx", s.grad_x_two, s.gx),
            ("co", s.conv_out, s.co),
            ("w", s.io_whole, s.w),
            ("b", s.streams.at[0], s.st.at[0, pl.ds(8, length)]),
            ("c", s.streams.at[1], s.st.at[1, pl.ds(8, length)]),
            ("x", s.streams.at[2], s.st.at[2, pl.ds(8, length)]),
            ("na", s.norm_one, s.na),
            ("xo", s.x_own, s.xo),
        ]
    ):
        loads[name] = pltpu.make_async_copy(source, target, s.local.at[slot])
        loads[name].start()
    enter()
    loads["flat"].wait()
    sent_a = hand_out(early, s.flat_a, s.part_a, s.from_a, 0)
    s.st[0, pl.ds(0, 8), :] = jnp.zeros((8, channels), jnp.float32)
    s.st[2, pl.ds(0, 8), :] = jnp.zeros((8, channels), jnp.float32)
    s.ha[pl.ds(tile, 8), :] = jnp.zeros((8, channels), jnp.float32)
    s.hb[pl.ds(tile, 8), :] = jnp.zeros((8, channels), jnp.float32)
    loads["gx"].wait()

    def branch_rows(i, carry):
        local_rows = pl.ds(pl.multiple_of(i * own_tile, own_tile), own_tile)
        rows = pl.ds(pl.multiple_of(member * own + i * own_tile, own_tile), own_tile)
        upper, lower = split_pair(s.gx[local_rows, :])
        s.gb[rows, :] = upper
        code = dot_against(upper, s.out_lift[...]) + dot_against(lower, s.out_lift[...])
        s.gco[rows, :] = (code * s.mask[...]).astype(jnp.bfloat16)
        return carry

    lax.fori_loop(0, own // own_tile, branch_rows, 0)
    swaps = team_copies(0, lambda p, o: s.gb.at[own_rows], lambda p, o: s.gb.at[own_rows])
    swaps += team_copies(1, lambda p, o: s.gco.at[own_rows], lambda p, o: s.gco.at[own_rows])
    for copy in swaps:
        copy.start()
    upper, lower = split_pair(s.gx[...])
    s.rep_b[:, pl.ds(width, width)] = (
        dot(s.code_out[...], upper) + dot(s.code_out[...], lower)
    ).astype(jnp.bfloat16)
    for copy in swaps:
        copy.wait_recv()

    def turn(i, carry):
        rows = pl.ds(pl.multiple_of(i * tile, tile), tile)
        s.gcot[:, rows] = dot_against(s.pick[...], s.gco[rows, :]).astype(jnp.bfloat16)
        return carry

    lax.fori_loop(0, tiles, turn, 0)
    loads["co"].wait()
    s.flat_b[:, pl.ds(3 * channels, channels)] = dot(s.gcot[...], s.co[...]).astype(jnp.bfloat16)
    pieces_a = pieces_of(early, s.early, 0)
    pieces_b = pieces_of(late, s.late, len(pieces_a))
    place_a = pltpu.make_async_copy(s.sum_a, s.early.at[spot], s.local.at[0])
    place_b = pltpu.make_async_copy(s.sum_b, s.late.at[spot], s.local.at[1])

    for name in ("w", "b", "c", "x"):
        loads[name].wait()

    def weights(first, amount):
        return s.w[:, :, :, :, pl.ds(first, amount)].reshape(width, amount)

    def back(j, carry):
        i = tiles - 1 - j
        start = pl.multiple_of(i * tile, tile)
        rows = pl.ds(start, tile)
        later = pl.ds(pl.multiple_of(start + 8, 8), tile)
        grad = dot(s.gb[rows, :], weights(3 * channels, channels)) + dot_against(
            s.gco[rows, :], s.out_reduce[...]
        )
        s.halo[pl.ds(0, 8), :] = s.st[0, pl.ds(start, 8), :] * s.st[2, pl.ds(start, 8), :]
        product = s.st[0, later, :] * s.st[2, later, :]
        s.halo[pl.ds(8, tile), :] = product
        masks = s.same[rows, :]
        taps = s.taps[...].astype(jnp.float32)
        mixed = (
            taps[0:1, :] * product
            + taps[1:2, :] * s.halo[pl.ds(7, tile), :] * masks[:, 0:1]
            + taps[2:3, :] * s.halo[pl.ds(6, tile), :] * masks[:, 1:2]
        )
        grad_mixed = grad * s.st[1, later, :]
        s.ha[pl.ds(0, tile), :] = taps[1:2, :] * grad_mixed * masks[:, 0:1]
        s.hb[pl.ds(0, tile), :] = taps[2:3, :] * grad_mixed * masks[:, 1:2]
        grad_product = taps[0:1, :] * grad_mixed + s.ha[pl.ds(1, tile), :] + s.hb[pl.ds(2, tile), :]
        s.ha[pl.ds(tile, 8), :] = s.ha[pl.ds(0, 8), :]
        s.hb[pl.ds(tile, 8), :] = s.hb[pl.ds(0, 8), :]
        s.gs[rows, pl.ds(0, channels)] = (grad_product * s.st[2, later, :]).astype(jnp.bfloat16)
        s.gs[rows, pl.ds(channels, channels)] = (grad * mixed).astype(jnp.bfloat16)
        s.gs[rows, pl.ds(2 * channels, channels)] = (grad_product * s.st[0, later, :]).astype(
            jnp.bfloat16
        )
        upper, lower = split_pair(dot_against(s.gs[rows, :], s.in_lift[...]) * s.mask[...])
        s.gci[0, rows, :] = upper
        s.gci[1, rows, :] = lower
        s.gcit[0, :, rows] = dot_against(s.pick[...], upper).astype(jnp.bfloat16)
        s.gcit[1, :, rows] = dot_against(s.pick[...], lower).astype(jnp.bfloat16)

        @pl.when(j == 0)
        def _():
            for copy in sent_a:
                copy.wait_recv()
            take_in(early, s.from_a, s.sum_a)
            place_a.start()

        @pl.when(j == 1)
        def _():
            place_a.wait()
            gather.start(pieces_a, 0)

        return carry

    lax.fori_loop(0, tiles, back, 0)
    forward_on(pieces_a[:2], 0)
    loads["na"].wait()
    s.rep_b[:, pl.ds(0, width)] = (
        dot(s.gcit[0], s.na[...]) + dot(s.gcit[1], s.na[...])
    ).astype(jnp.bfloat16)
    share = late.share
    more = team_copies(
        2,
        lambda p, o: s.rep_b.at[:, pl.ds(pl.multiple_of(p * share, LANES), share)],
        lambda p, o: s.got_b.at[o - 1],
    )
    for copy in more:
        copy.start()
    s.flat_b[:, pl.ds(0, 3 * channels)] = dot(s.code_in[...], s.gs[...]).astype(jnp.bfloat16)
    for copy in more:
        copy.wait_recv()
    value = s.rep_b[:, pl.ds(pl.multiple_of(member * share, LANES), share)].astype(jnp.float32)
    for peer in range(team - 1):
        value = value + s.got_b[peer].astype(jnp.float32)
    s.flat_b[:, pl.ds(late.split, share)] = value.astype(jnp.bfloat16)
    rest = count * late.block - late.total
    if rest:
        s.flat_b[:, pl.ds(late.total, rest)] = jnp.zeros((16, rest), jnp.bfloat16)
    sent_b = hand_out(late, s.flat_b, s.part_b, s.from_b, 1)
    forward_on(pieces_a[2:], 0)
    grads = team_copies(
        3,
        lambda p, o: s.pb.at[pl.ds(pl.multiple_of(p * own, own), own)],
        lambda p, o: s.rb.at[o - 1],
    )
    per_own = own // tile

    def norm_grads(j, carry):
        i = lax.rem((member + 1) * per_own + j, tiles)
        rows = pl.ds(pl.multiple_of(i * tile, tile), tile)
        s.pb[rows, :] = (
            dot_against(s.gs[rows, :], weights(0, 3 * channels))
            + dot_against(s.gci[0, rows, :], s.in_reduce[...])
            + dot_against(s.gci[1, rows, :], s.in_reduce[...])
        ).astype(jnp.bfloat16)
        for offset in range(1, team):

            @pl.when(j == offset * per_own - 1)
            def _():
                grads[offset - 1].start()

        @pl.when(j == 0)
        def _():
            forward_on(pieces_a[:2], 1)

        @pl.when(j == 1)
        def _():
            for copy in sent_b:
                copy.wait_recv()
            take_in(late, s.from_b, s.sum_b)
            place_b.start()

        @pl.when(j == 2)
        def _():
            place_b.wait()
            gather.start(pieces_b, 0)
            forward_on(pieces_a[2:], 1)

        return carry

    lax.fori_loop(0, tiles, norm_grads, 0)
    loads["xo"].wait()
    forward_on(pieces_b, 0)
    for copy in grads:
        copy.wait_recv()

    def residual_rows(i, carry):
        local_rows = pl.ds(pl.multiple_of(i * own_tile, own_tile), own_tile)
        rows = pl.ds(pl.multiple_of(member * own + i * own_tile, own_tile), own_tile)
        values = s.xo[local_rows, :].astype(jnp.float32)
        grad = s.pb[rows, :].astype(jnp.float32)
        for peer in range(team - 1):
            grad = grad + s.rb[peer, local_rows, :].astype(jnp.float32)
        s.out[local_rows, :] = (
            s.gx[local_rows, :]
            + normalize_back(values, norm_factor(values), s.conv_gain[...], grad)
        ).astype(jnp.bfloat16)
        return carry

    lax.fori_loop(0, own // own_tile, residual_rows, 0)
    result = pltpu.make_async_copy(s.out, s.grad_residual, s.local.at[2])
    result.start()

    def pass_on(share, whole, reps, spare, base):
        lifts = []
        for block in range(share.blocks):
            here = whole.at[position(share.first + block, dims)]
            lifts.append(pltpu.make_async_copy(here, spare.at[block], s.local.at[3 + block]))
        for lift in lifts:
            lift.start()
        for lift in lifts:
            lift.wait()
        out = team_copies(base, lambda p, o: spare, lambda p, o: reps.at[member])
        for copy in out:
            copy.start()
        keep = pltpu.make_async_copy(spare, reps.at[member], s.local.at[3])
        keep.start()
        return out, keep

    forward_on(pieces_b, 1)
    gather.arrive(pieces_a, 2)
    out_a, keep_a = pass_on(early, s.early, s.early_rep, s.spare_a, 4)
    keep_a.wait()
    gather.arrive(pieces_b, 2)
    out_b, keep_b = pass_on(late, s.late, s.late_rep, s.spare_b, 5)
    for copy in out_a + out_b:
        copy.wait_recv()
    for copy in out_a + out_b + swaps + grads + more + sent_a + sent_b:
        copy.wait_send()
    gather.drain(pieces_a + pieces_b)
    keep_b.wait()
    result.wait()


def backward(dims, team, early, late, operands):
    _, _, io_whole, _, _, conv_out, x_own = operands[:7]
    count = dims[0] * dims[1] * dims[2]
    own, width = x_own.shape
    length, channels = conv_out.shape
    lanes = sum(d - 1 for d in dims)
    bf16, f32 = jnp.bfloat16, jnp.float32
    anywhere = pl.BlockSpec(memory_space=pl.ANY)
    vmem = pl.BlockSpec(memory_space=pltpu.VMEM)
    rows = ADAPTER_COUNT * 16
    peers = max(team - 1, 1)
    outs = [
        ((own, width), bf16),
        (dims + (rows, early.block), bf16),
        (dims + (rows, late.block), bf16),
        ((team, early.blocks, rows, early.block), bf16),
        ((team, late.blocks, rows, late.block), bf16),
    ]
    scratch = [
        pltpu.VMEM(io_whole.shape, bf16),
        pltpu.VMEM((own, width), f32),
        pltpu.VMEM((length, width), bf16),
        pltpu.VMEM((length, LANES), bf16),
        pltpu.VMEM((16, length), bf16),
        pltpu.VMEM((3, length + 8, channels), f32),
        pltpu.VMEM((length, 3 * channels), bf16),
        pltpu.VMEM((2, length, LANES), bf16),
        pltpu.VMEM((ROW_TILE + 8, channels), f32),
        pltpu.VMEM((ROW_TILE + 8, channels), f32),
        pltpu.VMEM((ROW_TILE + 8, channels), f32),
        pltpu.VMEM((length, width), bf16),
        pltpu.VMEM((length, channels), bf16),
        pltpu.VMEM((length, width), bf16),
        pltpu.VMEM((2, 16, length), bf16),
        pltpu.VMEM((own, width), bf16),
        pltpu.VMEM((peers, own, width), bf16),
        pltpu.VMEM((16, late.shared), bf16),
        pltpu.VMEM((peers, 16, late.share), bf16),
        pltpu.VMEM((16, count * early.block), bf16),
        pltpu.VMEM((16, count * late.block), bf16),
        pltpu.VMEM((count, 16, early.block + LANES), bf16),
        pltpu.VMEM((count, 16, late.block + LANES), bf16),
        pltpu.VMEM((count, 16, early.block + LANES), bf16),
        pltpu.VMEM((count, 16, late.block + LANES), bf16),
        pltpu.VMEM((rows, early.block), bf16),
        pltpu.VMEM((rows, late.block), bf16),
        pltpu.VMEM((early.blocks, rows, early.block), bf16),
        pltpu.VMEM((late.blocks, rows, late.block), bf16),
        pltpu.VMEM((own, width), bf16),
        pltpu.SemaphoreType.DMA((12, lanes)),
        pltpu.SemaphoreType.DMA((12, lanes)),
        pltpu.SemaphoreType.DMA((2, count - 1)),
        pltpu.SemaphoreType.DMA((2, count - 1)),
        pltpu.SemaphoreType.DMA((6, peers)),
        pltpu.SemaphoreType.DMA((6, peers)),
        pltpu.SemaphoreType.DMA((max(10, 3 + max(early.blocks, late.blocks)),)),
    ]
    return pl.pallas_call(
        functools.partial(backward_kernel, (dims, team, width, channels, length, early, late)),
        out_shape=[jax.ShapeDtypeStruct(*o) for o in outs],
        in_specs=[anywhere] * 7 + [vmem] * (len(operands) - 7),
        out_specs=[anywhere] * 5,
        scratch_shapes=scratch,
        compiler_params=pltpu.CompilerParams(
            collective_id=1, has_side_effects=True, vmem_limit_bytes=67043328
        ),
    )(*operands)


def lagged_segments(segment_ids, lag):
    shifted = jnp.pad(segment_ids, ((0, 0), (lag, 0)), constant_values=-1)[
        :, : segment_ids.shape[1]
    ]
    return (segment_ids == shifted).astype(jnp.float32)


def pad_axis(values, axis, size):
    widths = [(0, 0)] * values.ndim
    widths[axis] = (0, size - values.shape[axis])
    return jnp.pad(values, widths)


def per_device(
    residual,
    cotangent,
    segment_ids,
    adapter_ids,
    conv_gain,
    proj_in,
    conv_taps,
    proj_out,
    ffn_gain,
    gate_up,
    proj_down,
    in_shrink,
    input_lift_weight,
    output_reduce_weight,
    output_lift_weight,
    ffn_reduce_weight,
    ffn_expand,
    down_shrink,
    down_lift_weight,
):
    own, width = residual.shape
    length = segment_ids.shape[1]
    team = length // own
    count = lax.axis_size("dp")
    dims = split_ring(count)
    rows, _, channels = proj_in.shape
    hidden = proj_down.shape[1]
    hc = HIDDEN_CHUNK
    chunks = -(-hidden // hc)
    padded = chunks * hc
    adapter = adapter_ids[0]

    in_shard = proj_in.reshape(rows, 3 * channels)
    gu_shard = pad_axis(jnp.transpose(gate_up, (1, 0, 2)), 2, padded)
    down_shard = pad_axis(proj_down, 1, padded)
    codes = ADAPTER_COUNT * ADAPTER_RANK
    in_reduce = in_shrink.reshape(width, codes)
    in_lift = input_lift_weight.reshape(codes, 3 * channels)
    out_reduce = output_reduce_weight.reshape(channels, codes)
    out_lift = output_lift_weight.reshape(codes, width)
    ffn_reduce = ffn_reduce_weight.reshape(width, 2 * codes)
    expand = pad_axis(ffn_expand.reshape(2, codes, hidden), 2, padded)
    shrink = pad_axis(down_shrink.reshape(hidden, codes), 0, padded)
    down_lift = down_lift_weight.reshape(codes, width)
    lane = jnp.arange(codes, dtype=jnp.int32)[None, :]
    row = jnp.arange(ADAPTER_RANK, dtype=jnp.int32)[:, None]
    mask = (lane // ADAPTER_RANK == adapter).astype(jnp.float32)
    pick = (lane == adapter * ADAPTER_RANK + row).astype(jnp.bfloat16)
    marks = jnp.broadcast_to(row == adapter, (ADAPTER_RANK, LANES)).astype(jnp.bfloat16)
    first_same, second_same = lagged_segments(segment_ids, 1)[0], lagged_segments(segment_ids, 2)[0]
    same = jnp.stack([first_same, second_same], axis=1)
    early = Share(count, team, 3 * padded, 3 * width)
    late = Share(count, team, 4 * channels, 2 * width)
    (
        io_whole,
        _,
        streams,
        norm_one,
        conv_out,
        code_in,
        code_out,
        block_output,
        grad_x_two,
        ffn_flat,
    ) = forward_and_ffn(
        dims,
        team,
        early,
        (
            in_shard,
            proj_out,
            gu_shard,
            down_shard,
            residual,
            cotangent,
            expand,
            shrink,
            same,
            conv_gain.reshape(1, width),
            ffn_gain.reshape(1, width),
            conv_taps,
            in_reduce,
            in_lift,
            out_reduce,
            out_lift,
            ffn_reduce,
            down_lift,
            mask,
            pick,
        ),
    )
    grad_residual, early_sums, late_sums, early_shared, late_shared = backward(
        dims,
        team,
        early,
        late,
        (
            grad_x_two,
            ffn_flat,
            io_whole,
            streams,
            norm_one,
            conv_out,
            residual,
            code_in,
            code_out,
            same,
            conv_gain.reshape(1, width),
            conv_taps,
            in_reduce,
            in_lift,
            out_reduce,
            out_lift,
            mask,
            pick,
            marks,
        ),
    )

    def columns_of(sums, share):
        sums = sums.reshape(count, ADAPTER_COUNT, ADAPTER_RANK, share.block)
        return jnp.transpose(sums, (1, 2, 0, 3)).reshape(
            ADAPTER_COUNT, ADAPTER_RANK, count * share.block
        )

    def shared_columns(sums, share):
        sums = sums.reshape(team, share.blocks, ADAPTER_COUNT, ADAPTER_RANK, share.block)
        sums = jnp.transpose(sums, (2, 3, 0, 1, 4)).reshape(
            ADAPTER_COUNT, ADAPTER_RANK, team, share.blocks * share.block
        )
        skip = share.split - share.first * share.block
        return sums[..., skip : skip + share.share].reshape(
            ADAPTER_COUNT, ADAPTER_RANK, share.shared
        )

    def rows_first(values):
        return jnp.transpose(values, (2, 0, 1)).astype(jnp.float32)

    early_columns, late_columns = columns_of(early_sums, early), columns_of(late_sums, late)
    early_rest, late_rest = shared_columns(early_shared, early), shared_columns(late_shared, late)
    ffn_e = jnp.stack([early_columns[..., :hidden], early_columns[..., padded : padded + hidden]])
    ffn_e = ffn_e.astype(jnp.float32)
    down_s = rows_first(early_columns[..., 2 * padded : 2 * padded + hidden])
    out_s = rows_first(late_columns[..., 3 * channels : 4 * channels])
    ffn_s = jnp.stack(
        [rows_first(early_rest[..., :width]), rows_first(early_rest[..., width : 2 * width])],
        axis=1,
    )
    down_e = early_rest[..., 2 * width : 3 * width].astype(jnp.float32)
    out_e = late_rest[..., width:].astype(jnp.float32)
    in_e = late_columns[..., : 3 * channels].astype(jnp.float32)
    in_e = in_e.reshape(ADAPTER_COUNT, ADAPTER_RANK, 3, channels)
    in_s = rows_first(late_rest[..., :width])
    return (block_output, grad_residual, in_s, in_e, out_s, out_e, ffn_s, ffn_e, down_s, down_e)


def solution(mesh):
    rows = P(("dp", "tensor"), None)
    placed = (
        rows,
        rows,
        P("dp", None),
        P("dp"),
        P(),
        P("dp", None, "tensor"),
        P(None, "tensor"),
        P("dp", "tensor"),
        P(),
        P("dp", None, "tensor"),
        P("dp", "tensor"),
        P(),
        P(None, None, None, "tensor"),
        P("tensor", None, None),
        P(),
        P(),
        P(None, None, None, "tensor"),
        P("tensor", None, None),
        P(),
    )
    return jax.shard_map(
        per_device,
        mesh=mesh,
        in_specs=placed,
        out_specs=(
            rows,
            rows,
            P(),
            P(None, None, None, "tensor"),
            P("tensor", None, None),
            P(),
            P(),
            P(None, None, None, "tensor"),
            P("tensor", None, None),
            P(),
        ),
        check_vma=False,
    )
```

time: 603 us -> 498 us (0.83)
  Pallas kernels: 542 us -> 457 us
  local copies, waits for them, and re-layouts: 44.7 us -> 25.6 us
    pallas_call x1, Pallas kernels: 413 us -> 367 us  [forward_and_ffn(): pl.pallas_call(functools.partial(forward_kernel, shape), out_shape=[jax.S...]
    pallas_call x1, Pallas kernels: 129 us -> 89.8 us  [backward(): pl.pallas_call(functools.partial(backward_kernel, (dims, team, width, cha...]
    pad x8 -> x0, local copies, waits for them, and re-layouts: 7.23 us -> none  [pad_axis(): return jnp.pad(values, widths)]
where the time goes in v3:
time: 498 us; the launch traced here: 494 us
  Pallas kernels  457 us (92%)
  local copies, waits for them, and re-layouts  25.6 us (5%)
  other arithmetic  10 us (2%)
    pallas_call x1, Pallas kernels, forward_and_ffn(): pl.pallas_call(functools.partial(forward_kernel, shape), out_shape=[jax.S...  367 us
    pallas_call x1, Pallas kernels, backward(): pl.pallas_call(functools.partial(backward_kernel, (dims, team, width, cha...  89.8 us
    unnamed x32, local copies, waits for them, and re-layouts  10.1 us

profile of v3, /device:TPU:0, one launch (start us, length us, event | category | flops | bytes accessed | tf_op | source)
XLA Modules:
  0.0 493.8 jit_solution(4347058098303259485)
XLA Ops:
  0.6 0.9 compare_bitcast_fusion.1
  1.6 0.3 copy.74
  1.8 0.0 copy-start.9
  1.9 0.8 stack.29.refs_8_.refs_9_
  3.4 0.7 fusion.refs_19_.refs_17_
  4.0 0.5 compare_convert_fusion.1.refs_18_.refs_16_
  4.5 0.0 copy-start.10
  4.5 1.5 copy.75
  6.1 0.0 copy-start.11
  6.1 0.0 copy-start.4
  6.1 0.9 copy.93
  7.0 0.0 copy-done.9
  7.0 0.9 copy.77.refs_12_
  7.9 0.0 copy-start.5
  7.9 0.0 copy-done.10
  7.9 0.8 copy.78.refs_14_
  8.7 0.0 copy-done.11
  8.7 0.6 reshape.163.refs_9_.refs_10_
  9.3 0.0 copy-done.4
  9.3 0.0 copy-start.6
  9.3 1.2 copy.98
  10.5 0.0 copy-done.5
  10.5 0.0 copy-start.8
  10.5 1.3 copy.76.refs_7_
  11.8 0.0 copy-start.12
  11.8 0.0 copy-done.6
  11.8 1.2 copy.79.refs_16_
  13.0 0.0 copy-done.8
  13.0 0.8 copy.89
  13.8 0.0 copy-done.12
  13.8 0.6 reshape.164.refs_10_
  14.4 366.9 %shard_map.258 = (bf16[4,2,2,96,3072]{4,3,2,1,0:T(8,128)(2,1)}, bf16[9,4,2,2,96,1152]{5,4,3,2,1,0:T(8,128)(2,1)}, f32[3,1024,768]{2,1,0:T(8,128)}, bf16[1024,153...) custom-call(bf16[96,2304]{1,0:T(8,128)(2,1)} %bitcast.80, ...), custom_call_target="tpu_custom_call" | custom-call | tf_op jit(solution)/shard_map/pallas_call | solution.py:801
  381.3 0.7 broadcast_in_dim.2.refs_18_
  382.0 89.8 %shard_map.259 = (bf16[512,1536]{1,0:T(8,128)(2,1)}, bf16[4,2,2,128,896]{4,3,2,1,0:T(8,128)(2,1)}, bf16[4,2,2,128,384]{4,3,2,1,0:T(8,128)(2,1)}, bf16[2,4,128,89...) custom-call(f32[512,1536]{1,0:T(8,128)} %get-tuple-element.25.refs_0_, bf16[16,14336]{1,0:T(8,128)(2,1)} %get-tuple-element.26.refs_1_, ...), custom_call_target="tpu_custom_call" | custom-call | tf_op jit(solution)/shard_map/pallas_call | solution.py:1273
  471.8 2.6 copy.92
  474.4 1.5 convert_bitcast_fusion
  475.9 0.0 copy-start
  475.9 2.0 maximum_convert_fusion
  477.9 0.2 copy-done
  478.1 1.4 copy.97
  479.6 1.7 reshape.177
  481.3 1.3 slice_bitcast_fusion
  482.6 0.0 copy-start.7
  482.6 0.1 copy.91
  482.7 1.0 copy-done.7
  483.8 0.6 copy.82
  484.4 0.6 reshape_reshape.3
  485.0 1.5 slice_convert_fusion.1
  486.4 0.0 copy-start.3
  486.4 1.2 maximum_convert_fusion.1
  487.7 0.7 copy-done.3
  488.4 0.2 copy.90
  488.7 0.1 slice_convert_fusion
  488.7 0.0 copy-start.1
  488.8 1.1 copy.99
  489.9 0.8 convert_bitcast_fusion.2
  490.7 0.0 copy-done.1
  490.7 0.0 copy-start.2
  490.7 1.1 copy.103
  491.8 0.8 copy-done.2
  492.7 1.1 copy.104
  (3 shorter events, 0.0 us)
Async XLA Ops:
  1.8 5.1 %copy-start.9 = (bf16[1536,8,16]{0,2,1:T(8,128)(2,1)S(1)}, bf16[1536,8,16]{0,2,1:T(8,128)(2,1)}, u32[]{:S(2)}) copy-start(bf16[1536,8,16]{0,2,1:T(8,128)(2,1)} %param.30) | copy-start | bytes 1179652
  4.5 3.3 copy-start.10
  6.1 2.6 copy-start.11
  6.1 3.2 copy-start.4
  7.9 2.6 copy-start.5
  9.3 2.5 copy-start.6
  10.5 2.5 copy-start.8
  11.8 2.0 copy-start.12
  475.9 2.3 copy-start
  482.6 1.1 copy-start.7
  486.4 2.0 copy-start.3
  488.7 1.9 copy-start.1
  490.7 2.0 copy-start.2

commit v4 on v3

v4 whole, which is shorter than its diff:
```python
import functools

import jax
import jax.numpy as jnp
from jax import lax
from jax.experimental import pallas as pl
from jax.experimental.pallas import tpu as pltpu
from jax.sharding import PartitionSpec as P

ADAPTER_COUNT = 8
ADAPTER_RANK = 16
EPSILON = 1e-05
MESH = pl.DeviceIdType.MESH
LANES = 128
HIDDEN_CHUNK = 384
ROW_TILE = 256


def dot(left, right):
    return jnp.dot(left, right, preferred_element_type=jnp.float32)


def dot_against(left, right):
    return lax.dot_general(
        left, right, (((1,), (1,)), ((), ())), preferred_element_type=jnp.float32
    )


def split_pair(values):
    upper = values.astype(jnp.bfloat16)
    lower = (values - upper.astype(jnp.float32)).astype(jnp.bfloat16)
    return (upper, lower)


def norm_factor(values):
    return lax.rsqrt(jnp.mean(values * values, axis=-1, keepdims=True) + EPSILON)


def normalize_back(values, factor, gain, grad):
    unit = values * factor
    scaled = grad * gain
    return factor * (scaled - unit * jnp.mean(scaled * unit, axis=-1, keepdims=True))


def split_ring(count):
    if count % 16 == 0:
        return (4, count // 8, 2)
    return (count, 1, 1)


def position(index, dims):
    return (index // (dims[1] * dims[2]), (index // dims[2]) % dims[1], index % dims[2])


def flat(spot, dims):
    return (spot[0] * dims[1] + spot[1]) * dims[2] + spot[2]


class Gather:
    def __init__(self, dims, spot, send, recv):
        self.dims, self.spot, self.send, self.recv = dims, spot, send, recv

    def place(self, piece, step, along=None):
        whole, columns, order = piece[:3]
        spot = list(self.spot)
        if along is not None:
            spot[order[step]] = along
        place = tuple(
            slice(None) if other in order[:step] else spot[other] for other in range(3)
        )
        return whole.at[place + (slice(None), columns)]

    def lined(self, piece, step):
        return piece[4] and piece[2][step] == 0 and self.dims[0] == 4

    def copies(self, piece, step, offsets=None):
        _, _, order, row, _ = piece
        axis = order[step]
        target = self.place(piece, step)
        base = sum(self.dims[other] - 1 for other in order[:step])
        out = []
        for offset in offsets or range(1, self.dims[axis]):
            peer = list(self.spot)
            peer[axis] = lax.rem(self.spot[axis] + offset, self.dims[axis])
            out.append(
                pltpu.make_async_remote_copy(
                    src_ref=target,
                    dst_ref=target,
                    send_sem=self.send.at[row, base + offset - 1],
                    recv_sem=self.recv.at[row, base + offset - 1],
                    device_id={"dp": flat(peer, self.dims)},
                    device_id_type=MESH,
                )
            )
        return out

    def passed(self, piece, step, here):
        _, _, order, row, _ = piece
        block = self.place(piece, step, 3 if here == 1 else 0)
        base = sum(self.dims[other] - 1 for other in order[:step])
        lanes = sum(d - 1 for d in self.dims)
        peer = list(self.spot)
        peer[0] = 0 if here == 1 else 3
        return pltpu.make_async_remote_copy(
            src_ref=block,
            dst_ref=block,
            send_sem=self.send.at[row, lanes],
            recv_sem=self.recv.at[row, base + (0 if here == 1 else 2)],
            device_id={"dp": flat(peer, self.dims)},
            device_id_type=MESH,
        )

    def own(self, piece, step, act):
        copies = self.copies(piece, step)
        if not self.lined(piece, step):
            for copy in copies:
                act(copy)
            return
        act(copies[1])
        pl.when(self.spot[0] != 3)(lambda: act(copies[0]))
        pl.when(self.spot[0] != 0)(lambda: act(copies[2]))

    def start(self, pieces, step):
        for piece in pieces:
            self.own(piece, step, lambda copy: copy.start())

    def relay(self, pieces, step):
        for piece in pieces:
            if self.lined(piece, step):
                self.copies(piece, step, (2,))[0].wait_recv()
                for here in (1, 2):
                    copy = self.passed(piece, step, here)
                    pl.when(self.spot[0] == here)(copy.start)

    def arrive(self, pieces, step):
        for piece in pieces:
            for copy in self.copies(piece, step, (1, 3) if self.lined(piece, step) else None):
                copy.wait_recv()

    def drain(self, pieces):
        for piece in pieces:
            for step in range(3):
                self.own(piece, step, lambda copy: copy.wait_send())
                if self.lined(piece, step):
                    for here in (1, 2):
                        copy = self.passed(piece, step, here)
                        pl.when(self.spot[0] == here)(copy.wait_send)


def greet(dims, spot, team, member):
    barrier = pltpu.get_barrier_semaphore()
    count = 0
    for axis in range(3):
        for offset in range(1, dims[axis]):
            peer = list(spot)
            peer[axis] = lax.rem(spot[axis] + offset, dims[axis])
            pl.semaphore_signal(
                barrier, inc=1, device_id={"dp": flat(peer, dims)}, device_id_type=MESH
            )
            count += 1
    for offset in range(1, team):
        pl.semaphore_signal(
            barrier,
            inc=1,
            device_id={"tensor": lax.rem(member + offset, team)},
            device_id_type=MESH,
        )
        count += 1
    pl.semaphore_wait(barrier, count)


class Plan:
    def __init__(self, chunks):
        self.crossed = [4, chunks - 2] if chunks >= 8 else [max(chunks - 2, 0)]
        self.plain = [k for k in range(chunks) if k not in self.crossed]
        self.top = [[] for _ in range(chunks)]
        self.bottom = [[] for _ in range(chunks)]
        for m, k in enumerate(self.plain):
            self.add(self.top, k, "second", m + 3)
            self.add(self.top, k, "relay", m + 4)
            self.add(self.top, k, "first", m + 6)
            self.add(self.bottom, k, "third", m + 2)
        for m, k in enumerate(self.crossed):
            self.top[1 + m].append(("cross_third", k))
            self.top[k - 1 - m].append(("cross_relay", k))

    def add(self, where, at, step, m):
        if m < len(self.plain):
            where[at].append((step, self.plain[m]))


def forward_kernel(
    shape,
    in_shard_ref,
    out_shard_ref,
    gu_shard_ref,
    down_shard_ref,
    x_own_ref,
    g_own_ref,
    expand_ref,
    down_shrink_ref,
    same_ref,
    conv_gain_ref,
    ffn_gain_ref,
    taps_ref,
    in_reduce_ref,
    in_lift_ref,
    out_reduce_ref,
    out_lift_ref,
    ffn_reduce_ref,
    down_lift_ref,
    mask_ref,
    pick_ref,
    io_whole_ref,
    ff_whole_ref,
    streams_ref,
    norm_one_ref,
    conv_out_ref,
    code_in_ref,
    code_out_ref,
    block_out_ref,
    grad_x_two_ref,
    ffn_flat_ref,
    x_all_ref,
    g_all_ref,
    na_ref,
    nb_ref,
    w_ref,
    acc_a_ref,
    acc_b_ref,
    x_two_ref,
    halo_ref,
    co_ref,
    cp_ref,
    gcf_ref,
    cf_ref,
    gd_ref,
    cft_ref,
    gdt_ref,
    act_ref,
    ggu_ref,
    eb_ref,
    dsb_ref,
    rb_ref,
    rc_ref,
    rd_ref,
    code_t_ref,
    flat_ref,
    rep_ref,
    got_ref,
    send_ref,
    recv_ref,
    team_send_ref,
    team_recv_ref,
    local_ref,
    load_sem_ref,
):
    dims, team, width, channels, length, chunks, early = shape
    own = length // team
    hc = HIDDEN_CHUNK
    tile = ROW_TILE
    tiles = length // tile
    own_tile = min(own, tile)
    per_own = own // tile
    member = lax.axis_index("tensor")
    spot = position(lax.axis_index("dp"), dims)
    gather = Gather(dims, spot, send_ref, recv_ref)
    own_rows = pl.ds(pl.multiple_of(member * own, own), own)
    plan = Plan(chunks)

    io_step = 4 * channels // 6
    half = io_step // 2
    io_pieces = [
        [
            (io_whole_ref, pl.ds(i * io_step, half), (0, 1, 2), 2 * i, False),
            (io_whole_ref, pl.ds(i * io_step + half, half), (0, 2, 1), 2 * i + 1, False),
        ]
        for i in range(6)
    ]
    cut = 640

    def chunk_pieces(k):
        orders = ((1, 2, 0), (2, 1, 0)) if k in plan.crossed else ((0, 1, 2), (0, 2, 1))
        whole = ff_whole_ref.at[k]
        return [
            (whole, pl.ds(0, cut), orders[0], 12 + 2 * k, True),
            (whole, pl.ds(cut, 3 * hc - cut), orders[1], 13 + 2 * k, True),
        ]

    def do(step, k):
        pieces = chunk_pieces(k)
        if step == "first" or step == "cross_first":
            gather.start(pieces, 0)
        elif step == "relay":
            gather.relay(pieces, 0)
        elif step == "second" or step == "cross_second":
            gather.arrive(pieces, 0)
            gather.start(pieces, 1)
        elif step == "third" or step == "cross_third":
            gather.arrive(pieces, 1)
            gather.start(pieces, 2)
        elif step == "cross_relay":
            gather.relay(pieces, 2)
        elif step == "last":
            gather.arrive(pieces, 2)

    def do_plain(step, m):
        if m < len(plan.plain):
            do(step, plan.plain[m])

    def team_copies(row, source, target):
        out = []
        for offset in range(1, team):
            peer = lax.rem(member + offset, team)
            out.append(
                pltpu.make_async_remote_copy(
                    src_ref=source(peer, offset),
                    dst_ref=target(peer, offset),
                    send_sem=team_send_ref.at[row, offset - 1],
                    recv_sem=team_recv_ref.at[row, offset - 1],
                    device_id={"tensor": peer},
                    device_id_type=MESH,
                )
            )
        return out

    def rows_of(ref):
        return lambda peer, offset: ref.at[pl.ds(pl.multiple_of(peer * own, own), own)]

    def slot_of(ref):
        return lambda peer, offset: ref.at[offset - 1]

    def spare(k):
        at = position(1 + k // 2, dims)
        return lambda first, amount: w_ref.at[at + (slice(None), pl.ds((k % 2) * 3 * hc + first, amount))]

    io_spare = w_ref.at[0, 0, 0, :, pl.ds(0, 4 * channels)]
    ins = [
        [
            pltpu.make_async_copy(
                in_shard_ref, w_ref.at[0, 0, 0, :, pl.ds(0, 3 * channels)], local_ref.at[2]
            ),
            pltpu.make_async_copy(
                out_shard_ref, w_ref.at[0, 0, 0, :, pl.ds(3 * channels, channels)], local_ref.at[3]
            ),
        ]
    ]
    outs = [pltpu.make_async_copy(io_spare, io_whole_ref.at[spot], local_ref.at[2])]
    for k in range(chunks):
        part = pl.ds(k * hc, hc)
        sources = (gu_shard_ref.at[0, :, part], gu_shard_ref.at[1, :, part], down_shard_ref.at[:, part])
        ins.append(
            [
                pltpu.make_async_copy(source, spare(k)(n * hc, hc), local_ref.at[4 + 3 * k + n])
                for n, source in enumerate(sources)
            ]
        )
        outs.append(
            pltpu.make_async_copy(
                spare(k)(0, 3 * hc), ff_whole_ref.at[(k,) + spot], local_ref.at[4 + 3 * k]
            )
        )
    for copies in ins:
        for copy in copies:
            copy.start()
    greet(dims, spot, team, member)
    x_copies = team_copies(0, lambda p, o: x_own_ref, lambda p, o: x_all_ref.at[own_rows])
    g_copies = team_copies(1, lambda p, o: g_own_ref, lambda p, o: g_all_ref.at[own_rows])
    for copy in x_copies + g_copies:
        copy.start()
    x_here = pltpu.make_async_copy(x_own_ref, x_all_ref.at[own_rows], local_ref.at[0])
    g_here = pltpu.make_async_copy(g_own_ref, g_all_ref.at[own_rows], local_ref.at[1])
    for first, second in zip(ins, outs):
        for copy in first:
            copy.wait()
        second.start()
    x_here.start()
    g_here.start()
    outs[0].wait()
    for pieces in io_pieces:
        gather.start(pieces, 0)
    for copy in outs[1:]:
        copy.wait()
    for k in plan.crossed:
        do("cross_first", k)
    do_plain("first", 0)
    do_plain("first", 1)

    x_here.wait()
    for copy in x_copies:
        copy.wait_recv()

    def first_norm(i, carry):
        rows = pl.ds(pl.multiple_of(i * tile, tile), tile)
        values = x_all_ref[rows, :].astype(jnp.float32)
        na_ref[rows, :] = (values * norm_factor(values) * conv_gain_ref[...]).astype(jnp.bfloat16)
        return carry

    def down_codes(i, carry):
        rows = pl.ds(pl.multiple_of(i * tile, tile), tile)
        code = dot_against(g_all_ref[rows, :], down_lift_ref[...]) * mask_ref[...]
        code = code.astype(jnp.bfloat16)
        gd_ref[rows, :] = code
        gdt_ref[:, rows] = dot_against(pick_ref[...], code).astype(jnp.bfloat16)
        return carry

    norm_store = pltpu.make_async_copy(na_ref, norm_one_ref, local_ref.at[0])
    for i in range(7):
        if i == 0:
            lax.fori_loop(0, tiles, first_norm, 0)
            norm_store.start()
            for k in plan.crossed:
                do("cross_second", k)
        if i == 1:
            g_here.wait()
            for copy in g_copies:
                copy.wait_recv()
            lax.fori_loop(0, tiles, down_codes, 0)
        if i < 6:
            gather.arrive(io_pieces[i], 0)
            gather.start(io_pieces[i], 1)
        if i > 0:
            gather.arrive(io_pieces[i - 1], 1)
            gather.start(io_pieces[i - 1], 2)
    do_plain("relay", 0)
    do_plain("relay", 1)
    do_plain("first", 2)
    do_plain("second", 0)
    io_loads = []
    for i in range(6):
        gather.arrive(io_pieces[i], 2)
        columns = pl.ds(i * io_step, io_step)
        load = pltpu.make_async_copy(
            io_whole_ref.at[:, :, :, :, columns], w_ref.at[:, :, :, :, columns], load_sem_ref.at[i]
        )
        load.start()
        io_loads.append(load)
    do_plain("second", 1)
    do_plain("first", 3)
    norm_store.wait()
    for load in io_loads:
        load.wait()

    def weights(first, count):
        return w_ref[:, :, :, :, pl.ds(first, count)].reshape(width, count)

    halo_ref[pl.ds(0, 8), :] = jnp.zeros((8, channels), jnp.float32)

    def convolve(i, carry):
        rows = pl.ds(pl.multiple_of(i * tile, tile), tile)
        normed = na_ref[rows, :]
        code = (dot(normed, in_reduce_ref[...]) * mask_ref[...]).astype(jnp.bfloat16)
        code_in_ref[:, rows] = dot_against(pick_ref[...], code).astype(jnp.bfloat16)
        lanes = []
        for lane in range(3):
            value = dot(normed, weights(lane * channels, channels)) + dot(
                code, in_lift_ref[:, pl.ds(lane * channels, channels)]
            )
            lanes.append(value)
            if lane < 2:
                acc_a_ref[rows, pl.ds(lane * channels, channels)] = value
            else:
                acc_b_ref[rows, pl.ds(0, channels)] = value
        product = lanes[0] * lanes[2]
        halo_ref[pl.ds(8, tile), :] = product
        masks = same_ref[rows, :]
        taps = taps_ref[...].astype(jnp.float32)
        mixed = (
            taps[0:1, :] * product
            + taps[1:2, :] * halo_ref[pl.ds(7, tile), :] * masks[:, 0:1]
            + taps[2:3, :] * halo_ref[pl.ds(6, tile), :] * masks[:, 1:2]
        )
        halo_ref[pl.ds(0, 8), :] = halo_ref[pl.ds(tile, 8), :]
        convolved = (lanes[1] * mixed).astype(jnp.bfloat16)
        co_ref[rows, :] = convolved
        na_ref[rows, :] = dot_against(convolved, weights(3 * channels, channels)).astype(jnp.bfloat16)
        cp_ref[rows, :] = dot(convolved, out_reduce_ref[...])

        @pl.when(i == 1)
        def _():
            do_plain("relay", 2)
            do_plain("third", 0)

        @pl.when(i == 2)
        def _():
            do_plain("first", 4)
            do_plain("second", 2)

        return carry

    lax.fori_loop(0, tiles, convolve, 0)
    stores = [
        pltpu.make_async_copy(acc_a_ref.at[:, pl.ds(0, channels)], streams_ref.at[0], local_ref.at[3]),
        pltpu.make_async_copy(
            acc_a_ref.at[:, pl.ds(channels, channels)], streams_ref.at[1], local_ref.at[4]
        ),
        pltpu.make_async_copy(acc_b_ref.at[:, pl.ds(0, channels)], streams_ref.at[2], local_ref.at[5]),
        pltpu.make_async_copy(co_ref, conv_out_ref, local_ref.at[6]),
    ]
    branch = team_copies(2, rows_of(na_ref), slot_of(rb_ref))
    codes = team_copies(3, rows_of(cp_ref), slot_of(rc_ref))
    for copy in codes + branch + stores:
        copy.start()
    do_plain("relay", 3)
    do_plain("first", 5)
    do_plain("third", 1)

    def load(c):
        slot = lax.rem(c, 2)
        columns = pl.ds(pl.multiple_of(slot * 3 * hc, LANES), 3 * hc)
        part = pl.ds(pl.multiple_of(c * hc, LANES), hc)
        return [
            pltpu.make_async_copy(
                ff_whole_ref.at[c], w_ref.at[:, :, :, :, columns], load_sem_ref.at[3 * slot]
            ),
            pltpu.make_async_copy(
                expand_ref.at[:, :, part], eb_ref.at[slot], load_sem_ref.at[3 * slot + 1]
            ),
            pltpu.make_async_copy(down_shrink_ref.at[part], dsb_ref.at[slot], load_sem_ref.at[3 * slot + 2]),
        ]

    for copy in branch + codes:
        copy.wait_recv()
    code = cp_ref[own_rows, :]
    for peer in range(team - 1):
        code = code + rc_ref[peer]
    code = (code * mask_ref[...]).astype(jnp.bfloat16)
    code_out_ref[...] = dot_against(pick_ref[...], code).astype(jnp.bfloat16)
    cf_ref[pl.ds(0, own), pl.ds(0, LANES)] = code

    def second_norm(i, carry):
        local_rows = pl.ds(pl.multiple_of(i * own_tile, own_tile), own_tile)
        rows = pl.ds(pl.multiple_of(member * own + i * own_tile, own_tile), own_tile)
        values = x_all_ref[rows, :].astype(jnp.float32) + na_ref[rows, :].astype(jnp.float32)
        for peer in range(team - 1):
            values = values + rb_ref[peer, local_rows, :].astype(jnp.float32)
        values = values + dot(cf_ref[local_rows, pl.ds(0, LANES)], out_lift_ref[...])
        x_two_ref[local_rows, :] = values
        nb_ref[rows, :] = (values * norm_factor(values) * ffn_gain_ref[...]).astype(jnp.bfloat16)
        return carry

    lax.fori_loop(0, own // own_tile, second_norm, 0)
    norms = team_copies(4, lambda p, o: nb_ref.at[own_rows], lambda p, o: nb_ref.at[own_rows])
    for copy in norms:
        copy.start()
    do("last", 0)
    for copy in load(0):
        copy.start()
    for copy in stores:
        copy.wait()
    acc_a_ref[...] = jnp.zeros_like(acc_a_ref)
    acc_b_ref[...] = jnp.zeros_like(acc_b_ref)
    for copy in branch + codes:
        copy.wait_send()
    cp_ref[...] = jnp.zeros_like(cp_ref)
    gcf_ref[...] = jnp.zeros_like(gcf_ref)
    for copy in norms:
        copy.wait_recv()

    def ffn_codes(i, carry):
        rows = pl.ds(pl.multiple_of(i * tile, tile), tile)
        value = dot(nb_ref[rows, :], ffn_reduce_ref[...])
        for n in range(2):
            code = (value[:, n * LANES : (n + 1) * LANES] * mask_ref[...]).astype(jnp.bfloat16)
            cf_ref[rows, pl.ds(n * LANES, LANES)] = code
            cft_ref[pl.ds(16 * n, 16), rows] = dot_against(pick_ref[...], code).astype(jnp.bfloat16)
        return carry

    lax.fori_loop(0, tiles, ffn_codes, 0)

    codes = team_copies(7, rows_of(cp_ref), slot_of(rc_ref))
    grads = team_copies(5, rows_of(x_all_ref), slot_of(rd_ref))
    downs = team_copies(6, rows_of(na_ref), slot_of(rb_ref))

    def finish(rows):
        na_ref[rows, :] = acc_a_ref[rows, :].astype(jnp.bfloat16)
        total = acc_b_ref[rows, :]
        for n in range(2):
            lanes = pl.ds(n * LANES, LANES)
            upper, lower = split_pair(gcf_ref[rows, lanes] * mask_ref[...])
            code_t_ref[0, pl.ds(16 * n, 16), rows] = dot_against(pick_ref[...], upper).astype(
                jnp.bfloat16
            )
            code_t_ref[1, pl.ds(16 * n, 16), rows] = dot_against(pick_ref[...], lower).astype(
                jnp.bfloat16
            )
            total = (
                total
                + dot_against(upper, ffn_reduce_ref[:, lanes])
                + dot_against(lower, ffn_reduce_ref[:, lanes])
            )
        acc_b_ref[rows, :] = total
        x_all_ref[rows, :] = total.astype(jnp.bfloat16)

    def chunk(c, carry):
        for k in range(chunks):
            if plan.top[k]:

                @pl.when(c == k)
                def _():
                    for step, which in plan.top[k]:
                        do(step, which)

        for copy in load(c):
            copy.wait()
        slot = lax.rem(c, 2)
        first = pl.multiple_of(slot * 3 * hc, LANES)
        down_first = pl.multiple_of(slot * 3 * hc + 2 * hc, LANES)

        def row_tile(j, inner):
            i = lax.rem((member + 1) * per_own + j, tiles)
            rows = pl.ds(pl.multiple_of(i * tile, tile), tile)
            both = dot(nb_ref[rows, :], weights(first, 2 * hc))
            grad = dot(g_all_ref[rows, :], weights(down_first, hc)) + dot_against(
                gd_ref[rows, :], dsb_ref[slot]
            )
            gate = both[:, :hc] + dot(cf_ref[rows, pl.ds(0, LANES)], eb_ref[slot, 0])
            up = both[:, hc:] + dot(cf_ref[rows, pl.ds(LANES, LANES)], eb_ref[slot, 1])
            gated = jax.nn.sigmoid(gate)
            silu = gate * gated
            act = (silu * up).astype(jnp.bfloat16)
            act_ref[rows, :] = act
            grad_gate = (grad * up * gated * (1.0 + gate * (1.0 - gated))).astype(jnp.bfloat16)
            grad_up = (grad * silu).astype(jnp.bfloat16)
            ggu_ref[rows, pl.ds(0, hc)] = grad_gate
            ggu_ref[rows, pl.ds(hc, hc)] = grad_up
            acc_a_ref[rows, :] += dot_against(act, weights(down_first, hc))
            cp_ref[rows, :] += dot(act, dsb_ref[slot])
            acc_b_ref[rows, :] += dot_against(ggu_ref[rows, :], weights(first, 2 * hc))
            gcf_ref[rows, pl.ds(0, LANES)] += dot_against(grad_gate, eb_ref[slot, 0])
            gcf_ref[rows, pl.ds(LANES, LANES)] += dot_against(grad_up, eb_ref[slot, 1])

            @pl.when(c == chunks - 1)
            def _():
                finish(rows)
                for offset in range(1, team):

                    @pl.when(j == offset * per_own - 1)
                    def _():
                        for copies in (codes, grads, downs):
                            copies[offset - 1].start()

            return inner

        lax.fori_loop(0, tiles, row_tile, 0)
        for k in range(chunks - 1):

            @pl.when(c == k)
            def _():
                for step, which in plan.bottom[k]:
                    do(step, which)
                do("last", k + 1)

        @pl.when(c + 1 < chunks)
        def _():
            for copy in load(c + 1):
                copy.start()

        at = pl.multiple_of(c * hc, LANES)
        padded = chunks * hc
        for n in range(2):
            value = dot(cft_ref[pl.ds(16 * n, 16), :], ggu_ref[:, pl.ds(n * hc, hc)])
            flat_ref[:, pl.ds(n * padded + at, hc)] = value.astype(jnp.bfloat16)
        value = dot(gdt_ref[...], act_ref[...])
        flat_ref[:, pl.ds(2 * padded + at, hc)] = value.astype(jnp.bfloat16)
        return carry

    lax.fori_loop(0, chunks, chunk, 0)

    for copy in codes:
        copy.wait_recv()
    code = cp_ref[own_rows, :]
    for peer in range(team - 1):
        code = code + rc_ref[peer]
    rounded = (code * mask_ref[...]).astype(jnp.bfloat16)
    cf_ref[pl.ds(0, own), pl.ds(0, LANES)] = rounded
    turned = dot_against(pick_ref[...], rounded).astype(jnp.bfloat16)
    shrunk = (dot(code_t_ref[0], nb_ref[...]) + dot(code_t_ref[1], nb_ref[...])).astype(jnp.bfloat16)
    rep_ref[:, pl.ds(0, width)] = shrunk[:16]
    rep_ref[:, pl.ds(width, width)] = shrunk[16:]
    rep_ref[:, pl.ds(2 * width, width)] = dot(turned, g_all_ref[own_rows, :]).astype(jnp.bfloat16)
    share = early.share
    reps = team_copies(
        8,
        lambda p, o: rep_ref.at[:, pl.ds(pl.multiple_of(p * share, LANES), share)],
        slot_of(got_ref),
    )
    for copy in reps:
        copy.start()
    for copy in grads + downs:
        copy.wait_recv()
    for copy in norms + grads + downs:
        copy.wait_send()

    def last_rows(i, carry):
        local_rows = pl.ds(pl.multiple_of(i * own_tile, own_tile), own_tile)
        rows = pl.ds(pl.multiple_of(member * own + i * own_tile, own_tile), own_tile)
        values = x_two_ref[local_rows, :]
        down = acc_a_ref[rows, :]
        grad = acc_b_ref[rows, :]
        for peer in range(team - 1):
            down = down + rb_ref[peer, local_rows, :].astype(jnp.float32)
            grad = grad + rd_ref[peer, local_rows, :].astype(jnp.float32)
        out = values + down + dot(cf_ref[local_rows, pl.ds(0, LANES)], down_lift_ref[...])
        nb_ref[local_rows, :] = out.astype(jnp.bfloat16)
        x_two_ref[local_rows, :] = g_all_ref[rows, :].astype(jnp.float32) + normalize_back(
            values, norm_factor(values), ffn_gain_ref[...], grad
        )
        return carry

    lax.fori_loop(0, own // own_tile, last_rows, 0)
    results = [
        pltpu.make_async_copy(nb_ref.at[pl.ds(0, own)], block_out_ref, local_ref.at[0]),
        pltpu.make_async_copy(x_two_ref, grad_x_two_ref, local_ref.at[1]),
    ]
    for copy in results:
        copy.start()
    for copy in reps:
        copy.wait_recv()
    value = rep_ref[:, pl.ds(pl.multiple_of(member * share, LANES), share)].astype(jnp.float32)
    for peer in range(team - 1):
        value = value + got_ref[peer].astype(jnp.float32)
    flat_ref[:, pl.ds(early.split, share)] = value.astype(jnp.bfloat16)
    rest = flat_ref.shape[1] - early.total
    if rest:
        flat_ref[:, pl.ds(early.total, rest)] = jnp.zeros((16, rest), jnp.bfloat16)
    flat_store = pltpu.make_async_copy(flat_ref, ffn_flat_ref, local_ref.at[2])
    flat_store.start()
    for copy in x_copies + g_copies + codes + reps:
        copy.wait_send()
    for pieces in io_pieces:
        gather.drain(pieces)
    for k in range(chunks):
        gather.drain(chunk_pieces(k))
    for copy in results:
        copy.wait()
    flat_store.wait()


def forward_and_ffn(dims, team, early, operands):
    in_shard, out_shard, gu_shard, down_shard, x_own = operands[:5]
    rows, channels = out_shard.shape
    hc = HIDDEN_CHUNK
    chunks = down_shard.shape[1] // hc
    own, width = x_own.shape
    length = own * team
    count = dims[0] * dims[1] * dims[2]
    columns = max(4 * channels, 6 * hc)
    lanes = sum(d - 1 for d in dims) + 1
    shape = (dims, team, width, channels, length, chunks, early)
    bf16, f32 = jnp.bfloat16, jnp.float32
    anywhere = pl.BlockSpec(memory_space=pl.ANY)
    vmem = pl.BlockSpec(memory_space=pltpu.VMEM)
    outs = [
        (dims + (rows, 4 * channels), bf16, anywhere),
        ((chunks,) + dims + (rows, 3 * hc), bf16, anywhere),
        ((3, length, channels), f32, anywhere),
        ((length, width), bf16, anywhere),
        ((length, channels), bf16, anywhere),
        ((16, length), bf16, vmem),
        ((16, own), bf16, vmem),
        ((own, width), bf16, anywhere),
        ((own, width), f32, anywhere),
        ((16, count * early.block), bf16, anywhere),
    ]
    peers = max(team - 1, 1)
    row_count = 12 + 2 * chunks
    scratch = [
        pltpu.VMEM((length, width), bf16),
        pltpu.VMEM((length, width), bf16),
        pltpu.VMEM((length, width), bf16),
        pltpu.VMEM((length, width), bf16),
        pltpu.VMEM(dims + (rows, columns), bf16),
        pltpu.VMEM((length, width), f32),
        pltpu.VMEM((length, width), f32),
        pltpu.VMEM((own, width), f32),
        pltpu.VMEM((ROW_TILE + 8, channels), f32),
        pltpu.VMEM((length, channels), bf16),
        pltpu.VMEM((length, LANES), f32),
        pltpu.VMEM((length, 2 * LANES), f32),
        pltpu.VMEM((length, 2 * LANES), bf16),
        pltpu.VMEM((length, LANES), bf16),
        pltpu.VMEM((32, length), bf16),
        pltpu.VMEM((16, length), bf16),
        pltpu.VMEM((length, hc), bf16),
        pltpu.VMEM((length, 2 * hc), bf16),
        pltpu.VMEM((2, 2, LANES, hc), bf16),
        pltpu.VMEM((2, hc, LANES), bf16),
        pltpu.VMEM((peers, own, width), bf16),
        pltpu.VMEM((peers, own, LANES), f32),
        pltpu.VMEM((peers, own, width), bf16),
        pltpu.VMEM((2, 32, length), bf16),
        pltpu.VMEM((16, count * early.block), bf16),
        pltpu.VMEM((16, 3 * width), bf16),
        pltpu.VMEM((peers, 16, 3 * width // team), bf16),
        pltpu.SemaphoreType.DMA((row_count, lanes)),
        pltpu.SemaphoreType.DMA((row_count, lanes)),
        pltpu.SemaphoreType.DMA((9, peers)),
        pltpu.SemaphoreType.DMA((9, peers)),
        pltpu.SemaphoreType.DMA((max(4 + 3 * chunks, 8),)),
        pltpu.SemaphoreType.DMA((6,)),
    ]
    return pl.pallas_call(
        functools.partial(forward_kernel, shape),
        out_shape=[jax.ShapeDtypeStruct(o[0], o[1]) for o in outs],
        in_specs=[anywhere] * 8 + [vmem] * 12,
        out_specs=[o[2] for o in outs],
        scratch_shapes=scratch,
        compiler_params=pltpu.CompilerParams(
            collective_id=0, has_side_effects=True, vmem_limit_bytes=67043328
        ),
    )(*operands)


class Share:
    def __init__(self, count, team, split, shared):
        self.split, self.shared, self.share = split, shared, shared // team
        self.total = split + self.share
        self.block = -(-self.total // (LANES * count)) * LANES
        self.first = split // self.block
        self.blocks = -(-self.total // self.block) - self.first


def backward_kernel(
    shape,
    grad_x_two_ref,
    ffn_flat_ref,
    io_whole_ref,
    streams_ref,
    norm_one_ref,
    conv_out_ref,
    x_own_ref,
    code_in_ref,
    code_out_ref,
    same_ref,
    conv_gain_ref,
    taps_ref,
    in_reduce_ref,
    in_lift_ref,
    out_reduce_ref,
    out_lift_ref,
    mask_ref,
    pick_ref,
    grad_residual_ref,
    early_ref,
    late_ref,
    early_rep_ref,
    w_ref,
    gx_ref,
    gb_ref,
    gco_ref,
    gcot_ref,
    st_ref,
    gs_ref,
    gci_ref,
    ha_ref,
    hb_ref,
    halo_ref,
    na_ref,
    co_ref,
    pb_ref,
    gcit_ref,
    xo_ref,
    rb_ref,
    rep_b_ref,
    got_b_ref,
    flat_a_ref,
    flat_b_ref,
    part_a_ref,
    part_b_ref,
    from_a_ref,
    from_b_ref,
    sum_a_ref,
    sum_b_ref,
    spare_a_ref,
    out_ref,
    send_ref,
    recv_ref,
    swap_send_ref,
    swap_recv_ref,
    team_send_ref,
    team_recv_ref,
    local_ref,
):
    dims, team, width, channels, length, early, late = shape
    count = dims[0] * dims[1] * dims[2]
    own = length // team
    tile = ROW_TILE
    tiles = length // tile
    own_tile = min(own, tile)
    member = lax.axis_index("tensor")
    me = lax.axis_index("dp")
    spot = position(me, dims)
    gather = Gather(dims, spot, send_ref, recv_ref)
    own_rows = pl.ds(pl.multiple_of(member * own, own), own)

    def enter():
        barrier = pltpu.get_barrier_semaphore()
        for offset in range(1, count):
            pl.semaphore_signal(
                barrier, inc=1, device_id={"dp": lax.rem(me + offset, count)}, device_id_type=MESH
            )
        for offset in range(1, team):
            pl.semaphore_signal(
                barrier,
                inc=1,
                device_id={"tensor": lax.rem(member + offset, team)},
                device_id_type=MESH,
            )
        pl.semaphore_wait(barrier, count - 1 + team - 1)

    def team_copies(row, source, target):
        out = []
        for offset in range(1, team):
            peer = lax.rem(member + offset, team)
            out.append(
                pltpu.make_async_remote_copy(
                    src_ref=source(peer, offset),
                    dst_ref=target(peer, offset),
                    send_sem=team_send_ref.at[row, offset - 1],
                    recv_sem=team_recv_ref.at[row, offset - 1],
                    device_id={"tensor": peer},
                    device_id_type=MESH,
                )
            )
        return out

    def swap_copies(row, part, landing):
        out = []
        for offset in range(1, count):
            peer = lax.rem(me + offset, count)
            out.append(
                pltpu.make_async_remote_copy(
                    src_ref=part.at[peer],
                    dst_ref=landing.at[me],
                    send_sem=swap_send_ref.at[row, offset - 1],
                    recv_sem=swap_recv_ref.at[row, offset - 1],
                    device_id={"dp": peer},
                    device_id_type=MESH,
                )
            )
        return out

    def pieces_of(share, whole, row):
        out = []
        step = max(share.block // 384, 1) * LANES
        for n, first in enumerate(range(0, share.block, step)):
            order = (0, 1, 2) if n % 2 == 0 else (0, 2, 1)
            out.append((whole, pl.ds(first, min(step, share.block - first)), order, row + n, False))
        return out

    def forward_on(pieces, step):
        for piece in pieces:
            gather.arrive([piece], step)
            gather.start([piece], step + 1)

    def hand_out(share, columns, part, landing, row):
        for peer in range(count):
            part[peer, :, pl.ds(0, share.block)] = columns[:, pl.ds(peer * share.block, share.block)]
            part[peer, :, pl.ds(share.block, LANES)] = pick_ref[...]
        landing[me] = part[me]
        copies = swap_copies(row, part, landing)
        for copy in copies:
            copy.start()
        return copies

    def take_in(share, landing, total):
        marks = landing[:, :, pl.ds(share.block, LANES)].reshape(count * 16, LANES)
        marks = jnp.transpose(marks.astype(jnp.float32)).astype(jnp.bfloat16)
        blocks = landing[:, :, pl.ds(0, share.block)].reshape(count * 16, share.block)
        total[...] = dot(marks, blocks).astype(jnp.bfloat16)

    first_columns, later_columns = pl.ds(0, 3 * channels), pl.ds(3 * channels, channels)
    loads = {}
    for slot, (name, source, target) in enumerate(
        [
            ("flat", ffn_flat_ref, flat_a_ref),
            ("gx", grad_x_two_ref, gx_ref),
            ("co", conv_out_ref, co_ref),
            ("w", io_whole_ref.at[:, :, :, :, later_columns], w_ref.at[:, :, :, :, later_columns]),
            ("b", streams_ref.at[0], st_ref.at[0, pl.ds(8, length)]),
            ("c", streams_ref.at[1], st_ref.at[1, pl.ds(8, length)]),
            ("x", streams_ref.at[2], st_ref.at[2, pl.ds(8, length)]),
            ("na", norm_one_ref, na_ref),
            ("xo", x_own_ref, xo_ref),
            ("in", io_whole_ref.at[:, :, :, :, first_columns], w_ref.at[:, :, :, :, first_columns]),
        ]
    ):
        loads[name] = pltpu.make_async_copy(source, target, local_ref.at[slot])
        loads[name].start()
    enter()
    loads["flat"].wait()
    sent_a = hand_out(early, flat_a_ref, part_a_ref, from_a_ref, 0)
    st_ref[0, pl.ds(0, 8), :] = jnp.zeros((8, channels), jnp.float32)
    st_ref[2, pl.ds(0, 8), :] = jnp.zeros((8, channels), jnp.float32)
    ha_ref[pl.ds(tile, 8), :] = jnp.zeros((8, channels), jnp.float32)
    hb_ref[pl.ds(tile, 8), :] = jnp.zeros((8, channels), jnp.float32)
    loads["gx"].wait()

    def branch_rows(i, carry):
        local_rows = pl.ds(pl.multiple_of(i * own_tile, own_tile), own_tile)
        rows = pl.ds(pl.multiple_of(member * own + i * own_tile, own_tile), own_tile)
        upper, lower = split_pair(gx_ref[local_rows, :])
        gb_ref[rows, :] = upper
        code = dot_against(upper, out_lift_ref[...]) + dot_against(lower, out_lift_ref[...])
        gco_ref[rows, :] = (code * mask_ref[...]).astype(jnp.bfloat16)
        return carry

    lax.fori_loop(0, own // own_tile, branch_rows, 0)
    swaps = team_copies(0, lambda p, o: gb_ref.at[own_rows], lambda p, o: gb_ref.at[own_rows])
    swaps += team_copies(1, lambda p, o: gco_ref.at[own_rows], lambda p, o: gco_ref.at[own_rows])
    for copy in swaps:
        copy.start()
    upper, lower = split_pair(gx_ref[...])
    rep_b_ref[:, pl.ds(width, width)] = (
        dot(code_out_ref[...], upper) + dot(code_out_ref[...], lower)
    ).astype(jnp.bfloat16)
    for copy in swaps:
        copy.wait_recv()

    def turn(i, carry):
        rows = pl.ds(pl.multiple_of(i * tile, tile), tile)
        gcot_ref[:, rows] = dot_against(pick_ref[...], gco_ref[rows, :]).astype(jnp.bfloat16)
        return carry

    lax.fori_loop(0, tiles, turn, 0)
    loads["co"].wait()
    flat_b_ref[:, pl.ds(3 * channels, channels)] = dot(gcot_ref[...], co_ref[...]).astype(jnp.bfloat16)
    pieces_a = pieces_of(early, early_ref, 0)
    pieces_b = pieces_of(late, late_ref, len(pieces_a))
    place_a = pltpu.make_async_copy(sum_a_ref, early_ref.at[spot], local_ref.at[0])
    place_b = pltpu.make_async_copy(sum_b_ref, late_ref.at[spot], local_ref.at[1])

    for name in ("w", "b", "c", "x"):
        loads[name].wait()

    def weights(first, amount):
        return w_ref[:, :, :, :, pl.ds(first, amount)].reshape(width, amount)

    for copy in sent_a:
        copy.wait_recv()
    take_in(early, from_a_ref, sum_a_ref)
    place_a.start()

    def back(j, carry):
        i = tiles - 1 - j
        start = pl.multiple_of(i * tile, tile)
        rows = pl.ds(start, tile)
        later = pl.ds(pl.multiple_of(start + 8, 8), tile)
        grad = dot(gb_ref[rows, :], weights(3 * channels, channels)) + dot_against(
            gco_ref[rows, :], out_reduce_ref[...]
        )
        halo_ref[pl.ds(0, 8), :] = st_ref[0, pl.ds(start, 8), :] * st_ref[2, pl.ds(start, 8), :]
        product = st_ref[0, later, :] * st_ref[2, later, :]
        halo_ref[pl.ds(8, tile), :] = product
        masks = same_ref[rows, :]
        taps = taps_ref[...].astype(jnp.float32)
        mixed = (
            taps[0:1, :] * product
            + taps[1:2, :] * halo_ref[pl.ds(7, tile), :] * masks[:, 0:1]
            + taps[2:3, :] * halo_ref[pl.ds(6, tile), :] * masks[:, 1:2]
        )
        grad_mixed = grad * st_ref[1, later, :]
        ha_ref[pl.ds(0, tile), :] = taps[1:2, :] * grad_mixed * masks[:, 0:1]
        hb_ref[pl.ds(0, tile), :] = taps[2:3, :] * grad_mixed * masks[:, 1:2]
        grad_product = taps[0:1, :] * grad_mixed + ha_ref[pl.ds(1, tile), :] + hb_ref[pl.ds(2, tile), :]
        ha_ref[pl.ds(tile, 8), :] = ha_ref[pl.ds(0, 8), :]
        hb_ref[pl.ds(tile, 8), :] = hb_ref[pl.ds(0, 8), :]
        gs_ref[rows, pl.ds(0, channels)] = (grad_product * st_ref[2, later, :]).astype(jnp.bfloat16)
        gs_ref[rows, pl.ds(channels, channels)] = (grad * mixed).astype(jnp.bfloat16)
        gs_ref[rows, pl.ds(2 * channels, channels)] = (grad_product * st_ref[0, later, :]).astype(
            jnp.bfloat16
        )
        upper, lower = split_pair(dot_against(gs_ref[rows, :], in_lift_ref[...]) * mask_ref[...])
        gci_ref[0, rows, :] = upper
        gci_ref[1, rows, :] = lower
        gcit_ref[0, :, rows] = dot_against(pick_ref[...], upper).astype(jnp.bfloat16)
        gcit_ref[1, :, rows] = dot_against(pick_ref[...], lower).astype(jnp.bfloat16)

        @pl.when(j == 0)
        def _():
            place_a.wait()
            gather.start(pieces_a, 0)

        for n in (2, 3):

            @pl.when(j == n)
            def _():
                forward_on(pieces_a[n - 2 : n - 1], 0)

        return carry

    lax.fori_loop(0, tiles, back, 0)
    loads["na"].wait()
    rep_b_ref[:, pl.ds(0, width)] = (
        dot(gcit_ref[0], na_ref[...]) + dot(gcit_ref[1], na_ref[...])
    ).astype(jnp.bfloat16)
    more = team_copies(2, lambda p, o: rep_b_ref, lambda p, o: got_b_ref.at[o - 1])
    for copy in more:
        copy.start()
    forward_on(pieces_a[2:3], 0)
    flat_b_ref[:, pl.ds(0, 3 * channels)] = dot(code_in_ref[...], gs_ref[...]).astype(jnp.bfloat16)
    for copy in more:
        copy.wait_recv()
    value = rep_b_ref[...].astype(jnp.float32)
    for peer in range(team - 1):
        value = value + got_b_ref[peer].astype(jnp.float32)
    flat_b_ref[:, pl.ds(late.split, 2 * width)] = value.astype(jnp.bfloat16)
    rest = count * late.block - late.total
    if rest:
        flat_b_ref[:, pl.ds(late.total, rest)] = jnp.zeros((16, rest), jnp.bfloat16)
    sent_b = hand_out(late, flat_b_ref, part_b_ref, from_b_ref, 1)
    forward_on(pieces_a[:1], 1)
    loads["in"].wait()
    grads = team_copies(
        6,
        lambda p, o: pb_ref.at[pl.ds(pl.multiple_of(p * own, own), own)],
        lambda p, o: rb_ref.at[o - 1],
    )
    per_own = own // tile

    def norm_grads(j, carry):
        i = lax.rem((member + 1) * per_own + j, tiles)
        rows = pl.ds(pl.multiple_of(i * tile, tile), tile)
        pb_ref[rows, :] = (
            dot_against(gs_ref[rows, :], weights(0, 3 * channels))
            + dot_against(gci_ref[0, rows, :], in_reduce_ref[...])
            + dot_against(gci_ref[1, rows, :], in_reduce_ref[...])
        ).astype(jnp.bfloat16)
        for offset in range(1, team):

            @pl.when(j == offset * per_own - 1)
            def _():
                grads[offset - 1].start()

        @pl.when(j == 0)
        def _():
            forward_on(pieces_a[3:], 0)
            forward_on(pieces_a[1:2], 1)

        @pl.when(j == 1)
        def _():
            for copy in sent_b:
                copy.wait_recv()
            take_in(late, from_b_ref, sum_b_ref)
            place_b.start()

        @pl.when(j == 2)
        def _():
            place_b.wait()
            gather.start(pieces_b, 0)
            forward_on(pieces_a[2:3], 1)

        return carry

    lax.fori_loop(0, tiles, norm_grads, 0)
    loads["xo"].wait()
    forward_on(pieces_a[3:], 1)
    forward_on(pieces_b, 0)
    for copy in grads:
        copy.wait_recv()

    def residual_rows(i, carry):
        local_rows = pl.ds(pl.multiple_of(i * own_tile, own_tile), own_tile)
        rows = pl.ds(pl.multiple_of(member * own + i * own_tile, own_tile), own_tile)
        values = xo_ref[local_rows, :].astype(jnp.float32)
        grad = pb_ref[rows, :].astype(jnp.float32)
        for peer in range(team - 1):
            grad = grad + rb_ref[peer, local_rows, :].astype(jnp.float32)
        out_ref[local_rows, :] = (
            gx_ref[local_rows, :]
            + normalize_back(values, norm_factor(values), conv_gain_ref[...], grad)
        ).astype(jnp.bfloat16)
        return carry

    lax.fori_loop(0, own // own_tile, residual_rows, 0)
    result = pltpu.make_async_copy(out_ref, grad_residual_ref, local_ref.at[2])
    result.start()

    def pass_on(share, whole, reps, spare, base):
        lifts = []
        for block in range(share.blocks):
            here = whole.at[position(share.first + block, dims)]
            lifts.append(pltpu.make_async_copy(here, spare.at[block], local_ref.at[3 + block]))
        for lift in lifts:
            lift.start()
        for lift in lifts:
            lift.wait()
        out = team_copies(base, lambda p, o: spare, lambda p, o: reps.at[member])
        for copy in out:
            copy.start()
        keep = pltpu.make_async_copy(spare, reps.at[member], local_ref.at[3])
        keep.start()
        return out, keep

    forward_on(pieces_b, 1)
    gather.arrive(pieces_a, 2)
    out_a, keep_a = pass_on(early, early_ref, early_rep_ref, spare_a_ref, 4)
    gather.arrive(pieces_b, 2)
    for copy in out_a:
        copy.wait_recv()
    for copy in out_a + swaps + grads + more + sent_a + sent_b:
        copy.wait_send()
    gather.drain(pieces_a + pieces_b)
    keep_a.wait()
    result.wait()


def backward(dims, team, early, late, operands):
    _, _, io_whole, _, _, conv_out, x_own = operands[:7]
    count = dims[0] * dims[1] * dims[2]
    own, width = x_own.shape
    length, channels = conv_out.shape
    lanes = sum(d - 1 for d in dims)
    bf16, f32 = jnp.bfloat16, jnp.float32
    anywhere = pl.BlockSpec(memory_space=pl.ANY)
    vmem = pl.BlockSpec(memory_space=pltpu.VMEM)
    rows = ADAPTER_COUNT * 16
    peers = max(team - 1, 1)
    outs = [
        ((own, width), bf16),
        (dims + (rows, early.block), bf16),
        (dims + (rows, late.block), bf16),
        ((team, early.blocks, rows, early.block), bf16),
    ]
    scratch = [
        pltpu.VMEM(io_whole.shape, bf16),
        pltpu.VMEM((own, width), f32),
        pltpu.VMEM((length, width), bf16),
        pltpu.VMEM((length, LANES), bf16),
        pltpu.VMEM((16, length), bf16),
        pltpu.VMEM((3, length + 8, channels), f32),
        pltpu.VMEM((length, 3 * channels), bf16),
        pltpu.VMEM((2, length, LANES), bf16),
        pltpu.VMEM((ROW_TILE + 8, channels), f32),
        pltpu.VMEM((ROW_TILE + 8, channels), f32),
        pltpu.VMEM((ROW_TILE + 8, channels), f32),
        pltpu.VMEM((length, width), bf16),
        pltpu.VMEM((length, channels), bf16),
        pltpu.VMEM((length, width), bf16),
        pltpu.VMEM((2, 16, length), bf16),
        pltpu.VMEM((own, width), bf16),
        pltpu.VMEM((peers, own, width), bf16),
        pltpu.VMEM((16, 2 * width), bf16),
        pltpu.VMEM((peers, 16, 2 * width), bf16),
        pltpu.VMEM((16, count * early.block), bf16),
        pltpu.VMEM((16, count * late.block), bf16),
        pltpu.VMEM((count, 16, early.block + LANES), bf16),
        pltpu.VMEM((count, 16, late.block + LANES), bf16),
        pltpu.VMEM((count, 16, early.block + LANES), bf16),
        pltpu.VMEM((count, 16, late.block + LANES), bf16),
        pltpu.VMEM((rows, early.block), bf16),
        pltpu.VMEM((rows, late.block), bf16),
        pltpu.VMEM((early.blocks, rows, early.block), bf16),
        pltpu.VMEM((own, width), bf16),
        pltpu.SemaphoreType.DMA((12, lanes)),
        pltpu.SemaphoreType.DMA((12, lanes)),
        pltpu.SemaphoreType.DMA((2, count - 1)),
        pltpu.SemaphoreType.DMA((2, count - 1)),
        pltpu.SemaphoreType.DMA((7, peers)),
        pltpu.SemaphoreType.DMA((7, peers)),
        pltpu.SemaphoreType.DMA((max(10, 3 + early.blocks),)),
    ]
    return pl.pallas_call(
        functools.partial(backward_kernel, (dims, team, width, channels, length, early, late)),
        out_shape=[jax.ShapeDtypeStruct(*o) for o in outs],
        in_specs=[anywhere] * 7 + [vmem] * (len(operands) - 7),
        out_specs=[anywhere] * 4,
        scratch_shapes=scratch,
        compiler_params=pltpu.CompilerParams(
            collective_id=1, has_side_effects=True, vmem_limit_bytes=67043328
        ),
    )(*operands)


def lagged_segments(segment_ids, lag):
    shifted = jnp.pad(segment_ids, ((0, 0), (lag, 0)), constant_values=-1)[
        :, : segment_ids.shape[1]
    ]
    return (segment_ids == shifted).astype(jnp.float32)


def pad_axis(values, axis, size):
    widths = [(0, 0)] * values.ndim
    widths[axis] = (0, size - values.shape[axis])
    return jnp.pad(values, widths)


def per_device(
    residual,
    cotangent,
    segment_ids,
    adapter_ids,
    conv_gain,
    proj_in,
    conv_taps,
    proj_out,
    ffn_gain,
    gate_up,
    proj_down,
    in_shrink,
    input_lift_weight,
    output_reduce_weight,
    output_lift_weight,
    ffn_reduce_weight,
    ffn_expand,
    down_shrink,
    down_lift_weight,
):
    own, width = residual.shape
    length = segment_ids.shape[1]
    team = length // own
    count = lax.axis_size("dp")
    dims = split_ring(count)
    rows, _, channels = proj_in.shape
    hidden = proj_down.shape[1]
    hc = HIDDEN_CHUNK
    chunks = -(-hidden // hc)
    padded = chunks * hc
    adapter = adapter_ids[0]

    in_shard = proj_in.reshape(rows, 3 * channels)
    gu_shard = pad_axis(jnp.transpose(gate_up, (1, 0, 2)), 2, padded)
    down_shard = pad_axis(proj_down, 1, padded)
    codes = ADAPTER_COUNT * ADAPTER_RANK
    in_reduce = in_shrink.reshape(width, codes)
    in_lift = input_lift_weight.reshape(codes, 3 * channels)
    out_reduce = output_reduce_weight.reshape(channels, codes)
    out_lift = output_lift_weight.reshape(codes, width)
    ffn_reduce = ffn_reduce_weight.reshape(width, 2 * codes)
    expand = pad_axis(ffn_expand.reshape(2, codes, hidden), 2, padded)
    shrink = pad_axis(down_shrink.reshape(hidden, codes), 0, padded)
    down_lift = down_lift_weight.reshape(codes, width)
    lane = jnp.arange(codes, dtype=jnp.int32)[None, :]
    row = jnp.arange(ADAPTER_RANK, dtype=jnp.int32)[:, None]
    mask = (lane // ADAPTER_RANK == adapter).astype(jnp.float32)
    pick = (lane == adapter * ADAPTER_RANK + row).astype(jnp.bfloat16)
    first_same, second_same = lagged_segments(segment_ids, 1)[0], lagged_segments(segment_ids, 2)[0]
    same = jnp.stack([first_same, second_same], axis=1)
    early = Share(count, team, 3 * padded, 3 * width)
    late = Share(count, 1, 4 * channels, 2 * width)
    (
        io_whole,
        _,
        streams,
        norm_one,
        conv_out,
        code_in,
        code_out,
        block_output,
        grad_x_two,
        ffn_flat,
    ) = forward_and_ffn(
        dims,
        team,
        early,
        (
            in_shard,
            proj_out,
            gu_shard,
            down_shard,
            residual,
            cotangent,
            expand,
            shrink,
            same,
            conv_gain.reshape(1, width),
            ffn_gain.reshape(1, width),
            conv_taps,
            in_reduce,
            in_lift,
            out_reduce,
            out_lift,
            ffn_reduce,
            down_lift,
            mask,
            pick,
        ),
    )
    grad_residual, early_sums, late_sums, early_shared = backward(
        dims,
        team,
        early,
        late,
        (
            grad_x_two,
            ffn_flat,
            io_whole,
            streams,
            norm_one,
            conv_out,
            residual,
            code_in,
            code_out,
            same,
            conv_gain.reshape(1, width),
            conv_taps,
            in_reduce,
            in_lift,
            out_reduce,
            out_lift,
            mask,
            pick,
        ),
    )

    def columns_of(sums, share):
        sums = sums.reshape(count, ADAPTER_COUNT, ADAPTER_RANK, share.block)
        return jnp.transpose(sums, (1, 2, 0, 3)).reshape(
            ADAPTER_COUNT, ADAPTER_RANK, count * share.block
        )

    def shared_columns(sums, share):
        sums = sums.reshape(team, share.blocks, ADAPTER_COUNT, ADAPTER_RANK, share.block)
        sums = jnp.transpose(sums, (2, 3, 0, 1, 4)).reshape(
            ADAPTER_COUNT, ADAPTER_RANK, team, share.blocks * share.block
        )
        skip = share.split - share.first * share.block
        return sums[..., skip : skip + share.share]

    def joined(values):
        return values.reshape(ADAPTER_COUNT, ADAPTER_RANK, team * values.shape[-1])

    def rows_first(values):
        return jnp.transpose(values, (2, 0, 1)).astype(jnp.float32)

    early_columns, late_columns = columns_of(early_sums, early), columns_of(late_sums, late)
    early_rest = joined(shared_columns(early_shared, early))
    ffn_e = jnp.stack([early_columns[..., :hidden], early_columns[..., padded : padded + hidden]])
    ffn_e = ffn_e.astype(jnp.float32)
    down_s = rows_first(early_columns[..., 2 * padded : 2 * padded + hidden])
    ffn_s = jnp.stack(
        [rows_first(early_rest[..., :width]), rows_first(early_rest[..., width : 2 * width])],
        axis=1,
    )
    down_e = early_rest[..., 2 * width :].astype(jnp.float32)
    in_e = late_columns[..., : 3 * channels].astype(jnp.float32)
    in_e = in_e.reshape(ADAPTER_COUNT, ADAPTER_RANK, 3, channels)
    out_s = rows_first(late_columns[..., 3 * channels : 4 * channels])
    in_s = rows_first(late_columns[..., 4 * channels : 4 * channels + width])
    out_e = late_columns[..., 4 * channels + width : 4 * channels + 2 * width].astype(jnp.float32)
    return (block_output, grad_residual, in_s, in_e, out_s, out_e, ffn_s, ffn_e, down_s, down_e)


def solution(mesh):
    rows = P(("dp", "tensor"), None)
    placed = (
        rows,
        rows,
        P("dp", None),
        P("dp"),
        P(),
        P("dp", None, "tensor"),
        P(None, "tensor"),
        P("dp", "tensor"),
        P(),
        P("dp", None, "tensor"),
        P("dp", "tensor"),
        P(),
        P(None, None, None, "tensor"),
        P("tensor", None, None),
        P(),
        P(),
        P(None, None, None, "tensor"),
        P("tensor", None, None),
        P(),
    )
    return jax.shard_map(
        per_device,
        mesh=mesh,
        in_specs=placed,
        out_specs=(
            rows,
            rows,
            P(),
            P(None, None, None, "tensor"),
            P("tensor", None, None),
            P(),
            P(),
            P(None, None, None, "tensor"),
            P("tensor", None, None),
            P(),
        ),
        check_vma=False,
    )
```

time: 498 us -> 472 us (0.948)
  Pallas kernels: 457 us -> 434 us
    pallas_call x1, Pallas kernels: 367 us -> 353 us  [forward_and_ffn(): pl.pallas_call(functools.partial(forward_kernel, shape), out_shape=[jax.S...]
    pallas_call x1, Pallas kernels: 89.8 us -> 81.6 us  [backward(): pl.pallas_call(functools.partial(backward_kernel, (dims, team, width, cha...]
    unnamed x32 -> x24, local copies, waits for them, and re-layouts: 10.1 us -> 8.46 us
where the time goes in v4:
time: 472 us; the launch traced here: 471 us
  Pallas kernels  434 us (92%)
  local copies, waits for them, and re-layouts  24.7 us (5%)
  other arithmetic  10 us (2%)
    pallas_call x1, Pallas kernels, forward_and_ffn(): pl.pallas_call(functools.partial(forward_kernel, shape), out_shape=[jax.S...  353 us
    pallas_call x1, Pallas kernels, backward(): pl.pallas_call(functools.partial(backward_kernel, (dims, team, width, cha...  81.6 us

profile of v4, /device:TPU:0, one launch (start us, length us, event | category | flops | bytes accessed | tf_op | source)
XLA Modules:
  0.0 470.5 jit_solution(15680403031635746283)
XLA Ops:
  0.6 0.0 copy-start.7
  0.7 0.0 copy-start.8
  1.4 0.5 compare_convert_fusion.mask_ref
  1.9 0.7 fusion.pick_ref
  2.6 1.3 reshape.155.conv_gain_ref
  3.9 1.3 reshape.156.ffn_gain_ref
  5.2 0.9 compare_bitcast_fusion.1
  6.1 0.3 copy.71
  6.4 1.7 copy.75.out_reduce_ref
  8.1 0.8 stack.29.same_ref
  9.0 1.9 copy.74.in_reduce_ref
  10.9 0.0 copy-done.8
  10.9 0.8 copy.85
  11.7 0.0 copy-start.6
  11.7 0.0 copy-done.7
  11.7 0.4 copy.72
  12.1 0.0 copy-start.5
  12.1 0.9 copy.89
  13.0 0.0 copy-done.6
  13.0 0.0 copy-start.4
  13.0 1.2 copy.76.ffn_reduce_ref
  14.1 0.0 copy-done.5
  14.1 1.3 copy.73.down_shrink_ref
  15.4 0.0 copy-done.4
  15.4 1.2 copy.94
  16.6 352.7 %shard_map.258 = (bf16[4,2,2,96,3072]{4,3,2,1,0:T(8,128)(2,1)}, bf16[9,4,2,2,96,1152]{5,4,3,2,1,0:T(8,128)(2,1)}, f32[3,1024,768]{2,1,0:T(8,128)}, bf16[1024,153...) custom-call(bf16[96,2304]{1,0:T(8,128)(2,1)} %bitcast.77, ...), custom_call_target="tpu_custom_call" | custom-call | tf_op jit(solution)/shard_map/pallas_call | solution.py:803
  369.3 81.6 %shard_map.259 = (bf16[512,1536]{1,0:T(8,128)(2,1)}, bf16[4,2,2,128,896]{4,3,2,1,0:T(8,128)(2,1)}, bf16[4,2,2,128,384]{4,3,2,1,0:T(8,128)(2,1)}, bf16[2,4,128,896]{3,2,1,0:T(8,128)(2,1)}) custom-call(f32[512,1536]{1,0:T(8,128)} %get-tuple-element.24.grad_x_two_ref, bf16[16,14336]{1,0:T(8,128)(2,1)} %get-tuple-element.25.ffn_flat_ref, ...), custom_call_target="tpu_custom_call" | custom-call | tf_op jit(solution)/shard_map/pallas_call | solution.py:1264
  451.0 1.6 copy.86
  452.6 0.8 convert_bitcast_fusion.2
  453.4 0.1 slice_convert_fusion
  453.5 0.0 copy-start.1
  453.5 1.1 copy.95
  454.6 0.8 copy-done.1
  455.4 1.4 copy.93
  456.8 1.6 reshape.168
  458.5 1.3 slice_bitcast_fusion
  459.8 0.1 copy.87
  459.9 0.0 copy-start
  459.9 1.5 slice_convert_fusion.1
  461.4 1.2 maximum_convert_fusion.1
  462.6 0.7 copy-done
  463.4 0.5 copy.88
  463.9 1.5 convert_bitcast_fusion
  465.4 0.0 copy-start.2
  465.4 2.0 maximum_convert_fusion
  467.4 0.0 copy-done.2
  467.4 0.0 copy-start.3
  467.4 1.1 copy.99
  468.6 0.8 copy-done.3
  469.4 1.1 copy.100
  (2 shorter events, 0.0 us)
Async XLA Ops:
  0.6 11.0 %copy-start.7 = (bf16[8,16,3,768]{3,1,2,0:T(8,128)(2,1)S(1)}, bf16[8,16,3,768]{3,1,2,0:T(8,128)(2,1)}, u32[]{:S(2)}) copy-start(bf16[8,16,3,768]{3,1,2,0:T(8,128)(2,1)} %param.31) | copy-start | bytes 1769476
  0.7 10.2 %copy-start.8 = (bf16[96,3,768]{2,0,1:T(8,128)(2,1)S(1)}, bf16[96,3,768]{2,0,1:T(8,128)(2,1)}, u32[]{:S(2)}) copy-start(bf16[96,3,768]{2,0,1:T(8,128)(2,1)} %param.24) | copy-start | bytes 1327108
  11.7 1.3 copy-start.6
  12.1 2.0 copy-start.5
  13.0 2.5 copy-start.4
  453.5 1.9 copy-start.1
  459.9 3.5 copy-start
  465.4 2.0 copy-start.2
  467.4 2.0 copy-start.3

commit v5 on v4

--- a/solution.py
+++ b/solution.py
@@ -212,7 +212,8 @@
     mask_ref,
     pick_ref,
     io_whole_ref,
-    ff_whole_ref,
+    ff_left_ref,
+    ff_right_ref,
     streams_ref,
     norm_one_ref,
     conv_out_ref,
@@ -270,21 +271,24 @@
 
     io_step = 4 * channels // 6
     half = io_step // 2
-    io_pieces = [
-        [
-            (io_whole_ref, pl.ds(i * io_step, half), (0, 1, 2), 2 * i, False),
-            (io_whole_ref, pl.ds(i * io_step + half, half), (0, 2, 1), 2 * i + 1, False),
-        ]
-        for i in range(6)
-    ]
-    cut = 640
+    every = pl.ds(0, half)
+    io_pieces = []
+    for i in range(6):
+        orders = ((0, 1, 2), (0, 2, 1)) if i < 5 else ((1, 2, 0), (2, 1, 0))
+        io_pieces.append(
+            [
+                (io_whole_ref.at[2 * i], every, orders[0], 2 * i, i > 1),
+                (io_whole_ref.at[2 * i + 1], every, orders[1], 2 * i + 1, i > 1),
+            ]
+        )
+    io_crossed = io_pieces[5]
+    cut = ff_left_ref.shape[-1]
 
     def chunk_pieces(k):
         orders = ((1, 2, 0), (2, 1, 0)) if k in plan.crossed else ((0, 1, 2), (0, 2, 1))
-        whole = ff_whole_ref.at[k]
         return [
-            (whole, pl.ds(0, cut), orders[0], 12 + 2 * k, True),
-            (whole, pl.ds(cut, 3 * hc - cut), orders[1], 13 + 2 * k, True),
+            (ff_left_ref.at[k], pl.ds(0, cut), orders[0], 12 + 2 * k, True),
+            (ff_right_ref.at[k], pl.ds(0, 3 * hc - cut), orders[1], 13 + 2 * k, True),
         ]
 
     def do(step, k):
@@ -334,7 +338,6 @@
         at = position(1 + k // 2, dims)
         return lambda first, amount: w_ref.at[at + (slice(None), pl.ds((k % 2) * 3 * hc + first, amount))]
 
-    io_spare = w_ref.at[0, 0, 0, :, pl.ds(0, 4 * channels)]
     ins = [
         [
             pltpu.make_async_copy(
@@ -345,7 +348,16 @@
             ),
         ]
     ]
-    outs = [pltpu.make_async_copy(io_spare, io_whole_ref.at[spot], local_ref.at[2])]
+    outs = [
+        [
+            pltpu.make_async_copy(
+                w_ref.at[0, 0, 0, :, pl.ds(i * half, half)],
+                io_whole_ref.at[(i,) + spot],
+                local_ref.at[4 + 3 * chunks + i],
+            )
+            for i in range(12)
+        ]
+    ]
     for k in range(chunks):
         part = pl.ds(k * hc, hc)
         sources = (gu_shard_ref.at[0, :, part], gu_shard_ref.at[1, :, part], down_shard_ref.at[:, part])
@@ -356,9 +368,16 @@
             ]
         )
         outs.append(
-            pltpu.make_async_copy(
-                spare(k)(0, 3 * hc), ff_whole_ref.at[(k,) + spot], local_ref.at[4 + 3 * k]
-            )
+            [
+                pltpu.make_async_copy(
+                    spare(k)(0, cut), ff_left_ref.at[(k,) + spot], local_ref.at[4 + 3 * k]
+                ),
+                pltpu.make_async_copy(
+                    spare(k)(cut, 3 * hc - cut),
+                    ff_right_ref.at[(k,) + spot],
+                    local_ref.at[5 + 3 * k],
+                ),
+            ]
         )
     for copies in ins:
         for copy in copies:
@@ -373,18 +392,19 @@
     for first, second in zip(ins, outs):
         for copy in first:
             copy.wait()
-        second.start()
+        for copy in second:
+            copy.start()
     x_here.start()
     g_here.start()
-    outs[0].wait()
-    for pieces in io_pieces:
+    for i, pieces in enumerate(io_pieces):
+        outs[0][2 * i].wait()
+        outs[0][2 * i + 1].wait()
         gather.start(pieces, 0)
-    for copy in outs[1:]:
-        copy.wait()
+    for copies in outs[1:]:
+        for copy in copies:
+            copy.wait()
     for k in plan.crossed:
         do("cross_first", k)
-    do_plain("first", 0)
-    do_plain("first", 1)
 
     x_here.wait()
     for copy in x_copies:
@@ -405,10 +425,12 @@
         return carry
 
     norm_store = pltpu.make_async_copy(na_ref, norm_one_ref, local_ref.at[0])
-    for i in range(7):
+    for i in range(6):
         if i == 0:
             lax.fori_loop(0, tiles, first_norm, 0)
             norm_store.start()
+            gather.arrive(io_crossed, 0)
+            gather.start(io_crossed, 1)
             for k in plan.crossed:
                 do("cross_second", k)
         if i == 1:
@@ -416,12 +438,20 @@
             for copy in g_copies:
                 copy.wait_recv()
             lax.fori_loop(0, tiles, down_codes, 0)
-        if i < 6:
+            gather.arrive(io_crossed, 1)
+            gather.start(io_crossed, 2)
+            do_plain("first", 0)
+            do_plain("first", 1)
+        if i == 5:
+            gather.relay(io_crossed, 2)
+        if i < 5:
             gather.arrive(io_pieces[i], 0)
             gather.start(io_pieces[i], 1)
         if i > 0:
             gather.arrive(io_pieces[i - 1], 1)
             gather.start(io_pieces[i - 1], 2)
+        if 1 <= i < 4:
+            gather.relay(io_pieces[i + 1], 0)
     do_plain("relay", 0)
     do_plain("relay", 1)
     do_plain("first", 2)
@@ -429,12 +459,14 @@
     io_loads = []
     for i in range(6):
         gather.arrive(io_pieces[i], 2)
-        columns = pl.ds(i * io_step, io_step)
-        load = pltpu.make_async_copy(
-            io_whole_ref.at[:, :, :, :, columns], w_ref.at[:, :, :, :, columns], load_sem_ref.at[i]
-        )
-        load.start()
-        io_loads.append(load)
+        for part in (2 * i, 2 * i + 1):
+            load = pltpu.make_async_copy(
+                io_whole_ref.at[part],
+                w_ref.at[:, :, :, :, pl.ds(part * half, half)],
+                load_sem_ref.at[part],
+            )
+            load.start()
+            io_loads.append(load)
     do_plain("second", 1)
     do_plain("first", 3)
     norm_store.wait()
@@ -507,16 +539,18 @@
 
     def load(c):
         slot = lax.rem(c, 2)
-        columns = pl.ds(pl.multiple_of(slot * 3 * hc, LANES), 3 * hc)
+        left = pl.ds(pl.multiple_of(slot * 3 * hc, LANES), cut)
+        right = pl.ds(pl.multiple_of(slot * 3 * hc + cut, LANES), 3 * hc - cut)
         part = pl.ds(pl.multiple_of(c * hc, LANES), hc)
+        pairs = [
+            (ff_left_ref.at[c], w_ref.at[:, :, :, :, left]),
+            (ff_right_ref.at[c], w_ref.at[:, :, :, :, right]),
+            (expand_ref.at[:, :, part], eb_ref.at[slot]),
+            (down_shrink_ref.at[part], dsb_ref.at[slot]),
+        ]
         return [
-            pltpu.make_async_copy(
-                ff_whole_ref.at[c], w_ref.at[:, :, :, :, columns], load_sem_ref.at[3 * slot]
-            ),
-            pltpu.make_async_copy(
-                expand_ref.at[:, :, part], eb_ref.at[slot], load_sem_ref.at[3 * slot + 1]
-            ),
-            pltpu.make_async_copy(down_shrink_ref.at[part], dsb_ref.at[slot], load_sem_ref.at[3 * slot + 2]),
+            pltpu.make_async_copy(source, target, load_sem_ref.at[4 * slot + n])
+            for n, (source, target) in enumerate(pairs)
         ]
 
     for copy in branch + codes:
@@ -752,8 +786,9 @@
     anywhere = pl.BlockSpec(memory_space=pl.ANY)
     vmem = pl.BlockSpec(memory_space=pltpu.VMEM)
     outs = [
-        (dims + (rows, 4 * channels), bf16, anywhere),
-        ((chunks,) + dims + (rows, 3 * hc), bf16, anywhere),
+        ((12,) + dims + (rows, 4 * channels // 12), bf16, anywhere),
+        ((chunks,) + dims + (rows, 640), bf16, anywhere),
+        ((chunks,) + dims + (rows, 3 * hc - 640), bf16, anywhere),
         ((3, length, channels), f32, anywhere),
         ((length, width), bf16, anywhere),
         ((length, channels), bf16, anywhere),
@@ -797,8 +832,8 @@
         pltpu.SemaphoreType.DMA((row_count, lanes)),
         pltpu.SemaphoreType.DMA((9, peers)),
         pltpu.SemaphoreType.DMA((9, peers)),
-        pltpu.SemaphoreType.DMA((max(4 + 3 * chunks, 8),)),
-        pltpu.SemaphoreType.DMA((6,)),
+        pltpu.SemaphoreType.DMA((16 + 3 * chunks,)),
+        pltpu.SemaphoreType.DMA((12,)),
     ]
     return pl.pallas_call(
         functools.partial(forward_kernel, shape),
@@ -881,6 +916,7 @@
     team_send_ref,
     team_recv_ref,
     local_ref,
+    weight_sem_ref,
 ):
     dims, team, width, channels, length, early, late = shape
     count = dims[0] * dims[1] * dims[2]
@@ -970,24 +1006,39 @@
         blocks = landing[:, :, pl.ds(0, share.block)].reshape(count * 16, share.block)
         total[...] = dot(marks, blocks).astype(jnp.bfloat16)
 
-    first_columns, later_columns = pl.ds(0, 3 * channels), pl.ds(3 * channels, channels)
+    piece = 4 * channels // 12
+
+    def weight_loads(parts):
+        return [
+            pltpu.make_async_copy(
+                io_whole_ref.at[part],
+                w_ref.at[:, :, :, :, pl.ds(part * piece, piece)],
+                weight_sem_ref.at[part],
+            )
+            for part in parts
+        ]
+
+    out_loads, in_loads = weight_loads(range(9, 12)), weight_loads(range(9))
     loads = {}
     for slot, (name, source, target) in enumerate(
         [
             ("flat", ffn_flat_ref, flat_a_ref),
             ("gx", grad_x_two_ref, gx_ref),
             ("co", conv_out_ref, co_ref),
-            ("w", io_whole_ref.at[:, :, :, :, later_columns], w_ref.at[:, :, :, :, later_columns]),
             ("b", streams_ref.at[0], st_ref.at[0, pl.ds(8, length)]),
             ("c", streams_ref.at[1], st_ref.at[1, pl.ds(8, length)]),
             ("x", streams_ref.at[2], st_ref.at[2, pl.ds(8, length)]),
             ("na", norm_one_ref, na_ref),
             ("xo", x_own_ref, xo_ref),
-            ("in", io_whole_ref.at[:, :, :, :, first_columns], w_ref.at[:, :, :, :, first_columns]),
         ]
     ):
         loads[name] = pltpu.make_async_copy(source, target, local_ref.at[slot])
         loads[name].start()
+        if name == "co":
+            for copy in out_loads:
+                copy.start()
+    for copy in in_loads:
+        copy.start()
     enter()
     loads["flat"].wait()
     sent_a = hand_out(early, flat_a_ref, part_a_ref, from_a_ref, 0)
@@ -1031,7 +1082,9 @@
     place_a = pltpu.make_async_copy(sum_a_ref, early_ref.at[spot], local_ref.at[0])
     place_b = pltpu.make_async_copy(sum_b_ref, late_ref.at[spot], local_ref.at[1])
 
-    for name in ("w", "b", "c", "x"):
+    for copy in out_loads:
+        copy.wait()
+    for name in ("b", "c", "x"):
         loads[name].wait()
 
     def weights(first, amount):
@@ -1111,7 +1164,8 @@
         flat_b_ref[:, pl.ds(late.total, rest)] = jnp.zeros((16, rest), jnp.bfloat16)
     sent_b = hand_out(late, flat_b_ref, part_b_ref, from_b_ref, 1)
     forward_on(pieces_a[:1], 1)
-    loads["in"].wait()
+    for copy in in_loads:
+        copy.wait()
     grads = team_copies(
         6,
         lambda p, o: pb_ref.at[pl.ds(pl.multiple_of(p * own, own), own)],
@@ -1224,7 +1278,7 @@
         ((team, early.blocks, rows, early.block), bf16),
     ]
     scratch = [
-        pltpu.VMEM(io_whole.shape, bf16),
+        pltpu.VMEM(dims + (io_whole.shape[4], 4 * channels), bf16),
         pltpu.VMEM((own, width), f32),
         pltpu.VMEM((length, width), bf16),
         pltpu.VMEM((length, LANES), bf16),
@@ -1260,6 +1314,7 @@
         pltpu.SemaphoreType.DMA((7, peers)),
         pltpu.SemaphoreType.DMA((7, peers)),
         pltpu.SemaphoreType.DMA((max(10, 3 + early.blocks),)),
+        pltpu.SemaphoreType.DMA((12,)),
     ]
     return pl.pallas_call(
         functools.partial(backward_kernel, (dims, team, width, channels, length, early, late)),
@@ -1341,6 +1396,7 @@
     late = Share(count, 1, 4 * channels, 2 * width)
     (
         io_whole,
+        _,
         _,
         streams,
         norm_one,

time: 472 us -> 464 us (0.983)
  Pallas kernels: 434 us -> 427 us
    pallas_call x1, Pallas kernels: 353 us -> 344 us  [forward_and_ffn(): pl.pallas_call(functools.partial(forward_kernel, shape), out_shape=[jax.S...]
where the time goes in v5:
time: 464 us; the launch traced here: 463 us
  Pallas kernels  427 us (92%)
  local copies, waits for them, and re-layouts  24.7 us (5%)
  other arithmetic  10 us (2%)
    pallas_call x1, Pallas kernels, forward_and_ffn(): pl.pallas_call(functools.partial(forward_kernel, shape), out_shape=[jax.S...  344 us
    pallas_call x1, Pallas kernels, backward(): pl.pallas_call(functools.partial(backward_kernel, (dims, team, width, cha...  82.2 us

profile of v5, /device:TPU:0, one launch (start us, length us, event | category | flops | bytes accessed | tf_op | source)
XLA Modules:
  0.0 462.8 jit_solution(12501659873787318023)
XLA Ops:
  0.6 0.0 copy-start.7
  0.7 0.0 copy-start.8
  1.4 0.5 compare_convert_fusion.mask_ref
  1.9 0.7 fusion.pick_ref
  2.6 1.3 reshape.155.conv_gain_ref
  3.9 1.3 reshape.156.ffn_gain_ref
  5.2 0.9 compare_bitcast_fusion.1
  6.1 0.3 copy.71
  6.4 1.7 copy.75.out_reduce_ref
  8.1 0.8 stack.29.same_ref
  9.0 1.9 copy.74.in_reduce_ref
  10.9 0.0 copy-done.8
  10.9 0.8 copy.85
  11.7 0.0 copy-start.6
  11.7 0.0 copy-done.7
  11.7 0.4 copy.72
  12.1 0.0 copy-start.5
  12.1 0.9 copy.89
  13.0 0.0 copy-done.6
  13.0 0.0 copy-start.4
  13.0 1.2 copy.76.ffn_reduce_ref
  14.1 0.0 copy-done.5
  14.1 1.3 copy.73.down_shrink_ref
  15.4 0.0 copy-done.4
  15.4 1.2 copy.94
  16.6 344.3 %shard_map.258 = (bf16[12,4,2,2,96,256]{5,4,3,2,1,0:T(8,128)(2,1)}, bf16[9,4,2,2,96,640]{5,4,3,2,1,0:T(8,128)(2,1)}, bf16[9,4,2,2,96,512]{5,4,3,2,1,0:T(8,128)(2...) custom-call(bf16[96,2304]{1,0:T(8,128)(2,1)} %bitcast.77, ...), custom_call_target="tpu_custom_call" | custom-call | tf_op jit(solution)/shard_map/pallas_call | solution.py:838
  361.0 82.2 %shard_map.259 = (bf16[512,1536]{1,0:T(8,128)(2,1)}, bf16[4,2,2,128,896]{4,3,2,1,0:T(8,128)(2,1)}, bf16[4,2,2,128,384]{4,3,2,1,0:T(8,128)(2,1)}, bf16[2,4,128,896]{3,2,1,0:T(8,128)(2,1)}) custom-call(f32[512,1536]{1,0:T(8,128)} %get-tuple-element.24.grad_x_two_ref, bf16[16,14336]{1,0:T(8,128)(2,1)} %get-tuple-element.25.ffn_flat_ref, ...), custom_call_target="tpu_custom_call" | custom-call | tf_op jit(solution)/shard_map/pallas_call | solution.py:1319
  443.2 1.6 copy.86
  444.8 0.8 convert_bitcast_fusion.2
  445.6 0.1 slice_convert_fusion
  445.7 0.0 copy-start.1
  445.7 1.1 copy.95
  446.8 0.8 copy-done.1
  447.6 1.4 copy.93
  449.0 1.6 reshape.168
  450.7 1.3 slice_bitcast_fusion
  452.0 0.1 copy.87
  452.1 0.0 copy-start
  452.1 1.5 slice_convert_fusion.1
  453.6 1.2 maximum_convert_fusion.1
  454.9 0.7 copy-done
  455.6 0.5 copy.88
  456.1 1.5 convert_bitcast_fusion
  457.6 0.0 copy-start.2
  457.6 2.0 maximum_convert_fusion
  459.6 0.0 copy-done.2
  459.6 0.0 copy-start.3
  459.6 1.1 copy.99
  460.8 0.8 copy-done.3
  461.6 1.1 copy.100
  (2 shorter events, 0.0 us)
Async XLA Ops:
  0.6 11.0 %copy-start.7 = (bf16[8,16,3,768]{3,1,2,0:T(8,128)(2,1)S(1)}, bf16[8,16,3,768]{3,1,2,0:T(8,128)(2,1)}, u32[]{:S(2)}) copy-start(bf16[8,16,3,768]{3,1,2,0:T(8,128)(2,1)} %param.31) | copy-start | bytes 1769476
  0.7 10.2 %copy-start.8 = (bf16[96,3,768]{2,0,1:T(8,128)(2,1)S(1)}, bf16[96,3,768]{2,0,1:T(8,128)(2,1)}, u32[]{:S(2)}) copy-start(bf16[96,3,768]{2,0,1:T(8,128)(2,1)} %param.24) | copy-start | bytes 1327108
  11.7 1.3 copy-start.6
  12.1 2.0 copy-start.5
  13.0 2.5 copy-start.4
  445.7 1.9 copy-start.1
  452.1 3.5 copy-start
  457.6 2.0 copy-start.2
  459.6 2.0 copy-start.3
